TPU v7x, 128 devices: a whole 4x4x4 slice. The times are simulated.
128 devices in a mesh: seq: 32 (over x, y_lo, z), dp: 4 (over y_hi, core).
Axes of the slice: x: 4, y: 4 (y_hi: 2, y_lo: 2; y = y_hi * 2 + y_lo), z: 4, core: 2. Of those that a mesh axis runs over, the one named last changes fastest.
Arguments:
- conv_input: bfloat16 [4, 8192, 2816], P('dp', 'seq'), may hold values from -6 to 6
- gate_input: bfloat16 [4, 8192, 2560], P('dp', 'seq'), may hold values from -6 to 6
- step_input: float32 [4, 40, 8192], P('dp', None, 'seq'), may hold values from -7.5 to 8192
- filter_taps: float32 [4, 2816], replicated, may hold values from -3 to 3
- filter_bias: float32 [2816], replicated, may hold values from -0.5 to 0.5
- step_bias: float32 [40], replicated, may hold values from -1 to 1
- decay_log: float32 [40], replicated, may hold values from -13 to 3
- skip_gain: float32 [40], replicated, may hold values from 0.5 to 1.5
- norm_weight: float32 [2560], replicated, may hold values from 0.5 to 1.5
- output_weight: bfloat16 [2560, 1280], P('dp'), may hold values from -0.125 to 0.125
- output_grad: bfloat16 [4, 8192, 1280], P('dp', 'seq'), may hold values from -6 to 6
Outputs:
- input_grad: bfloat16 [4, 8192, 2816], P('dp', 'seq')
- gate_grad: bfloat16 [4, 8192, 2560], P('dp', 'seq')
- step_grad: float32 [4, 40, 8192], P('dp', None, 'seq')
- weight_grad: float32 [2560, 1280], P('dp')
- filter_grads: float32 [5, 2816], replicated
- norm_grad: float32 [2560], replicated
- head_grads: float32 [3, 40], replicated
All inputs are finite; a program needn't handle non-finite values.
Results may differ from a plain program's by a relative error of at most 0.0029.
Values may be sent and summed in bfloat16 or wider, within the bound.
A program may use at most 192 MiB of HBM per device.

v0:
```python
import jax
import jax.numpy as jnp
from jax import lax
from jax.sharding import Mesh
from jax.sharding import PartitionSpec as P

HEADS = 40
HEAD_DIM = 64
STATE = 128
SPAN = 256
INNER = 2560
SEQ = ("seq_0", "seq_1", "seq_2")
SEQ_DP = ("seq_0", "seq_1", "seq_2", "dp")


HIGHEST = lax.Precision.HIGHEST
MASKED = -1e30
EPSILON = 1e-05


def passed_along(value, axis, steps):
    count = lax.axis_size(axis)
    first, last = (max(0, -steps), min(count, count - steps))
    return lax.ppermute(value, axis, [(source, source + steps) for source in range(first, last)])


def filled_with(value, identity):
    return jax.tree.map(
        lambda part, zero: jnp.zeros_like(part) + jnp.asarray(zero, part.dtype), value, identity
    )


def carried_in(value, axes, combine, identity, reverse):
    before = start = filled_with(value, identity)
    total = value
    for axis in reversed(axes):
        length, position = (lax.axis_size(axis), lax.axis_index(axis))
        pieces = jax.tree.map(lambda part: lax.all_gather(part, axis), total)
        inside, total = (start, start)
        for k in reversed(range(length)) if reverse else range(length):
            passed = k > position if reverse else k < position
            total = combine(total, jax.tree.map(lambda part: part[k], pieces))
            inside = jax.tree.map(lambda new, old: jnp.where(passed, new, old), total, inside)
        before = combine(inside, before)
    return before


def rows_for(lines, length):
    spare = -lines.shape[0] % length
    if not spare:
        return lines
    return jnp.concatenate([lines, jnp.zeros((spare, *lines.shape[1:]), lines.dtype)])


def sum_in_two_steps(value, axis):
    lines = value.reshape(-1, *value.shape[1:][-1:])
    own = lax.psum_scatter(
        rows_for(lines, lax.axis_size(axis)), axis, scatter_dimension=0, tiled=True
    )
    whole = lax.all_gather(own, axis).reshape(-1, *lines.shape[1:])
    return lax.slice_in_dim(whole, 0, len(lines)).reshape(value.shape)


def in_one(arrays, axis):
    ends = [0]
    for a in arrays:
        ends.append(ends[-1] + a.size)
    total = lax.psum(jnp.concatenate([a.ravel() for a in arrays]), axis)
    return tuple((total[b:e].reshape(a.shape) for a, b, e in zip(arrays, ends, ends[1:])))


def affine(earlier, later):
    return (earlier[0] * later[0], later[0][:, None, None] * earlier[1] + later[1])


def prepare(extended, step_rows, filter_taps, filter_bias, step_bias, decay_log):
    width = filter_taps.shape[0]
    length = extended.shape[0] - width + 1
    filtered = filter_bias + filter_taps[0] * extended[0:length]
    for offset in range(1, width):
        filtered = filtered + filter_taps[offset] * extended[offset : offset + length]
    activated = jax.nn.silu(filtered)
    step_sizes = jax.nn.softplus(step_rows + step_bias[:, None])
    decay_rates = step_sizes * (-jnp.exp(decay_log))[:, None]
    blocks = length // SPAN
    cumsums = jnp.cumsum(decay_rates.reshape(HEADS, blocks, SPAN), axis=2)
    values = activated[:, :INNER].reshape(blocks, SPAN, HEADS, HEAD_DIM)
    key_side = activated[:, INNER : INNER + STATE].reshape(blocks, SPAN, STATE)
    scaled = values * step_sizes.reshape(HEADS, blocks, SPAN).transpose(1, 2, 0)[..., None]
    to_end = jnp.exp(cumsums[:, :, -1:] - cumsums)
    block_states = jnp.einsum("hcs,cshp,csn->chpn", to_end, scaled, key_side, precision=HIGHEST)
    decays = jnp.exp(cumsums[:, :, -1]).T
    return (activated, cumsums, scaled, block_states, decays)


def summarize(block_states, decays):
    product = jnp.ones((decays.shape[1],), jnp.float32)
    running = jnp.zeros(block_states.shape[1:], jnp.float32)
    running = decays[0][:, None, None] * running + block_states[0]
    product = product * decays[0]
    return (product, running)


def finish(
    activated, cumsums, scaled, block_states, decays, entering, skip_gain, gate_rows, norm_weight
):
    blocks = cumsums.shape[1]
    length = blocks * SPAN
    values = activated[:, :INNER].reshape(blocks, SPAN, HEADS, HEAD_DIM)
    key_side = activated[:, INNER : INNER + STATE].reshape(blocks, SPAN, STATE)
    query_side = activated[:, INNER + STATE :].reshape(blocks, SPAN, STATE)
    starting = []
    starting.append(entering)
    starting = jnp.stack(starting)
    scores = jnp.einsum("ctn,csn->cts", query_side, key_side, precision=HIGHEST)
    differences = cumsums[:, :, :, None] - cumsums[:, :, None, :]
    causal = jnp.tril(jnp.ones((SPAN, SPAN), dtype=bool))
    weights = scores[None] * jnp.exp(jnp.where(causal, differences, MASKED))
    inside = jnp.einsum("hcts,cshp->cthp", weights, scaled, precision=HIGHEST)
    from_state = (
        jnp.einsum("ctn,chpn->cthp", query_side, starting, precision=HIGHEST)
        * jnp.exp(cumsums).transpose(1, 2, 0)[..., None]
    )
    result = inside + from_state + skip_gain[:, None] * values
    scanned = result.reshape(length, INNER)
    gated = scanned * jax.nn.silu(gate_rows)
    inverse_rms = lax.rsqrt(jnp.mean(gated * gated, axis=1, keepdims=True) + EPSILON)
    return gated * inverse_rms * norm_weight


def body(
    conv_input,
    gate_input,
    step_input,
    filter_taps,
    filter_bias,
    step_bias,
    decay_log,
    skip_gain,
    norm_weight,
    output_weight,
    output_grad,
):
    kernel_rows = filter_taps.shape[0] - 1
    raw_rows = conv_input[0]
    before = passed_along(raw_rows[-kernel_rows:], SEQ, 1)
    extended = jnp.concatenate([before, raw_rows], axis=0).astype(jnp.float32)
    gate_rows = gate_input[0].astype(jnp.float32)
    step_rows = step_input[0]
    cotangent = output_grad[0]
    tokens = cotangent.shape[0]
    primals, pull_first = jax.vjp(
        prepare, extended, step_rows, filter_taps, filter_bias, step_bias, decay_log
    )
    activated, cumsums, scaled, block_states, decays = primals
    summary, pull_summary = jax.vjp(summarize, block_states, decays)
    identity = (jnp.ones_like(summary[0]), jnp.zeros_like(summary[1]))
    _, entering = carried_in(summary, SEQ, affine, identity, False)
    normed, pull_second = jax.vjp(
        finish,
        activated,
        cumsums,
        scaled,
        block_states,
        decays,
        entering,
        skip_gain,
        gate_rows,
        norm_weight,
    )
    normed_low = normed.astype(jnp.bfloat16)
    groups = lax.axis_size("dp")
    own_rows = output_weight.shape[0]
    partial_columns = lax.dot_general(
        lax.all_gather(cotangent, "dp", axis=0, tiled=True),
        output_weight,
        (((1,), (1,)), ((), ())),
        preferred_element_type=jnp.float32,
    )
    regrouped = partial_columns.reshape(groups, tokens, own_rows)
    normed_grad = lax.all_to_all(regrouped, "dp", split_axis=0, concat_axis=2, tiled=True).reshape(
        tokens, groups * own_rows
    )
    weight_piece = lax.psum_scatter(
        lax.dot_general(
            normed_low, cotangent, (((0,), (0,)), ((), ())), preferred_element_type=jnp.float32
        ),
        "dp",
        scatter_dimension=0,
        tiled=True,
    )
    weight_grad = sum_in_two_steps(weight_piece, SEQ)
    second = pull_second(normed_grad)
    (
        grad_activated,
        grad_cumsums,
        grad_scaled,
        grad_states,
        grad_decays,
        grad_entering,
        grad_skip,
        grad_gate,
        grad_norm,
    ) = second
    _, end_grad = carried_in((summary[0], grad_entering), SEQ, affine, identity, True)
    decay_grad = jnp.sum(end_grad * entering, axis=(1, 2))
    more_states, more_decays = pull_summary((decay_grad, end_grad))
    first = pull_first(
        (
            grad_activated,
            grad_cumsums,
            grad_scaled,
            grad_states + more_states,
            grad_decays + more_decays,
        )
    )
    grad_extended, grad_steps, grad_taps, grad_bias, grad_step_bias, grad_decay_log = first
    returned = passed_along(grad_extended[:kernel_rows], SEQ, -1)
    own_part = grad_extended[kernel_rows:]
    own_part = jnp.concatenate(
        [own_part[:-kernel_rows], own_part[-kernel_rows:] + returned], axis=0
    )
    filter_part = jnp.concatenate([grad_taps, grad_bias[None]], axis=0)
    head_part = jnp.stack([grad_step_bias, grad_decay_log, grad_skip])
    filter_grads, norm_grad, head_grads = in_one((filter_part, grad_norm, head_part), SEQ_DP)
    input_grad = own_part.astype(jnp.bfloat16)[None]
    gate_grad = grad_gate.astype(jnp.bfloat16)[None]
    step_grad = grad_steps[None]
    return (input_grad, gate_grad, step_grad, weight_grad, filter_grads, norm_grad, head_grads)


def solution(mesh):
    finer = Mesh(mesh.devices.reshape(4, 2, 4, mesh.shape["dp"]), ("seq_0", "seq_1", "seq_2", "dp"))
    return jax.shard_map(
        body,
        mesh=finer,
        in_specs=(
            P("dp", SEQ, None),
            P("dp", SEQ, None),
            P("dp", None, SEQ),
            P(),
            P(),
            P(),
            P(),
            P(),
            P(),
            P("dp", None),
            P("dp", SEQ, None),
        ),
        out_specs=(
            P("dp", SEQ, None),
            P("dp", SEQ, None),
            P("dp", None, SEQ),
            P("dp", None),
            P(),
            P(),
            P(),
        ),
        check_vma=False,
    )
```

profile of v0, /device:TPU:0, one launch (start us, length us, event | category | flops | bytes accessed | tf_op | source)
XLA Modules:
  0.0 963.1 jit_solution(3706765679044331213)
XLA Ops:
  36.2 10.0 %all-reduce.15 = f32[160]{0:T(256)S(1)} all-reduce(f32[160]{0:T(256)S(1)} %dynamic-update-slice), channel_id=3, replica_groups=mesh['seq_0'=4,'seq_1'=2,'seq_2'=4,'dp'=4] {'seq_2'}, use_global_device_ids=true, to_apply=%add.15 | all-reduce | flops 160 | bytes 1280
  51.2 42.6 %all-gather.29.cloned.1.call-done = f32[160,64,128]{2,1,0:T(8,128)} async-done(((f32[40,64,128]{2,1,0:T(8,128)}), f32[160,64,128]{2,1,0:T(8,128)}) %all-gather.29.cloned.1.call-update) | async-done | bytes 5242896 | tf_op jit(solution)/shard_map/all_gather | solution.py:38
  103.5 36.4 %all-gather.19.cloned.1.call-done = f32[2,40,64,128]{3,2,1,0:T(8,128)} async-done(((f32[1,40,64,128]{3,2,1,0:T(8,128)}), f32[2,40,64,128]{3,2,1,0:T(8,128)}) %all-gather.19.cloned.1.call-update) | async-done | bytes 2621456 | tf_op jit(solution)/shard_map/all_gather | solution.py:38
  142.9 29.2 %all-gather.27.cloned.1.call-done = bf16[1,1024,1280]{2,1,0:T(8,128)(2,1)} async-done(((bf16[1,256,1280]{2,1,0:T(8,128)(2,1)}), bf16[1,1024,1280]{2,1,0:T(8,128)(2,1)}) %all-gather.27.cloned.1.call-update) | async-done | bytes 2621456 | tf_op jit(solution)/shard_map/all_gather | solution.py:175
  184.4 10.1 %all-gather.6 = f32[4,1,40]{2,1,0:T(1,128)S(1)} all-gather(f32[1,1,40]{2,1,0:T(1,128)S(1)} %get-tuple-element.94), channel_id=1, replica_groups=mesh['seq_0'=4,'seq_1'=2,'seq_2'=4,'dp'=4] {'seq_0'}, dimensions={0}, use_global_device_ids=true | all-gather | bytes 800 | tf_op jit(solution)/shard_map/all_gather | solution.py:38
  196.0 19.2 %all-to-all-done = f32[4,256,640]{2,1,0:T(8,128)} async-done(((f32[4,256,640]{2,1,0:T(8,128)}), f32[4,256,640]{2,1,0:T(8,128)}, u32[]{:S(2)}, u32[]{:S(2)}) %all-to-all-start) | async-done | bytes 2621472 | tf_op jit(solution)/shard_map/all_to_all | solution.py:181
  218.5 12.1 %all-gather.21.cloned.1.call-done = f32[4,40,64,128]{3,2,1,0:T(8,128)} async-done(((f32[1,40,64,128]{3,2,1,0:T(8,128)}), f32[4,40,64,128]{3,2,1,0:T(8,128)}) %all-gather.21.cloned.1.call-update) | async-done | bytes 5242896 | tf_op jit(solution)/shard_map/all_gather | solution.py:38
  230.6 7.0 add_add_fusion.4
  241.0 13.2 %multiply_reduce_fusion.8 = (f32[256]{0:T(256)S(1)}, f32[256]{0:T(256)S(1)}, f32[1,256,40,64]{1,3,2,0:T(8,128)S(1)}, f32[1,256,40,64]{1,3,2,0:T(8,128)}) fusion(f32[1,256,40,64]{1,3,2,0:T(8,128)S(1)} %bitcast.466, f32[40,64]{1,0:T(8,128)S(1)} %mul.982, f32[1,256,40,64]{1,3,2,0:T(8,128)S(1)} %bitcast.470, f32[1,256,40,64]{1,3,2,0:T(8,128)S(1)} %bitcast.461, ...), kind=kOutput, calls=%fused_computation.73 | convolution fusion | flops 2030960128 | bytes 18813088 | tf_op jit(solution)/shard_map/jvp(hcts,cshp->cthp)/dot_general | solution.py:119
  262.6 57.8 %all-gather.31.cloned.1.call-done = f32[160,64,128]{2,1,0:T(8,128)} async-done(((f32[40,64,128]{2,1,0:T(8,128)}), f32[160,64,128]{2,1,0:T(8,128)}) %all-gather.31.cloned.1.call-update) | async-done | bytes 5242896 | tf_op jit(solution)/shard_map/all_gather | solution.py:38
  324.5 41.9 %all-gather.23.cloned.1.call-done = f32[2,40,64,128]{3,2,1,0:T(8,128)} async-done(((f32[1,40,64,128]{3,2,1,0:T(8,128)}), f32[2,40,64,128]{3,2,1,0:T(8,128)}) %all-gather.23.cloned.1.call-update) | async-done | bytes 2621456 | tf_op jit(solution)/shard_map/all_gather | solution.py:38
  369.9 8.1 fusion.109
  381.1 9.9 %all-gather.8 = f32[4,1,40]{2,1,0:T(1,128)S(1)} all-gather(f32[1,1,40]{2,1,0:T(1,128)S(1)} %get-tuple-element.81), channel_id=1, replica_groups=mesh['seq_0'=4,'seq_1'=2,'seq_2'=4,'dp'=4] {'seq_0'}, dimensions={0}, use_global_device_ids=true | all-gather | bytes 800 | tf_op jit(solution)/shard_map/all_gather | solution.py:38
  394.9 16.4 %fusion.7 = (f32[40,256]{1,0:T(8,128)S(1)}, f32[40,256]{1,0:T(8,128)}, f32[256,256]{1,0:T(8,128)S(1)}) fusion(f32[40,256]{1,0:T(8,128)S(1)} %get-tuple-element.64, f32[256,256]{1,0:T(8,128)S(1)} %fusion.119, pred[256,256]{1,0:T(8,128)(4,1)S(1)} %iota_compare_fusion, f32[256,40,64]{0,2,1:T(8,128)} %bitcast.458, f32[256,40]{0,1:T(8,128)S(1)} %fusion.127, ...), kind=kOutput, calls=%fused_computation.7 | convolution fusion | flops 2037428224 | bytes 5996544 | tf_op jit(solution)/shard_map/transpose(jvp(hcts,cshp->cthp))/dot_general | solution.py:119
  420.8 6.0 fusion.104
  431.5 7.0 add_add_fusion.3
  442.0 11.0 %multiply_reduce_fusion.5 = (f32[40]{0:T(128)}, f32[256,40]{0,1:T(8,128)S(1)}, f32[1,256,40,64]{1,3,2,0:T(8,128)}) fusion(f32[1,256,40,64]{1,3,2,0:T(8,128)S(1)} %copy-done.16, f32[1,256,40,64]{1,3,2,0:T(8,128)S(1)} %bitcast.463, f32[256,40]{0,1:T(8,128)S(1)} %fusion.127, f32[256,40]{0,1:T(8,128)S(1)} %get-tuple-element.63, ...), kind=kOutput, calls=%fused_computation.69 | convolution fusion | flops 2025707520 | bytes 10977440 | tf_op jit(solution)/shard_map/transpose(jvp(hcts,cshp->cthp))/dot_general | solution.py:119
  456.3 6.1 fusion.99
  462.6 6.1 multiply_reduce_fusion.4
  469.6 6.0 multiply_reduce_fusion.9
  485.0 55.9 %reduce-scatter.4.cloned.1.call-done = f32[640,1280]{1,0:T(8,128)} async-done(((f32[2560,1280]{1,0:T(8,128)}), f32[640,1280]{1,0:T(8,128)}) %reduce-scatter.4.cloned.1.call-update) | async-done | bytes 3276816 | tf_op jit(solution)/shard_map/reduce_scatter | solution.py:184
  540.9 100.2 %fusion = f32[24,1280]{1,0:T(8,128)S(1)} fusion(f32[640,1280]{1,0:T(8,128)} %reduce-scatter.4.cloned.1.call-done), kind=kCustom, calls=%all-reduce-scatter | all-reduce-scatter fusion | flops 983041 | bytes 3400192
  672.8 121.0 %all-reduce.20.cloned.1.call-done = f32[16760]{0:T(1024)} async-done(((f32[16760]{0:T(1024)}), f32[16760]{0:T(1024)}) %all-reduce.20.cloned.1.call-update) | async-done | bytes 67056 | tf_op jit(solution)/shard_map/psum | solution.py:68
  800.2 151.1 %all-gather.33.cloned.1.call-done = f32[32,20,1280]{2,1,0:T(8,128)} async-done(((f32[1,20,1280]{2,1,0:T(8,128)}), f32[32,20,1280]{2,1,0:T(8,128)}) %all-gather.33.cloned.1.call-update) | async-done | bytes 3276816 | tf_op jit(solution)/shard_map/all_gather | solution.py:60
  (307 shorter events, 161.3 us)
Async XLA Ops:
  7.2 86.7 %all-gather.29.cloned.1.call-start = ((), (), s32[]{:S(2)}) async-start(), calls=%async_computation.9 | async-start | bytes 6553600 | tf_op jit(solution)/shard_map/all_gather | solution.py:38
  8.1 10.2 %collective-permute-start = (bf16[3,2816]{1,0:T(4,128)(2,1)S(1)}, bf16[3,2816]{1,0:T(4,128)(2,1)S(1)}, u32[]{:S(2)}, u32[]{:S(2)}) collective-permute-start(bf16[3,2816]{1,0:T(4,128)(2,1)S(1)} %slice_bitcast_fusion), channel_id=1, source_target_pairs={{0,4},{4,8},{8,12},{12,16},{16,20},{20,24},{24,28},{28,32},{32,36}... | collective-permute-start | bytes 50696 | tf_op jit(solution)/shard_map/ppermute | solution.py:24
  17.3 377.6 %copy-start.27 = (f32[40,256]{1,0:T(8,128)}, f32[40,256]{1,0:T(8,128)S(1)}, u32[]{:S(2)}) copy-start(f32[40,256]{1,0:T(8,128)S(1)} %get-tuple-element.64) | copy-start | bytes 122884
  34.6 105.2 %all-gather.19.cloned.1.call-start = ((), (), s32[]{:S(2)}) async-start(), calls=%async_computation.2 | async-start | bytes 3932160 | tf_op jit(solution)/shard_map/all_gather | solution.py:38
  51.2 380.2 %copy-start.35 = (f32[40]{0:T(128)}, f32[40]{0:T(128)S(1)}, u32[]{:S(2)}) copy-start(f32[40]{0:T(128)S(1)} %get-tuple-element.84) | copy-start | bytes 484
  51.2 380.2 %copy-start.37 = (f32[40]{0:T(128)}, f32[40]{0:T(128)S(1)}, u32[]{:S(2)}) copy-start(f32[40]{0:T(128)S(1)} %get-tuple-element.87) | copy-start | bytes 484
  51.2 380.2 %copy-start.39 = (f32[40]{0:T(128)}, f32[40]{0:T(128)S(1)}, u32[]{:S(2)}) copy-start(f32[40]{0:T(128)S(1)} %get-tuple-element.89) | copy-start | bytes 484
  97.8 74.3 %all-gather.27.cloned.1.call-start = ((), (), s32[]{:S(2)}) async-start(), calls=%async_computation.8 | async-start | bytes 3276800 | tf_op jit(solution)/shard_map/all_gather | solution.py:175
  98.6 132.0 %all-gather.21.cloned.1.call-start = ((), (), s32[]{:S(2)}) async-start(), calls=%async_computation.3 | async-start | bytes 6553600 | tf_op jit(solution)/shard_map/all_gather | solution.py:38
  177.6 37.6 %all-to-all-start = ((f32[4,256,640]{2,1,0:T(8,128)}), f32[4,256,640]{2,1,0:T(8,128)}, u32[]{:S(2)}, u32[]{:S(2)}) async-start(f32[4,256,640]{2,1,0:T(8,128)} %bitcast.476), calls=%async_computation | async-start | bytes 5242880 | tf_op jit(solution)/shard_map/all_to_all | solution.py:181
  182.3 138.0 %all-gather.31.cloned.1.call-start = ((), (), s32[]{:S(2)}) async-start(), calls=%async_computation.10 | async-start | bytes 6553600 | tf_op jit(solution)/shard_map/all_gather | solution.py:38
  194.6 200.3 %copy-start.24 = (pred[256,256]{1,0:T(8,128)(4,1)}, pred[256,256]{1,0:T(8,128)(4,1)S(1)}, u32[]{:S(2)}) copy-start(pred[256,256]{1,0:T(8,128)(4,1)S(1)} %iota_compare_fusion) | copy-start | bytes 196612
  262.6 103.8 %all-gather.23.cloned.1.call-start = ((), (), s32[]{:S(2)}) async-start(), calls=%async_computation.4 | async-start | bytes 3932160 | tf_op jit(solution)/shard_map/all_gather | solution.py:38
  324.4 107.0 %all-gather.25.cloned.1.call-start = ((), (), s32[]{:S(2)}) async-start(), calls=%async_computation.5 | async-start | bytes 6553600 | tf_op jit(solution)/shard_map/all_gather | solution.py:38
  369.4 171.5 %reduce-scatter.4.cloned.1.call-start = ((), (), s32[]{:S(2)}) async-start(), calls=%async_computation.6 | async-start | bytes 16384000 | tf_op jit(solution)/shard_map/reduce_scatter | solution.py:184
  378.0 415.8 %all-reduce.20.cloned.1.call-start = ((), (), s32[]{:S(2)}) async-start(), calls=%async_computation.7 | async-start | bytes 139264 | tf_op jit(solution)/shard_map/psum | solution.py:68
  641.1 6.7 collective-permute-start.7
  642.6 7.8 collective-permute-start.6
  643.9 6.5 collective-permute-start.5
  645.2 5.2 collective-permute-start.4
  646.5 4.0 collective-permute-start.3
  647.8 4.3 collective-permute-start.2
  650.3 300.9 %all-gather.33.cloned.1.call-start = ((), (), s32[]{:S(2)}) async-start(), calls=%async_computation.11 | async-start | bytes 4055040 | tf_op jit(solution)/shard_map/all_gather | solution.py:60
  666.2 131.7 %collective-permute-start.1 = (f32[3,2816]{1,0:T(4,128)S(1)}, f32[3,2816]{1,0:T(4,128)S(1)}, u32[]{:S(2)}, u32[]{:S(2)}) collective-permute-start(f32[3,2816]{1,0:T(4,128)S(1)} %pad_add_fusion.1), channel_id=1, source_target_pairs={{4,0},{8,4},{12,8},{16,12},{20,16},{24,20},{28,24},{32,28},{36,32}... | collective-permute-start | bytes 101384 | tf_op jit(solution)/shard_map/ppermute | solution.py:24
  (74 other events, 1872.6 us)
Sparse Core Ops, SparseCore 0:
  34.7 59.0 all-gather.28
  98.0 41.8 all-gather.18
  141.5 30.5 all-gather.26
  174.2 56.2 all-gather.20
  262.7 57.6 all-gather.30
  324.5 41.8 all-gather.22
  369.6 57.8 all-gather.24
  430.2 110.7 reduce-scatter.3
  650.5 143.2 all-reduce.19
  795.3 155.8 all-gather.32
where the time goes:
time: 971 us; the launch traced here: 963 us
  waiting for transfers between devices  570 us (59%)
  blocking collectives  139 us (14%)
  matrix products  86.4 us (9%)
  other arithmetic  81.4 us (8%)
  local copies, waits for them, and re-layouts  50.3 us (5%)
  starting transfers between devices  19.1 us (2%)
  between operations  17.5 us (2%)
    all_gather x6, waiting for transfers between devices, carried_in(): pieces = jax.tree.map(lambda part: lax.all_gather(part, axis), total)  191 us
    all_gather x1, waiting for transfers between devices, sum_in_two_steps(): whole = lax.all_gather(own, axis).reshape(-1, *lines.shape[1:])  151 us
    psum x1, waiting for transfers between devices, in_one(): total = lax.psum(jnp.concatenate([a.ravel() for a in arrays]), axis)  121 us
    unnamed x2, blocking collectives  110 us
    reduce_scatter x1, waiting for transfers between devices, body(): lax.psum_scatter(lax.dot_general(normed_low, cotangent, (((0,), (0,)), ((...  55.9 us
    dot_general x3, matrix products, finish(): inside = jnp.einsum('hcts,cshp->cthp', weights, scaled, precision=HIGHEST)  40.6 us
    all_gather x1, waiting for transfers between devices, body(): lax.all_gather(cotangent, 'dp', axis=0, tiled=True)  29.2 us
    all_gather x4, blocking collectives, carried_in(): pieces = jax.tree.map(lambda part: lax.all_gather(part, axis), total)  28.5 us
  transfers between devices with their start and end apart: 19, of which 11 were waited for; matrix products, arithmetic and copies ran while one was open for 16% of the time, Pallas kernels for 0%

commit v1 on v0

v1 whole, which is shorter than its diff:
```python
import functools

import jax
import jax.numpy as jnp
from jax import lax
from jax.experimental import pallas as pl
from jax.experimental.pallas import tpu as pltpu
from jax.sharding import PartitionSpec as P

HEADS = 40
HEAD_DIM = 64
STATE = 128
INNER = 2560
CHANNELS = 2816
WIDTH = 1280
TOKENS = 256
TAPS = 4
PAIRS = 20
HALF = 1280
CHUNK = HALF + 128
SEQ = 32
DP = 4
ROWS = INNER // DP
PIECE = 208
MASKED = -1e30
EPSILON = 1e-05

F32 = jnp.float32
BF16 = jnp.bfloat16
MESH = pl.DeviceIdType.MESH
NN = ((1,), (0,))
NT = ((1,), (1,))
TN = ((0,), (0,))


def mm(a, b, dims):
    return lax.dot_general(a, b, (dims, ((), ())), preferred_element_type=F32)


def split(x):
    high = x.astype(BF16)
    return high, (x - high.astype(F32)).astype(BF16)


def dot3(a, b, dims):
    return mm(a[0], b[0], dims) + mm(a[0], b[1], dims) + mm(a[1], b[0], dims)


def iota(shape, dim):
    return lax.broadcasted_iota(jnp.int32, shape, dim)


def lanes(p):
    return pl.ds(pl.multiple_of(p * 128, 128), 128)


def rates_of(step_ref, bias_ref, log_ref):
    raw = step_ref[...] + bias_ref[...]
    sizes = jnp.maximum(raw, 0.0) + jnp.log1p(jnp.exp(-jnp.abs(raw)))
    gain = -jnp.exp(log_ref[...])
    rates = sizes * gain
    lane = iota(rates.shape, 1)
    cums = rates
    shift = 1
    while shift < TOKENS:
        cums = cums + jnp.where(lane >= shift, pltpu.roll(cums, shift, 1), 0.0)
        shift *= 2
    return raw, sizes, gain, rates, cums


def turned(x):
    return jnp.transpose(jnp.concatenate([x, jnp.zeros((128 - HEADS, TOKENS), F32)], axis=0))


def widen(columns, p):
    first = iota((TOKENS, 128), 1) < HEAD_DIM
    return jnp.where(first, columns[:, 2 * p : 2 * p + 1], columns[:, 2 * p + 1 : 2 * p + 2])


def head_sum(v, p):
    into = (iota((128, 128), 1) == 2 * p + iota((128, 128), 0) // HEAD_DIM).astype(BF16)
    high, low = split(v)
    return mm(high, into, NN) + mm(low, into, NN)


def sigmoid(x):
    return 1.0 / (1.0 + jnp.exp(-x))


def filtered_of(x_ref, halo_ref, taps_ref, bias_ref, ext_ref, cols):
    ext_ref[0:8, :] = halo_ref[:, cols].astype(F32)
    ext_ref[8 : 8 + TOKENS, :] = x_ref[:, cols].astype(F32)
    total = bias_ref[:, cols] + taps_ref[0:1, cols] * ext_ref[5 : 5 + TOKENS, :]
    for k in range(1, TAPS):
        total = total + taps_ref[k : k + 1, cols] * ext_ref[5 + k : 5 + k + TOKENS, :]
    return total


def write_decays(pay_ref, cums_turned):
    decays = jnp.exp(cums_turned[TOKENS - 1 : TOKENS, :])
    for half in range(2):
        pay_ref[half, :, HALF:] = jnp.broadcast_to(decays, (STATE, 128))


def first_kernel(x_ref, halo_ref, taps_ref, fbias_ref, step_ref, sbias_ref, dlog_ref, act_ref, pay_ref, ext_ref):
    def activate(j, carry):
        cols = lanes(j)
        f = filtered_of(x_ref, halo_ref, taps_ref, fbias_ref, ext_ref, cols)
        act_ref[:, cols] = f * sigmoid(f)
        return carry

    lax.fori_loop(0, CHANNELS // 128, activate, 0)
    _, sizes, _, _, cums = rates_of(step_ref, sbias_ref, dlog_ref)
    to_end = turned(jnp.exp(cums[:, TOKENS - 1 :] - cums) * sizes)
    key_turned = split(jnp.transpose(act_ref[:, INNER : INNER + STATE]))
    for p in range(PAIRS):
        a = act_ref[:, p * 128 : p * 128 + 128] * widen(to_end, p)
        half, at = divmod(p, PAIRS // 2)
        pay_ref[half, :, at * 128 : at * 128 + 128] = dot3(key_turned, split(a), NN)
    write_decays(pay_ref, turned(cums))


def middle_kernel(
    dp_ref, act_ref, gate_ref, step_ref, sbias_ref, dlog_ref, skip_ref, weight_ref, ent_ref, cot_ref,
    w0_ref, w1_ref, w2_ref, w3_ref,
    low_ref, ggate_ref, pay_ref, dy_ref, dx_ref, dq_ref, dk_ref, dcum_ref, dnorm_ref, dskip_ref,
    col_ref, cum_ref, stepx_ref, expx_ref, scores_ref, turn_ref, scan_ref, ng_ref, acc_ref, dsc_ref,
):
    me = dp_ref[0]
    for k, w_ref in enumerate((w0_ref, w1_ref, w2_ref, w3_ref)):
        at = pl.multiple_of(jnp.bitwise_xor(me, k) * ROWS, 128)
        ng_ref[:, pl.ds(at, ROWS)] = mm(cot_ref[...], w_ref[...], NT)
    _, sizes, _, _, cums = rates_of(step_ref, sbias_ref, dlog_ref)
    for h in range(HEADS):
        cum_ref[h] = cums[h : h + 1, :]
    cum_t = turned(cums)
    size_t = turned(sizes)
    exp_t = jnp.exp(cum_t)
    for h in range(HEADS):
        col_ref[h] = jnp.broadcast_to(cum_t[:, h : h + 1], (TOKENS, 128))
    for p in range(PAIRS):
        stepx_ref[:, p * 128 : p * 128 + 128] = widen(size_t, p)
        expx_ref[:, p * 128 : p * 128 + 128] = widen(exp_t, p)
    write_decays(pay_ref, cum_t)
    key = act_ref[:, INNER : INNER + STATE]
    query = act_ref[:, INNER + STATE :]
    key_s, query_s = split(key), split(query)
    query_turned = split(jnp.transpose(query))
    scores_ref[...] = dot3(query_s, key_s, NT)
    turn_ref[...] = dot3(key_s, query_s, NT)
    first = iota((TOKENS, 128), 1) < HEAD_DIM
    down = iota((TOKENS, TOKENS), 0)
    across = iota((TOKENS, TOKENS), 1)

    def column(h):
        c = col_ref[h]
        return jnp.concatenate([c, c], axis=1)

    acc_ref[...] = jnp.zeros_like(acc_ref)

    def forward(p, carry):
        cols = lanes(p)
        half = p // (PAIRS // 2)
        values = act_ref[:, cols]
        high, low = split(values * stepx_ref[:, cols])
        both = jnp.concatenate([high, low], axis=1)
        parts = []
        for i in range(2):
            h = 2 * p + i
            e = jnp.exp(jnp.where(down >= across, column(h) - cum_ref[h], MASKED))
            wh, wl = split(scores_ref[...] * e)
            r = mm(wh, both, NN)
            parts.append(r[:, :128] + r[:, 128:] + mm(wl, high, NN))
        state = split(ent_ref[half, :, lanes(p - half * (PAIRS // 2))])
        scanned = (
            jnp.where(first, parts[0], parts[1])
            + dot3(query_s, state, NN) * expx_ref[:, cols]
            + skip_ref[:, cols] * values
        )
        scan_ref[:, cols] = scanned
        gate = gate_ref[:, cols].astype(F32)
        gated = scanned * (gate * sigmoid(gate))
        acc_ref[...] += gated * gated
        return carry

    lax.fori_loop(0, PAIRS, forward, 0)
    inverse = lax.rsqrt(jnp.sum(acc_ref[...], axis=1, keepdims=True) / INNER + EPSILON)
    acc_ref[...] = jnp.zeros_like(acc_ref)

    def norm(p, carry):
        cols = lanes(p)
        gate = gate_ref[:, cols].astype(F32)
        gated = scan_ref[:, cols] * (gate * sigmoid(gate))
        weight = weight_ref[:, cols]
        unit = gated * inverse
        low_ref[:, cols] = (unit * weight).astype(BF16)
        ng = ng_ref[:, cols]
        dnorm_ref[:, cols] = jnp.sum(ng * unit, axis=0, keepdims=True)
        acc_ref[...] += ng * weight * gated
        return carry

    lax.fori_loop(0, PAIRS, norm, 0)
    lean = jnp.sum(acc_ref[...], axis=1, keepdims=True) * (inverse * inverse * inverse) / INNER
    dsc_ref[...] = jnp.zeros_like(dsc_ref)
    dq_ref[...] = jnp.zeros_like(dq_ref)
    dcum_ref[...] = jnp.zeros_like(dcum_ref)
    dskip_ref[...] = jnp.zeros_like(dskip_ref)

    def backward(p, carry):
        cols = lanes(p)
        half = p // (PAIRS // 2)
        inner = lanes(p - half * (PAIRS // 2))
        gate = gate_ref[:, cols].astype(F32)
        gain = sigmoid(gate)
        silu = gate * gain
        scanned = scan_ref[:, cols]
        dgated = inverse * (ng_ref[:, cols] * weight_ref[:, cols]) - scanned * silu * lean
        ggate_ref[:, cols] = (dgated * scanned * (gain * (1.0 + gate * (1.0 - gain)))).astype(BF16)
        dy = dgated * silu
        dy_ref[:, cols] = dy
        dh, dl = split(dy)
        both = jnp.concatenate([dh, dl], axis=1)
        twice = jnp.concatenate([dh, dh], axis=1)
        values = act_ref[:, cols]
        scaled = values * stepx_ref[:, cols]
        parts = []
        for i in range(2):
            h = 2 * p + i
            e = jnp.exp(jnp.where(across >= down, cum_ref[h] - column(h), MASKED))
            wh, wl = split(turn_ref[...] * e)
            r = mm(wh, both, NN)
            parts.append(r[:, :128] + r[:, 128:] + mm(wl, dh, NN))
            own = first if i == 0 else jnp.logical_not(first)
            xh, xl = split(jnp.where(own, scaled, 0.0))
            dw = mm(jnp.concatenate([xh, xl], axis=1), twice, NT) + mm(xh, dl, NT)
            dsc_ref[...] += dw * e
        dx = jnp.where(first, parts[0], parts[1])
        dx_ref[:, cols] = dx
        z = split(dy * expx_ref[:, cols])
        pay_ref[half, :, inner] = dot3(query_turned, z, NN)
        dq_ref[...] += dot3(z, split(ent_ref[half, :, inner]), NT)
        skipped = dy * values
        dcum_ref[...] += head_sum(dy * scanned - skipped * skip_ref[:, cols] - scaled * dx, p)
        dskip_ref[...] += head_sum(jnp.sum(skipped.reshape(TOKENS // 8, 8, 128), axis=0), p)
        return carry

    lax.fori_loop(0, PAIRS, backward, 0)
    dsc = dsc_ref[...]
    dk_ref[...] = dot3(split(dsc), query_s, NN)
    dq_ref[...] += dot3(split(jnp.transpose(dsc)), key_s, NN)


def last_kernel(
    x_ref, halo_ref, taps_ref, fbias_ref, act_ref, step_ref, sbias_ref, dlog_ref, skip_ref, ent_ref, end_ref,
    dy_ref, dx_ref, dq_ref, dk_ref, dcum_ref, dskip_ref,
    gin_ref, tail_ref, ret_ref, gstep_ref, gfilt_ref, ghead_ref,
    ext_ref, dfilt_ref, stepx_ref, endx_ref, dact_ref, dstep_ref, zsum_ref, ded_ref, dkey_ref,
):
    raw, sizes, gain, rates, cums = rates_of(step_ref, sbias_ref, dlog_ref)
    size_t = turned(sizes)
    end_t = turned(jnp.exp(cums[:, TOKENS - 1 :] - cums))
    for p in range(PAIRS):
        stepx_ref[:, p * 128 : p * 128 + 128] = widen(size_t, p)
        endx_ref[:, p * 128 : p * 128 + 128] = widen(end_t, p)
    key_s = split(act_ref[:, INNER : INNER + STATE])
    dstep_ref[...] = jnp.zeros_like(dstep_ref)
    zsum_ref[...] = jnp.zeros_like(zsum_ref)
    ded_ref[...] = jnp.zeros_like(ded_ref)
    dkey_ref[...] = dk_ref[...]

    def pair(p, carry):
        cols = lanes(p)
        half = p // (PAIRS // 2)
        inner = lanes(p - half * (PAIRS // 2))
        values = act_ref[:, cols]
        step = stepx_ref[:, cols]
        ending = endx_ref[:, cols]
        end = end_ref[half, :, inner]
        end_s = split(end)
        z = dot3(key_s, end_s, NN) * ending
        dx = dx_ref[:, cols] + z
        dact_ref[:, cols] = dx * step + skip_ref[:, cols] * dy_ref[:, cols]
        dstep_ref[...] += head_sum(dx * values, p)
        scaled = values * step
        zsum_ref[...] += head_sum(scaled * z, p)
        dkey_ref[...] += dot3(split(scaled * ending), end_s, NT)
        both = end * ent_ref[half, :, inner]
        ded_ref[...] += head_sum(jnp.sum(both.reshape(STATE // 8, 8, 128), axis=0), p)
        return carry

    lax.fori_loop(0, PAIRS, pair, 0)
    dact_ref[:, INNER : INNER + STATE] = dkey_ref[...]
    dact_ref[:, INNER + STATE :] = dq_ref[...]
    zsum = zsum_ref[...]
    cum_t = turned(cums)
    decays = jnp.exp(cum_t[TOKENS - 1 :, :])
    final = jnp.sum(zsum, axis=0, keepdims=True) + decays * jnp.sum(ded_ref[...], axis=0, keepdims=True)
    row = iota((TOKENS, 128), 0)
    dcum = dcum_ref[...] - zsum + jnp.where(row == TOKENS - 1, final, 0.0)
    shift = 1
    while shift < TOKENS:
        dcum = dcum + jnp.where(row < TOKENS - shift, pltpu.roll(dcum, TOKENS - shift, 0), 0.0)
        shift *= 2
    gain_t = turned(jnp.broadcast_to(gain, (HEADS, TOKENS)))
    draw = (dstep_ref[...] + dcum * gain_t) * turned(sigmoid(raw))
    gstep_ref[...] = jnp.transpose(draw)[:HEADS, :]
    ghead_ref[0:1, :] = jnp.sum(draw, axis=0, keepdims=True)
    ghead_ref[1:2, :] = jnp.sum(dcum * turned(rates), axis=0, keepdims=True)
    ghead_ref[2:3, :] = jnp.sum(dskip_ref[...], axis=0, keepdims=True)
    ghead_ref[3:8, :] = jnp.zeros((5, 128), F32)
    dfilt_ref[0:8, :] = jnp.zeros((8, 128), F32)
    dfilt_ref[8 + TOKENS :, :] = jnp.zeros((8, 128), F32)

    def filters(j, carry):
        cols = lanes(j)
        f = filtered_of(x_ref, halo_ref, taps_ref, fbias_ref, ext_ref, cols)
        s = sigmoid(f)
        dfilt = dact_ref[:, cols] * (s * (1.0 + f * (1.0 - s)))
        dfilt_ref[8 : 8 + TOKENS, :] = dfilt
        dx = taps_ref[TAPS - 1 : TAPS, cols] * dfilt
        back = taps_ref[0:1, cols] * dfilt_ref[8:16, :]
        for k in range(TAPS):
            gfilt_ref[k : k + 1, cols] = jnp.sum(dfilt * ext_ref[5 + k : 5 + k + TOKENS, :], axis=0, keepdims=True)
            if k < TAPS - 1:
                dx = dx + taps_ref[k : k + 1, cols] * dfilt_ref[11 - k : 11 - k + TOKENS, :]
            if 0 < k < TAPS - 1:
                back = back + taps_ref[k : k + 1, cols] * dfilt_ref[8 - k : 16 - k, :]
        gfilt_ref[TAPS : TAPS + 1, cols] = jnp.sum(dfilt, axis=0, keepdims=True)
        gin_ref[:, cols] = dx.astype(BF16)
        tail_ref[:, cols] = dx[TOKENS - 8 :, :]
        ret_ref[:, cols] = back
        return carry

    lax.fori_loop(0, CHANNELS // 128, filters, 0)


def outer_kernel(l0, l1, l2, l3, g0, g1, g2, g3, out_ref):
    lows = [jnp.transpose(r[...]) for r in (l0, l1, l2, l3)]
    cots = (g0, g1, g2, g3)

    for j in range(WIDTH // 256):
        total = mm(lows[0], cots[0][:, j * 256 : j * 256 + 256], NN)
        for k in range(1, DP):
            total = total + mm(lows[k], cots[k][:, j * 256 : j * 256 + 256], NN)
        for i in range(2):
            at = (2 * j + i) * ROWS
            out_ref[at : at + ROWS, :] = total[:, i * 128 : i * 128 + 128].astype(BF16)
    out_ref[10 * ROWS :, :] = jnp.zeros((SEQ * PIECE - 10 * ROWS, 128), BF16)


def greet(seq, dp, with_dp):
    barrier = pltpu.get_barrier_semaphore()

    def hello(i, carry):
        peer = lax.rem(seq + i, SEQ)
        pl.semaphore_signal(barrier, inc=1, device_id=(peer, dp), device_id_type=MESH)
        return carry

    lax.fori_loop(1, SEQ, hello, 0)
    count = SEQ - 1
    if with_dp:
        for k in range(1, DP):
            other = lax.rem(dp + k, DP)
            pl.semaphore_signal(barrier, inc=1, device_id=(seq, other), device_id_type=MESH)
        count += DP - 1
    pl.semaphore_wait(barrier, count)


def to_peer(src, dst, send, recv, device):
    return pltpu.make_async_remote_copy(
        src_ref=src, dst_ref=dst, send_sem=send, recv_sem=recv, device_id=device, device_id_type=MESH
    )


def scan_kernel(reverse, pay_ref, out_ref, recv, outgoing, coef, sems):
    seq, dp = lax.axis_index("seq"), lax.axis_index("dp")
    greet(seq, dp, False)

    def each_peer(act):
        def step(i, carry):
            act(i, lax.rem(seq + i, SEQ))
            return carry

        lax.fori_loop(1, SEQ, step, 0)

    def spread(i, peer):
        return to_peer(pay_ref.at[peer], recv.at[seq], sems.at[0, i], sems.at[1, seq], (peer, dp))

    def spread_here(i, peer):
        return to_peer(pay_ref.at[peer], recv.at[peer], sems.at[0, i], sems.at[1, peer], (peer, dp))

    each_peer(lambda i, peer: spread(i, peer).start())
    recv[seq] = pay_ref[seq]
    each_peer(lambda i, peer: spread_here(i, peer).wait_recv())

    decays = jnp.concatenate([recv[k, 0:1, HALF:] for k in range(SEQ)], axis=0)
    head = (seq // (SEQ // 2)) * (HEADS // 2) + iota((128, HALF), 1) // HEAD_DIM
    into = (iota((128, HALF), 0) == head).astype(F32)
    wide = lax.dot_general(
        decays, into, (NN, ((), ())), preferred_element_type=F32, precision=lax.Precision.HIGHEST
    )
    for k in range(SEQ):
        coef[k] = wide[k : k + 1, :]

    def scan(j, state):
        k = SEQ - 1 - j if reverse else j
        outgoing[k] = state
        return coef[k] * state + recv[k, :, :HALF]

    lax.fori_loop(0, SEQ, scan, jnp.zeros((8, HALF), F32))

    def back(i, peer):
        return to_peer(outgoing.at[peer], out_ref.at[seq], sems.at[2, i], sems.at[3, seq], (peer, dp))

    def back_here(i, peer):
        return to_peer(outgoing.at[peer], out_ref.at[peer], sems.at[2, i], sems.at[3, peer], (peer, dp))

    each_peer(lambda i, peer: back(i, peer).start())
    out_ref[seq] = outgoing[seq]
    each_peer(lambda i, peer: back_here(i, peer).wait_recv())
    each_peer(lambda i, peer: spread(i, peer).wait_send())
    each_peer(lambda i, peer: back(i, peer).wait_send())


def sum_kernel(wide_ref, small_ref, wout_ref, sout_ref, wrecv, srecv, wown, sown, sdp, wacc, sems, dsems):
    seq, dp = lax.axis_index("seq"), lax.axis_index("dp")
    greet(seq, dp, True)

    def each_peer(act):
        def step(i, carry):
            act(i, lax.rem(seq + i, SEQ))
            return carry

        lax.fori_loop(1, SEQ, step, 0)

    def out(src, dst, row):
        return lambda i, peer: to_peer(src.at[peer], dst.at[seq], sems.at[row, i], sems.at[row + 1, seq], (peer, dp))

    def out_here(src, dst, row):
        return lambda i, peer: to_peer(src.at[peer], dst.at[peer], sems.at[row, i], sems.at[row + 1, peer], (peer, dp))

    def all_of(src, dst, row):
        return lambda i, peer: to_peer(src, dst.at[seq], sems.at[row, i], sems.at[row + 1, seq], (peer, dp))

    def all_here(src, dst, row):
        return lambda i, peer: to_peer(src, dst.at[peer], sems.at[row, i], sems.at[row + 1, peer], (peer, dp))

    each_peer(lambda i, peer: out(small_ref, srecv, 0)(i, peer).start())
    each_peer(lambda i, peer: out(wide_ref, wrecv, 2)(i, peer).start())
    srecv[seq] = small_ref[seq]
    wrecv[seq] = wide_ref[seq]
    each_peer(lambda i, peer: out_here(small_ref, srecv, 0)(i, peer).wait_recv())
    sdp[dp] = lax.fori_loop(0, SEQ, lambda k, total: total + srecv[k], jnp.zeros((8, 128), F32))

    def across(k):
        other = lax.rem(dp + k, DP)
        return to_peer(sdp.at[dp], sdp.at[dp], dsems.at[0, k], dsems.at[1, dp], (seq, other))

    def across_here(k):
        other = lax.rem(dp + k, DP)
        return to_peer(sdp.at[dp], sdp.at[other], dsems.at[0, k], dsems.at[1, other], (seq, other))

    for k in range(1, DP):
        across(k).start()
    for k in range(1, DP):
        across_here(k).wait_recv()
    sown[...] = sdp[0] + sdp[1] + sdp[2] + sdp[3]
    each_peer(lambda i, peer: all_of(sown, sout_ref, 4)(i, peer).start())
    sout_ref[seq] = sown[...]

    each_peer(lambda i, peer: out_here(wide_ref, wrecv, 2)(i, peer).wait_recv())
    wacc[...] = jnp.zeros_like(wacc)

    def add(k, carry):
        wacc[...] += wrecv[k].astype(F32)
        return carry

    lax.fori_loop(0, SEQ, add, 0)
    wown[...] = wacc[...].astype(BF16)
    each_peer(lambda i, peer: all_of(wown, wout_ref, 6)(i, peer).start())
    wout_ref[seq] = wown[...]
    each_peer(lambda i, peer: all_here(sown, sout_ref, 4)(i, peer).wait_recv())
    each_peer(lambda i, peer: all_here(wown, wout_ref, 6)(i, peer).wait_recv())
    for k in range(1, DP):
        across(k).wait_send()
    each_peer(lambda i, peer: out(small_ref, srecv, 0)(i, peer).wait_send())
    each_peer(lambda i, peer: out(wide_ref, wrecv, 2)(i, peer).wait_send())
    each_peer(lambda i, peer: all_of(sown, sout_ref, 4)(i, peer).wait_send())
    each_peer(lambda i, peer: all_of(wown, wout_ref, 6)(i, peer).wait_send())


VMEM = pl.BlockSpec(memory_space=pltpu.VMEM)
SMEM = pl.BlockSpec(memory_space=pltpu.SMEM)


def call(kernel, outs, scratch, args, specs=None, collective=None, flops=0, traffic=0, name=None):
    params = dict(vmem_limit_bytes=60 * 2**20)
    if collective is not None:
        params.update(collective_id=collective, has_side_effects=True)
    return pl.pallas_call(
        kernel,
        out_shape=[jax.ShapeDtypeStruct(shape, kind) for shape, kind in outs],
        in_specs=specs or [VMEM] * len(args),
        out_specs=[VMEM] * len(outs),
        scratch_shapes=scratch,
        compiler_params=pltpu.CompilerParams(**params),
        cost_estimate=pl.CostEstimate(flops=flops, bytes_accessed=traffic, transcendentals=0),
        name=name,
    )(*args)


def vmem(*shape, kind=F32):
    return pltpu.VMEM(shape, kind)


def state_scan(payload, reverse, collective):
    (out,) = call(
        functools.partial(scan_kernel, reverse),
        [((SEQ, 8, HALF), F32)],
        [vmem(SEQ, 8, CHUNK), vmem(SEQ, 8, HALF), vmem(SEQ, 1, HALF), pltpu.SemaphoreType.DMA((4, SEQ))],
        (payload.reshape(SEQ, 8, CHUNK),),
        collective=collective,
        flops=30_000_000_000,
        name="scan_back" if reverse else "scan_on",
    )
    return out.reshape(2, STATE, HALF)


def moved(value, bits):
    return lax.ppermute(value, "dp", [(d, d ^ bits) for d in range(DP)])


def body(
    conv_input, gate_input, step_input, filter_taps, filter_bias, step_bias, decay_log, skip_gain, norm_weight,
    output_weight, output_grad,
):
    raw_rows, gate_rows, step_rows, cotangent = conv_input[0], gate_input[0], step_input[0], output_grad[0]
    dp = lax.axis_index("dp")
    crossing = [(s * DP + d, (s ^ 4) * DP + (d ^ 2)) for s in range(SEQ) for d in range(DP)]
    halo = lax.ppermute(raw_rows[-8:], "seq", [(s, s + 1) for s in range(SEQ - 1)])
    weight_2 = lax.ppermute(output_weight, ("seq", "dp"), crossing)
    weight_1 = moved(output_weight, 1)
    weight_3 = moved(weight_2, 1)
    cot_1, cot_2 = moved(cotangent, 1), moved(cotangent, 2)
    cot_3 = moved(cot_2, 1)

    fbias = filter_bias[None]
    heads = (step_rows, step_bias[:, None], decay_log[:, None])
    skip = jnp.repeat(skip_gain, HEAD_DIM)[None]
    act, payload = call(
        first_kernel,
        [((TOKENS, CHANNELS), F32), ((2, STATE, CHUNK), F32)],
        [vmem(TOKENS + 8, 128)],
        (raw_rows, halo, filter_taps, fbias, *heads),
        flops=5_000_000_000,
        name="first",
    )
    entering = state_scan(payload, False, 0)
    wide = (TOKENS, INNER)
    small = (TOKENS, STATE)
    low, gate_grad, payload, dy, dx, dq, dk, dcum, dnorm, dskip = call(
        middle_kernel,
        [(wide, BF16), (wide, BF16), ((2, STATE, CHUNK), F32), (wide, F32), (wide, F32), (small, F32), (small, F32),
         (small, F32), ((1, INNER), F32), ((8, 128), F32)],
        [vmem(HEADS, TOKENS, 128), vmem(HEADS, 1, TOKENS), vmem(*wide), vmem(*wide), vmem(TOKENS, TOKENS),
         vmem(TOKENS, TOKENS), vmem(*wide), vmem(*wide), vmem(TOKENS, 128), vmem(TOKENS, TOKENS)],
        (dp[None].astype(jnp.int32), act, gate_rows, *heads, skip, norm_weight[None], entering, cotangent,
         output_weight, weight_1, weight_2, weight_3),
        specs=[SMEM] + [VMEM] * 13,
        flops=20_000_000_000,
        name="middle",
    )
    lows = [
        lax.dynamic_slice_in_dim(low, jnp.bitwise_xor(dp, k) * ROWS, ROWS, axis=1) for k in range(DP)
    ]
    lows = [lows[0]] + [moved(lows[k], k) for k in range(1, DP)]
    ending = state_scan(payload, True, 1)
    (partial,) = call(
        outer_kernel, [((SEQ * PIECE, 128), BF16)], [], (*lows, cotangent, cot_1, cot_2, cot_3),
        flops=4_000_000_000, name="outer",
    )
    gin, tail, back, gstep, gfilt, ghead = call(
        last_kernel,
        [((TOKENS, CHANNELS), BF16), ((8, CHANNELS), F32), ((8, CHANNELS), F32), ((HEADS, TOKENS), F32),
         ((TAPS + 1, CHANNELS), F32), ((8, 128), F32)],
        [vmem(TOKENS + 8, 128), vmem(TOKENS + 16, 128), vmem(*wide), vmem(*wide), vmem(TOKENS, CHANNELS),
         vmem(*small), vmem(*small), vmem(8, 128), vmem(*small)],
        (raw_rows, halo, filter_taps, fbias, act, *heads, skip, entering, ending, dy, dx, dq, dk, dcum, dskip),
        flops=8_000_000_000,
        name="last",
    )
    returned = lax.ppermute(back, "seq", [(s + 1, s) for s in range(SEQ - 1)])
    parts = jnp.concatenate([gfilt.ravel(), dnorm.ravel(), ghead[:3, :HEADS].ravel()])
    count = parts.shape[0]
    parts = jnp.concatenate([parts, jnp.zeros((SEQ * 1024 - count,), F32)]).reshape(SEQ, 8, 128)
    wsum, ssum = call(
        sum_kernel,
        [((SEQ, PIECE, 128), BF16), ((SEQ, 8, 128), F32)],
        [vmem(SEQ, PIECE, 128, kind=BF16), vmem(SEQ, 8, 128), vmem(PIECE, 128, kind=BF16), vmem(8, 128),
         vmem(DP, 8, 128), vmem(PIECE, 128), pltpu.SemaphoreType.DMA((8, SEQ)), pltpu.SemaphoreType.DMA((2, DP))],
        (partial.reshape(SEQ, PIECE, 128), parts),
        collective=2,
        flops=30_000_000_000,
        name="sums",
    )
    weight_grad = wsum.reshape(SEQ * PIECE, 128)[: 10 * ROWS].reshape(10, ROWS, 128).transpose(1, 0, 2)
    weight_grad = weight_grad.reshape(ROWS, WIDTH).astype(F32)
    sums = ssum.ravel()
    filters, norms = (TAPS + 1) * CHANNELS, INNER
    filter_grads = sums[:filters].reshape(TAPS + 1, CHANNELS)
    norm_grad = sums[filters : filters + norms]
    head_grads = sums[filters + norms : count].reshape(3, HEADS)
    tail = jnp.concatenate([tail[:5], tail[5:] + returned[:3]], axis=0).astype(BF16)
    input_grad = lax.dynamic_update_slice(gin, tail, (TOKENS - 8, 0))
    return input_grad[None], gate_grad[None], gstep[None], weight_grad, filter_grads, norm_grad, head_grads


def solution(mesh):
    tokens, by_head, rows = P("dp", "seq", None), P("dp", None, "seq"), P("dp", None)
    return jax.shard_map(
        body,
        mesh=mesh,
        in_specs=(tokens, tokens, by_head, P(), P(), P(), P(), P(), P(), rows, tokens),
        out_specs=(tokens, tokens, by_head, rows, P(), P(), P()),
        check_vma=False,
    )
```

time: 971 us -> 345 us (0.36)
  waiting for transfers between devices: 570 us -> 41.9 us
  Pallas kernels: 0 us -> 254 us
  blocking collectives: 139 us -> 0 us
  matrix products: 86.4 us -> 0 us
  other arithmetic: 81.4 us -> 1.84 us
  local copies, waits for them, and re-layouts: 50.3 us -> 27.4 us
  between operations: 17.5 us -> 0.83 us
    all_gather x8 -> x0, waiting for transfers between devices: 371 us -> none  [the longest x6 191 us: carried_in(): pieces = jax.tree.map(lambda part: lax.all_gather(part, axis), total)]
    pallas_call x0 -> x7, Pallas kernels: none -> 254 us  [call(): pl.pallas_call(kernel, out_shape=[jax.ShapeDtypeStruct(shape, kind) for s...]
    psum x1 -> x0, waiting for transfers between devices: 121 us -> none  [in_one(): total = lax.psum(jnp.concatenate([a.ravel() for a in arrays]), axis)]
    unnamed x2 -> x0, blocking collectives: 110 us -> none
    dot_general x14 -> x0, matrix products: 86.4 us -> none  [the longest x3 40.6 us: finish(): inside = jnp.einsum('hcts,cshp->cthp', weights, scaled, precision=HIGHEST)]
    reduce_scatter x1 -> x0, waiting for transfers between devices: 55.9 us -> none  [body(): lax.psum_scatter(lax.dot_general(normed_low, cotangent, (((0,), (0,)), ((...]
    ppermute x2 -> x11, waiting for transfers between devices: 0.01 us -> 41.9 us  [the longest x1 29.6 us: body(): weight_2 = lax.ppermute(output_weight, ('seq', 'dp'), crossing)]
    all_gather x4 -> x0, blocking collectives: 28.5 us -> none  [carried_in(): pieces = jax.tree.map(lambda part: lax.all_gather(part, axis), total)]
  transfers between devices with their start and end apart: 19 -> 11, of which waited for: 11 -> 3; matrix products, arithmetic and copies ran while one was open for 16% -> 4% of each run, Pallas kernels for 0% -> 53%
where the time goes in v1:
time: 345 us; the launch traced here: 340 us
  Pallas kernels  254 us (74%)
  waiting for transfers between devices  41.9 us (12%)
  local copies, waits for them, and re-layouts  27.4 us (8%)
  starting transfers between devices  14.4 us (4%)
    pallas_call x7, Pallas kernels, call(): pl.pallas_call(kernel, out_shape=[jax.ShapeDtypeStruct(shape, kind) for s...  254 us
    ppermute x1, waiting for transfers between devices, body(): weight_2 = lax.ppermute(output_weight, ('seq', 'dp'), crossing)  29.6 us
    ppermute x8, waiting for transfers between devices, moved(): return lax.ppermute(value, 'dp', [(d, d ^ bits) for d in range(DP)])  10.3 us
    unnamed x17, local copies, waits for them, and re-layouts  7.13 us
  transfers between devices with their start and end apart: 11, of which 3 were waited for; matrix products, arithmetic and copies ran while one was open for 4% of the time, Pallas kernels for 53%

profile of v1, /device:TPU:0, one launch (start us, length us, event | category | flops | bytes accessed | tf_op | source)
XLA Modules:
  0.0 340.3 jit_solution(4502037170775058971)
XLA Ops:
  0.6 3.2 collective-permute-start.2
  4.6 3.8 %collective-permute-start = (bf16[8,2816]{1,0:T(8,128)(2,1)S(1)}, bf16[8,2816]{1,0:T(8,128)(2,1)S(1)}, u32[]{:S(2)}, u32[]{:S(2)}) collective-permute-start(bf16[8,2816]{1,0:T(8,128)(2,1)S(1)} %slice_bitcast_fusion), channel_id=1, source_target_pairs={{0,4},{4,8},{8,12},{12,16},{16,20},{20,24},{24,28},{28,32},{32,36}... | collective-permute-start | bytes 135176 | tf_op jit(solution)/shard_map/ppermute | solution.py:540
  9.4 1.3 copy.32.sbias_ref
  10.7 1.3 copy.33.dlog_ref
  12.1 1.3 broadcast_in_dim.30.fbias_ref
  14.8 1.3 broadcast_in_dim.35.weight_ref
  16.7 7.5 %first.1 = (f32[256,2816]{1,0:T(8,128)}, f32[2,128,1408]{2,1,0:T(8,128)}) custom-call(bf16[256,2816]{1,0:T(8,128)(2,1)} %bitcast.36, bf16[8,2816]{1,0:T(8,128)(2,1)} %copy-done.7, f32[4,2816]{1,0:T(4,128)} %taps_ref.3, f32[1,2816]{1,0:T(1,128)} %broadcast_in_dim.30.fbias_ref, f32[40,256]{1,0:T(8,128)} %bitcast.46, f32[40,1]{1,0:T(8,128)} %copy.32.sbias_ref, ...), custom_call_target="tpu_custom_call" | custom-call | flops 5000000000 | tf_op jit(solution)/shard_map/first/pallas_call | solution.py:500
  24.3 29.6 %collective-permute-done.2.w2_ref = bf16[640,1280]{1,0:T(8,128)(2,1)S(1)} collective-permute-done((bf16[640,1280]{1,0:T(8,128)(2,1)}, bf16[640,1280]{1,0:T(8,128)(2,1)S(1)}, u32[]{:S(2)}, u32[]{:S(2)}) %collective-permute-start.2) | collective-permute-done | bytes 1638432 | tf_op jit(solution)/shard_map/ppermute | solution.py:541
  53.9 53.9 %scan_on.1 = f32[32,8,1280]{2,1,0:T(8,128)} custom-call(f32[32,8,1408]{2,1,0:T(8,128)} %bitcast.51), custom_call_target="tpu_custom_call" | custom-call | flops 30000001024 | tf_op jit(solution)/shard_map/scan_on/pallas_call | solution.py:500
  108.2 1.2 copy-done.3
  109.4 37.9 %middle.1 = (bf16[256,2560]{1,0:T(8,128)(2,1)}, bf16[256,2560]{1,0:T(8,128)(2,1)}, f32[2,128,1408]{2,1,0:T(8,128)}, f32[256,2560]{1,0:T(8,128)}, f32[256,2560]{1...) custom-call(s32[1]{0:T(128)} %bitcast.7.dp_ref, ...), custom_call_target="tpu_custom_call" | custom-call | flops 20000000000 | tf_op jit(solution)/shard_map/middle/pallas_call | solution.py:500
  147.3 53.5 %scan_back.1 = f32[32,8,1280]{2,1,0:T(8,128)} custom-call(f32[32,8,1408]{2,1,0:T(8,128)} %bitcast.50), custom_call_target="tpu_custom_call" | custom-call | flops 30000001024 | tf_op jit(solution)/shard_map/scan_back/pallas_call | solution.py:500
  201.6 4.7 %collective-permute-start.6 = (bf16[256,640]{1,0:T(8,128)(2,1)S(1)}, bf16[256,640]{1,0:T(8,128)(2,1)S(1)}, u32[]{:S(2)}, u32[]{:S(2)}) collective-permute-start(bf16[256,640]{1,0:T(8,128)(2,1)S(1)} %get-tuple-element.62), channel_id=1, source_target_pairs={{0,2},{1,3},{2,0},{3,1},{4,6},{5,7},{6,4},{7,5},{8,10},{9,11},{10,... | collective-permute-start | bytes 983048 | tf_op jit(solution)/shard_map/ppermute | solution.py:530
  206.3 26.1 %last.1 = (bf16[256,2816]{1,0:T(8,128)(2,1)}, f32[8,2816]{1,0:T(8,128)}, f32[8,2816]{1,0:T(8,128)}, f32[40,256]{1,0:T(8,128)}, f32[5,2816]{1,0:T(8,128)}, /*index=5*/f32[8,128]{1,0:T(8,128)}) custom-call(bf16[256,2816]{1,0:T(8,128)(2,1)} %bitcast.37, bf16[8,2816]{1,0:T(8,128)(2,1)} %copy-done.7, f32[4,2816]{1,0:T(4,128)} %taps_ref.3, ...), custom_call_target="tpu_custom_call" | custom-call | flops 8000000000 | tf_op jit(solution)/shard_map/last/pallas_call | solution.py:500
  232.4 1.5 collective-permute-start.4
  237.3 2.0 collective-permute-done.4
  239.3 0.9 fusion.2
  240.9 10.3 %collective-permute-done.7.l3 = bf16[256,640]{1,0:T(8,128)(2,1)S(1)} collective-permute-done((bf16[256,640]{1,0:T(8,128)(2,1)S(1)}, bf16[256,640]{1,0:T(8,128)(2,1)S(1)}, u32[]{:S(2)}, u32[]{:S(2)}) %collective-permute-start.7) | collective-permute-done | bytes 327712 | tf_op jit(solution)/shard_map/ppermute | solution.py:530
  251.9 5.2 %outer.1 = bf16[6656,128]{1,0:T(8,128)(2,1)} custom-call(bf16[256,640]{1,0:T(8,128)(2,1)} %get-tuple-element.64.l0, bf16[256,640]{1,0:T(8,128)(2,1)} %copy-done.4, bf16[256,640]{1,0:T(8,128)(2,1)} %copy-done.5, bf16[256,640]{1,0:T(8,128)(2,1)} %copy-done.6, bf16[256,1280]{1,0:T(8,128)(2,1)} %bitcast.45, bf16[256,1280]{1,0:T(8,128)(2,1)} %collective-permute-done.8.g1, ...), custom_call_target="tpu_custom_call" | custom-call | flops 4000000000 | tf_op jit(solution)/shard_map/outer/pallas_call | solution.py:500
  257.1 69.7 %sums.1 = (bf16[32,208,128]{2,1,0:T(8,128)(2,1)}, f32[32,8,128]{2,1,0:T(8,128)}) custom-call(bf16[32,208,128]{2,1,0:T(8,128)(2,1)} %bitcast.49, f32[32,8,128]{2,1,0:T(8,128)} %bitcast.32), custom_call_target="tpu_custom_call" | custom-call | flops 30000001024 | tf_op jit(solution)/shard_map/sums/pallas_call | solution.py:500
  327.7 1.3 slice.45
  329.7 1.5 slice.43
  331.5 3.0 copy.38
  334.4 4.6 %copy.39 = f32[640,1280]{1,0:T(8,128)} copy(f32[640,1280]{0,1:T(8,128)} %bitcast.29) | data formatting | bytes 6553600
  (47 shorter events, 12.7 us)
Async XLA Ops:
  0.6 53.3 %collective-permute-start.2 = (bf16[640,1280]{1,0:T(8,128)(2,1)}, bf16[640,1280]{1,0:T(8,128)(2,1)S(1)}, u32[]{:S(2)}, u32[]{:S(2)}) collective-permute-start(bf16[640,1280]{1,0:T(8,128)(2,1)} %w0_ref.1), channel_id=1, source_target_pairs={{0,18},{1,19},{2,16},{3,17},{4,22},{5,23},{6,20},{7,21},{8,26},{9,... | collective-permute-start | bytes 4915208 | tf_op jit(solution)/shard_map/ppermute | solution.py:541
  4.6 11.5 %collective-permute-start = (bf16[8,2816]{1,0:T(8,128)(2,1)S(1)}, bf16[8,2816]{1,0:T(8,128)(2,1)S(1)}, u32[]{:S(2)}, u32[]{:S(2)}) collective-permute-start(bf16[8,2816]{1,0:T(8,128)(2,1)S(1)} %slice_bitcast_fusion), channel_id=1, source_target_pairs={{0,4},{4,8},{8,12},{12,16},{16,20},{20,24},{24,28},{28,32},{32,36}... | collective-permute-start | bytes 135176 | tf_op jit(solution)/shard_map/ppermute | solution.py:540
  8.4 99.7 %collective-permute-start.1 = (bf16[640,1280]{1,0:T(8,128)(2,1)}, bf16[640,1280]{1,0:T(8,128)(2,1)S(1)}, u32[]{:S(2)}, u32[]{:S(2)}) collective-permute-start(bf16[640,1280]{1,0:T(8,128)(2,1)} %w0_ref.1), channel_id=1, source_target_pairs={{0,1},{1,0},{2,3},{3,2},{4,5},{5,4},{6,7},{7,6},{8,9},{9,8},{10,11... | collective-permute-start | bytes 4915208 | tf_op jit(solution)/shard_map/ppermute | solution.py:530
  8.5 99.3 %collective-permute-start.9 = (bf16[256,1280]{1,0:T(8,128)(2,1)}, bf16[256,1280]{1,0:T(8,128)(2,1)}, u32[]{:S(2)}, u32[]{:S(2)}) collective-permute-start(bf16[256,1280]{1,0:T(8,128)(2,1)} %bitcast.42), channel_id=1, source_target_pairs={{0,2},{1,3},{2,0},{3,1},{4,6},{5,7},{6,4},{7,5},{8,10},{9,11},{10,... | collective-permute-start | bytes 1966088 | tf_op jit(solution)/shard_map/ppermute | solution.py:530
  9.3 231.6 %collective-permute-start.8 = (bf16[256,1280]{1,0:T(8,128)(2,1)}, bf16[256,1280]{1,0:T(8,128)(2,1)}, u32[]{:S(2)}, u32[]{:S(2)}) collective-permute-start(bf16[256,1280]{1,0:T(8,128)(2,1)} %bitcast.43), channel_id=1, source_target_pairs={{0,1},{1,0},{2,3},{3,2},{4,5},{5,4},{6,7},{7,6},{8,9},{9,8},{10,11... | collective-permute-start | bytes 1966088 | tf_op jit(solution)/shard_map/ppermute | solution.py:530
  16.1 0.6 copy-start.7
  53.9 54.0 %copy-start.2 = (bf16[640,1280]{1,0:T(8,128)(2,1)}, bf16[640,1280]{1,0:T(8,128)(2,1)S(1)}, u32[]{:S(2)}) copy-start(bf16[640,1280]{1,0:T(8,128)(2,1)S(1)} %collective-permute-done.2.w2_ref) | copy-start | bytes 4915204
  53.9 54.3 %collective-permute-start.3 = (bf16[640,1280]{1,0:T(8,128)(2,1)S(1)}, bf16[640,1280]{1,0:T(8,128)(2,1)}, u32[]{:S(2)}, u32[]{:S(2)}) collective-permute-start(bf16[640,1280]{1,0:T(8,128)(2,1)S(1)} %collective-permute-done.2.w2_ref), channel_id=1, source_target_pairs={{0,1},{1,0},{2,3},{3,2},{4,5},{5,4},{6,7},{7,6},{8,9},{9,8},{10,11... | collective-permute-start | bytes 4915208 | tf_op jit(solution)/shard_map/ppermute | solution.py:530
  107.9 133.0 %collective-permute-start.10 = (bf16[256,1280]{1,0:T(8,128)(2,1)}, bf16[256,1280]{1,0:T(8,128)(2,1)}, u32[]{:S(2)}, u32[]{:S(2)}) collective-permute-start(bf16[256,1280]{1,0:T(8,128)(2,1)} %collective-permute-done.9.g2), channel_id=1, source_target_pairs={{0,1},{1,0},{2,3},{3,2},{4,5},{5,4},{6,7},{7,6},{8,9},{9,8},{10,11... | collective-permute-start | bytes 1966088 | tf_op jit(solution)/shard_map/ppermute | solution.py:530
  108.2 1.2 copy-start.3
  147.3 53.5 %copy-start = (bf16[256,2560]{1,0:T(8,128)(2,1)S(1)}, bf16[256,2560]{1,0:T(8,128)(2,1)}, u32[]{:S(2)}) copy-start(bf16[256,2560]{1,0:T(8,128)(2,1)} %get-tuple-element.41) | copy-start | bytes 3932164
  201.6 39.2 %collective-permute-start.5 = (bf16[256,640]{1,0:T(8,128)(2,1)S(1)}, bf16[256,640]{1,0:T(8,128)(2,1)S(1)}, u32[]{:S(2)}, u32[]{:S(2)}) collective-permute-start(bf16[256,640]{1,0:T(8,128)(2,1)S(1)} %get-tuple-element.63), channel_id=1, source_target_pairs={{0,1},{1,0},{2,3},{3,2},{4,5},{5,4},{6,7},{7,6},{8,9},{9,8},{10,11... | collective-permute-start | bytes 983048 | tf_op jit(solution)/shard_map/ppermute | solution.py:530
  201.6 39.2 %collective-permute-start.6 = (bf16[256,640]{1,0:T(8,128)(2,1)S(1)}, bf16[256,640]{1,0:T(8,128)(2,1)S(1)}, u32[]{:S(2)}, u32[]{:S(2)}) collective-permute-start(bf16[256,640]{1,0:T(8,128)(2,1)S(1)} %get-tuple-element.62), channel_id=1, source_target_pairs={{0,2},{1,3},{2,0},{3,1},{4,6},{5,7},{6,4},{7,5},{8,10},{9,11},{10,... | collective-permute-start | bytes 983048 | tf_op jit(solution)/shard_map/ppermute | solution.py:530
  206.3 30.2 %copy-start.1 = (f32[1,2560]{1,0:T(1,128)S(1)}, f32[1,2560]{1,0:T(1,128)}, u32[]{:S(2)}) copy-start(f32[1,2560]{1,0:T(1,128)} %get-tuple-element.43) | copy-start | bytes 30724
  232.4 6.9 %collective-permute-start.4 = (f32[8,2816]{1,0:T(8,128)}, f32[8,2816]{1,0:T(8,128)S(1)}, u32[]{:S(2)}, u32[]{:S(2)}) collective-permute-start(f32[8,2816]{1,0:T(8,128)} %get-tuple-element.38), channel_id=1, source_target_pairs={{4,0},{8,4},{12,8},{16,12},{20,16},{24,20},{28,24},{32,28},{36,32}... | collective-permute-start | bytes 270344 | tf_op jit(solution)/shard_map/ppermute | solution.py:592
  239.3 11.9 %collective-permute-start.7 = (bf16[256,640]{1,0:T(8,128)(2,1)S(1)}, bf16[256,640]{1,0:T(8,128)(2,1)S(1)}, u32[]{:S(2)}, u32[]{:S(2)}) collective-permute-start(bf16[256,640]{1,0:T(8,128)(2,1)S(1)} %get-tuple-element.61), channel_id=1, source_target_pairs={{0,3},{1,2},{2,1},{3,0},{4,7},{5,6},{6,5},{7,4},{8,11},{9,10},{10,... | collective-permute-start | bytes 983048 | tf_op jit(solution)/shard_map/ppermute | solution.py:530
  240.8 10.3 %copy-start.4 = (bf16[256,640]{1,0:T(8,128)(2,1)}, bf16[256,640]{1,0:T(8,128)(2,1)S(1)}, u32[]{:S(2)}) copy-start(bf16[256,640]{1,0:T(8,128)(2,1)S(1)} %collective-permute-done.5.l1) | copy-start | bytes 983044
  240.9 10.3 %copy-start.5 = (bf16[256,640]{1,0:T(8,128)(2,1)}, bf16[256,640]{1,0:T(8,128)(2,1)S(1)}, u32[]{:S(2)}) copy-start(bf16[256,640]{1,0:T(8,128)(2,1)S(1)} %collective-permute-done.6.l2) | copy-start | bytes 983044
  251.2 0.7 copy-start.6

commit v2 on v0

v2 whole, which is shorter than its diff:
```python
import jax
import jax.numpy as jnp
from jax import lax
from jax.experimental import pallas as pl
from jax.experimental.pallas import tpu as pltpu
from jax.sharding import PartitionSpec as P

HEADS = 40
HEAD_DIM = 64
STATE = 128
INNER = 2560
CHANNELS = 2816
WIDTH = 1280
TOKENS = 256
TAPS = 4
PAIRS = 20
HALF = 1280
CHUNK = HALF + 128
SEQ = 32
DP = 4
ROWS = INNER // DP
EDGE = 16
PIECE = 208
MASKED = -1e30
EPSILON = 1e-05

F32 = jnp.float32
BF16 = jnp.bfloat16
MESH = pl.DeviceIdType.MESH
NN = ((1,), (0,))
NT = ((1,), (1,))
TN = ((0,), (0,))


def mm(a, b, dims):
    return lax.dot_general(a, b, (dims, ((), ())), preferred_element_type=F32)


def split(x):
    high = x.astype(BF16)
    return high, (x - high.astype(F32)).astype(BF16)


def dot3(a, b, dims):
    return mm(a[0], b[0], dims) + mm(a[0], b[1], dims) + mm(a[1], b[0], dims)


def iota(shape, dim):
    return lax.broadcasted_iota(jnp.int32, shape, dim)


def lanes(p):
    return pl.ds(pl.multiple_of(p * 128, 128), 128)


def turned(x):
    return jnp.transpose(jnp.concatenate([x, jnp.zeros((128 - HEADS, TOKENS), F32)], axis=0))


def rates_of(step_ref, table_ref):
    columns = jnp.transpose(jnp.concatenate([table_ref[7:9, :128], jnp.zeros((126, 128), F32)], axis=0))
    raw = step_ref[...] + columns[:HEADS, 0:1]
    sizes = jnp.maximum(raw, 0.0) + jnp.log1p(jnp.exp(-jnp.abs(raw)))
    gain = -jnp.exp(columns[:HEADS, 1:2])
    rates = sizes * gain
    lane = iota(rates.shape, 1)
    cums = rates
    shift = 1
    while shift < TOKENS:
        cums = cums + jnp.where(lane >= shift, pltpu.roll(cums, shift, 1), 0.0)
        shift *= 2
    return raw, sizes, gain, rates, cums


def widen(columns, p):
    first = iota((TOKENS, 128), 1) < HEAD_DIM
    return jnp.where(first, columns[:, 2 * p : 2 * p + 1], columns[:, 2 * p + 1 : 2 * p + 2])


def head_sum(v, p):
    into = (iota((128, 128), 1) == 2 * p + iota((128, 128), 0) // HEAD_DIM).astype(BF16)
    high, low = split(v)
    return mm(high, into, NN) + mm(low, into, NN)


def sigmoid(x):
    return 1.0 / (1.0 + jnp.exp(-x))


def filtered_of(x_ref, table_ref, ext_ref, edge, cols):
    ext_ref[0:EDGE, :] = edge
    ext_ref[EDGE : EDGE + TOKENS, :] = x_ref[:, cols].astype(F32)
    total = table_ref[TAPS : TAPS + 1, cols]
    for k in range(TAPS):
        at = EDGE - TAPS + 1 + k
        total = total + table_ref[k : k + 1, cols] * ext_ref[at : at + TOKENS, :]
    return total


def write_decays(pay_ref, cums_turned):
    decays = jnp.exp(cums_turned[TOKENS - 1 : TOKENS, :])
    for c in range(SEQ):
        pay_ref[c, :, HALF:] = jnp.broadcast_to(decays, (8, 128))


def write_state(pay_ref, p, state):
    half = p // (PAIRS // 2)
    at = lanes(p - half * (PAIRS // 2))
    for c in range(SEQ // 2):
        pay_ref[half * (SEQ // 2) + c, :, at] = state[c * 8 : c * 8 + 8, :]


def read_state(ref, p):
    half = p // (PAIRS // 2)
    at = lanes(p - half * (PAIRS // 2))
    return jnp.concatenate([ref[half * (SEQ // 2) + c, :, at] for c in range(SEQ // 2)], axis=0)


def to_peer(src, dst, send, recv, device):
    return pltpu.make_async_remote_copy(
        src_ref=src, dst_ref=dst, send_sem=send, recv_sem=recv, device_id=device, device_id_type=MESH
    )


def greet(seq, dp, others):
    barrier = pltpu.get_barrier_semaphore()

    def hello(i, carry):
        peer = lax.rem(seq + i, SEQ)
        pl.semaphore_signal(barrier, inc=1, device_id=(peer, dp), device_id_type=MESH)
        return carry

    lax.fori_loop(1, SEQ, hello, 0)
    for other in others:
        pl.semaphore_signal(barrier, inc=1, device_id=other, device_id_type=MESH)
    pl.semaphore_wait(barrier, SEQ - 1 + len(others))


def each_peer(seq, act):
    def step(i, carry):
        act(i, lax.rem(seq + i, SEQ))
        return carry

    lax.fori_loop(1, SEQ, step, 0)


class Scatter:
    def __init__(self, seq, dp, src, dst, sems, row, whole=False):
        self.seq, self.dp, self.src, self.dst, self.sems, self.row, self.whole = seq, dp, src, dst, sems, row, whole

    def copy(self, i, peer, slot):
        src = self.src if self.whole else self.src.at[peer]
        sems = self.sems
        return to_peer(src, self.dst.at[slot], sems.at[self.row, i], sems.at[self.row + 1, slot], (peer, self.dp))

    def start(self):
        each_peer(self.seq, lambda i, peer: self.copy(i, peer, self.seq).start())
        self.dst[self.seq] = self.src[...] if self.whole else self.src[self.seq]

    def received(self):
        each_peer(self.seq, lambda i, peer: self.copy(i, peer, peer).wait_recv())

    def sent(self):
        each_peer(self.seq, lambda i, peer: self.copy(i, peer, self.seq).wait_send())


def scan_chunks(seq, reverse, recv, outgoing, coef):
    decays = jnp.concatenate([recv[k, 0:1, HALF:] for k in range(SEQ)], axis=0)
    head = (seq // (SEQ // 2)) * (HEADS // 2) + iota((128, HALF), 1) // HEAD_DIM
    into = (iota((128, HALF), 0) == head).astype(F32)
    wide = lax.dot_general(
        decays, into, (NN, ((), ())), preferred_element_type=F32, precision=lax.Precision.HIGHEST
    )
    for k in range(SEQ):
        coef[k] = wide[k : k + 1, :]

    def scan(j, state):
        k = SEQ - 1 - j if reverse else j
        outgoing[k] = state
        return coef[k] * state + recv[k, :, :HALF]

    lax.fori_loop(0, SEQ, scan, jnp.zeros((8, HALF), F32))


def place():
    seq, dp = lax.axis_index("seq"), lax.axis_index("dp")
    partner = dp + 1 - 2 * lax.rem(dp, 2)
    across = lax.rem(dp + 2, DP)
    return seq, dp, partner, across


def forward_kernel(
    x_ref, table_ref, step_ref, cot_ref, w_ref,
    act_ref, inside_ref, ng_ref, ent_ref, halo_ref,
    edge_ref, ext_ref, pay_ref, recv, outgoing, coef, wrecv, col_ref, cum_ref, stepx_ref, scores_ref, sems, wsems, hsems,
):
    seq, dp, partner, across = place()
    beside = seq + 4 - 8 * lax.rem(seq // 4, 2)
    after, before = lax.rem(seq + 1, SEQ), lax.rem(seq + SEQ - 1, SEQ)
    greet(seq, dp, [(seq, partner), (beside, across)])
    last_rows = x_ref.at[pl.ds(TOKENS - EDGE, EDGE)]
    halo = to_peer(last_rows, edge_ref, hsems.at[0], hsems.at[1], (after, dp))
    halo.start()
    quarter = ROWS // 4

    def piece(q):
        return pl.ds(q * quarter, quarter)

    cross = [
        to_peer(w_ref.at[piece(q)], wrecv.at[1, piece(q)], wsems.at[0, q], wsems.at[1, q], (beside, across))
        for q in range(4)
    ]
    relay = [
        to_peer(wrecv.at[1, piece(q)], wrecv.at[2, piece(q)], wsems.at[2, q], wsems.at[3, q], (seq, partner))
        for q in range(4)
    ]
    near = to_peer(w_ref, wrecv.at[0], wsems.at[4, 0], wsems.at[5, 0], (seq, partner))
    for copy in cross:
        copy.start()
    near.start()
    _, sizes, _, _, cums = rates_of(step_ref, table_ref)
    cum_t = turned(cums)
    size_t = turned(sizes)
    end_t = turned(jnp.exp(cums[:, TOKENS - 1 :] - cums) * sizes)
    write_decays(pay_ref, cum_t)
    halo.wait_recv()
    halo_ref[...] = jnp.where(seq > 0, edge_ref[...].astype(F32), 0.0)

    def activate(j, carry):
        cols = lanes(j)
        f = filtered_of(x_ref, table_ref, ext_ref, halo_ref[:, cols], cols)
        act_ref[:, cols] = f * sigmoid(f)
        return carry

    lax.fori_loop(0, CHANNELS // 128, activate, 0)
    key = act_ref[:, INNER : INNER + STATE]
    key_turned = split(jnp.transpose(key))
    for p in range(PAIRS):
        a = act_ref[:, p * 128 : p * 128 + 128] * widen(end_t, p)
        write_state(pay_ref, p, dot3(key_turned, split(a), NN))
    out = Scatter(seq, dp, pay_ref, recv, sems, 0)
    out.start()

    for h in range(HEADS):
        cum_ref[h] = cums[h : h + 1, :]
        col_ref[h] = jnp.broadcast_to(cum_t[:, h : h + 1], (TOKENS, 128))
    for p in range(PAIRS):
        stepx_ref[:, p * 128 : p * 128 + 128] = widen(size_t, p)
    query = act_ref[:, INNER + STATE :]
    scores_ref[...] = dot3(split(query), split(key), NT)
    first = iota((TOKENS, 128), 1) < HEAD_DIM
    causal = iota((TOKENS, TOKENS), 0) >= iota((TOKENS, TOKENS), 1)

    def forward(p, carry):
        cols = lanes(p)
        high, low = split(act_ref[:, cols] * stepx_ref[:, cols])
        both = jnp.concatenate([high, low], axis=1)
        parts = []
        for i in range(2):
            h = 2 * p + i
            c = col_ref[h]
            e = jnp.exp(jnp.where(causal, jnp.concatenate([c, c], axis=1) - cum_ref[h], MASKED))
            wh, wl = split(scores_ref[...] * e)
            r = mm(wh, both, NN)
            parts.append(r[:, :128] + r[:, 128:] + mm(wl, high, NN))
        inside_ref[:, cols] = jnp.where(first, parts[0], parts[1])
        return carry

    def normed_grad(block, weights):
        at = pl.multiple_of(block * ROWS, 128)
        ng_ref[:, pl.ds(at, ROWS)] = mm(cot_ref[...], weights[...], NT)

    lax.fori_loop(0, PAIRS, forward, 0)
    normed_grad(dp, w_ref)
    out.received()
    scan_chunks(seq, False, recv, outgoing, coef)
    back = Scatter(seq, dp, outgoing, ent_ref, sems, 2)
    back.start()
    near.wait_recv()
    normed_grad(partner, wrecv.at[0])
    for q in range(4):
        cross[q].wait_recv()
        relay[q].start()
    normed_grad(across, wrecv.at[1])
    for copy in relay:
        copy.wait_recv()
    normed_grad(DP - 1 - dp, wrecv.at[2])
    back.received()
    for copy in [halo, near, *cross, *relay]:
        copy.wait_send()
    out.sent()
    back.sent()


def backward_kernel(
    act_ref, gate_ref, table_ref, step_ref, ent_ref, inside_ref, ng_ref, cot_ref,
    ggate_ref, dy_ref, dx_ref, dq_ref, dk_ref, dcum_ref, dnorm_ref, dskip_ref, end_ref, part_ref,
    pay_ref, recv, outgoing, coef, low_ref, lrecv, crecv, col_ref, cum_ref, stepx_ref, expx_ref, turn_ref, scan_ref,
    acc_ref, dsc_ref, sems, dsems,
):
    seq, dp, partner, across = place()
    corner = DP - 1 - dp
    greet(seq, dp, [(seq, partner), (seq, across), (seq, corner)])
    near = to_peer(cot_ref, crecv.at[0], dsems.at[0, 0], dsems.at[1, 0], (seq, partner))
    cross = to_peer(cot_ref, crecv.at[1], dsems.at[0, 1], dsems.at[1, 1], (seq, across))
    relay = to_peer(crecv.at[1], crecv.at[2], dsems.at[0, 2], dsems.at[1, 2], (seq, partner))
    near.start()
    cross.start()

    _, sizes, _, _, cums = rates_of(step_ref, table_ref)
    cum_t = turned(cums)
    size_t = turned(sizes)
    exp_t = jnp.exp(cum_t)
    write_decays(pay_ref, cum_t)
    for p in range(PAIRS):
        expx_ref[:, p * 128 : p * 128 + 128] = widen(exp_t, p)
    query = act_ref[:, INNER + STATE :]
    query_s = split(query)
    query_turned = split(jnp.transpose(query))
    acc_ref[...] = jnp.zeros_like(acc_ref)

    def forward(p, carry):
        cols = lanes(p)
        carried = dot3(query_s, split(read_state(ent_ref, p)), NN) * expx_ref[:, cols]
        scanned = inside_ref[:, cols] + carried + table_ref[6:7, cols] * act_ref[:, cols]
        scan_ref[:, cols] = scanned
        gate = gate_ref[:, cols].astype(F32)
        gated = scanned * (gate * sigmoid(gate))
        acc_ref[...] += gated * gated
        return carry

    lax.fori_loop(0, PAIRS, forward, 0)
    inverse = lax.rsqrt(jnp.sum(acc_ref[...], axis=1, keepdims=True) / INNER + EPSILON)
    acc_ref[...] = jnp.zeros_like(acc_ref)

    def norm(p, carry):
        cols = lanes(p)
        gate = gate_ref[:, cols].astype(F32)
        gated = scan_ref[:, cols] * (gate * sigmoid(gate))
        weight = table_ref[5:6, cols]
        unit = gated * inverse
        block = p // 5
        low_ref[block, :, lanes(p - block * 5)] = (unit * weight).astype(BF16)
        ng = ng_ref[:, cols]
        dnorm_ref[:, cols] = jnp.sum(ng * unit, axis=0, keepdims=True)
        acc_ref[...] += ng * weight * gated
        return carry

    lax.fori_loop(0, PAIRS, norm, 0)
    lows = [
        to_peer(low_ref.at[other], lrecv.at[k], dsems.at[2, k], dsems.at[3, k], (seq, other))
        for k, other in enumerate((partner, across, corner))
    ]
    for copy in lows:
        copy.start()
    lean = jnp.sum(acc_ref[...], axis=1, keepdims=True) * (inverse * inverse * inverse) / INNER

    def cotangents(p, carry):
        cols = lanes(p)
        gate = gate_ref[:, cols].astype(F32)
        gain = sigmoid(gate)
        silu = gate * gain
        scanned = scan_ref[:, cols]
        dgated = inverse * (ng_ref[:, cols] * table_ref[5:6, cols]) - scanned * silu * lean
        ggate_ref[:, cols] = (dgated * scanned * (gain * (1.0 + gate * (1.0 - gain)))).astype(BF16)
        dy = dgated * silu
        dy_ref[:, cols] = dy
        write_state(pay_ref, p, dot3(query_turned, split(dy * expx_ref[:, cols]), NN))
        return carry

    lax.fori_loop(0, PAIRS, cotangents, 0)
    out = Scatter(seq, dp, pay_ref, recv, sems, 0)
    out.start()

    for h in range(HEADS):
        cum_ref[h] = cums[h : h + 1, :]
        col_ref[h] = jnp.broadcast_to(cum_t[:, h : h + 1], (TOKENS, 128))
    for p in range(PAIRS):
        stepx_ref[:, p * 128 : p * 128 + 128] = widen(size_t, p)
    key_s = split(act_ref[:, INNER : INNER + STATE])
    turn_ref[...] = dot3(key_s, query_s, NT)
    first = iota((TOKENS, 128), 1) < HEAD_DIM
    causal = iota((TOKENS, TOKENS), 1) >= iota((TOKENS, TOKENS), 0)
    for ref in (dsc_ref, dq_ref, dcum_ref, dskip_ref):
        ref[...] = jnp.zeros_like(ref)

    def backward(p, carry):
        cols = lanes(p)
        dy = dy_ref[:, cols]
        dh, dl = split(dy)
        both = jnp.concatenate([dh, dl], axis=1)
        twice = jnp.concatenate([dh, dh], axis=1)
        values = act_ref[:, cols]
        scaled = values * stepx_ref[:, cols]
        parts = []
        for i in range(2):
            h = 2 * p + i
            c = col_ref[h]
            e = jnp.exp(jnp.where(causal, cum_ref[h] - jnp.concatenate([c, c], axis=1), MASKED))
            wh, wl = split(turn_ref[...] * e)
            r = mm(wh, both, NN)
            parts.append(r[:, :128] + r[:, 128:] + mm(wl, dh, NN))
            own = first if i == 0 else jnp.logical_not(first)
            xh, xl = split(jnp.where(own, scaled, 0.0))
            dw = mm(jnp.concatenate([xh, xl], axis=1), twice, NT) + mm(xh, dl, NT)
            dsc_ref[...] += dw * e
        dx = jnp.where(first, parts[0], parts[1])
        dx_ref[:, cols] = dx
        dq_ref[...] += dot3(split(dy * expx_ref[:, cols]), split(read_state(ent_ref, p)), NT)
        skipped = dy * values
        dcum_ref[...] += head_sum(dy * scan_ref[:, cols] - skipped * table_ref[6:7, cols] - scaled * dx, p)
        dskip_ref[...] += head_sum(jnp.sum(skipped.reshape(TOKENS // 8, 8, 128), axis=0), p)
        return carry

    lax.fori_loop(0, PAIRS, backward, 0)
    out.received()
    scan_chunks(seq, True, recv, outgoing, coef)
    back = Scatter(seq, dp, outgoing, end_ref, sems, 2)
    back.start()
    cross.wait_recv()
    relay.start()
    dsc = dsc_ref[...]
    dk_ref[...] = dot3(split(dsc), query_s, NN)
    dq_ref[...] += dot3(split(jnp.transpose(dsc)), key_s, NN)
    near.wait_recv()
    for copy in lows:
        copy.wait_recv()
    relay.wait_recv()
    left = [jnp.transpose(block) for block in (low_ref[dp], lrecv[0], lrecv[1], lrecv[2])]
    right = [cot_ref, crecv.at[0], crecv.at[1], crecv.at[2]]
    for j in range(WIDTH // 256):
        total = mm(left[0], right[0][:, j * 256 : j * 256 + 256], NN)
        for k in range(1, DP):
            total = total + mm(left[k], right[k][:, j * 256 : j * 256 + 256], NN)
        for i in range(2):
            at = (2 * j + i) * ROWS
            part_ref[at : at + ROWS, :] = total[:, i * 128 : i * 128 + 128].astype(BF16)
    part_ref[10 * ROWS :, :] = jnp.zeros((SEQ * PIECE - 10 * ROWS, 128), BF16)
    back.received()
    for copy in [near, cross, relay, *lows]:
        copy.wait_send()
    out.sent()
    back.sent()


def last_kernel(
    x_ref, halo_ref, table_ref, act_ref, step_ref, ent_ref, end_ref, dy_ref, dx_ref, dq_ref, dk_ref, dcum_ref,
    dnorm_ref, dskip_ref, wide_ref,
    gin_ref, gstep_ref, gfilt_ref, gnorm_ref, ghead_ref, gweight_ref,
    ext_ref, dfilt_ref, stepx_ref, endx_ref, dact_ref, dstep_ref, zsum_ref, ded_ref, dkey_ref,
    tail_ref, ret_ref, rrecv, small_ref, srecv, sall, sown, sdp, wrecv, wall, wown, wacc, sems, dsems, hsems,
):
    seq, dp, partner, across = place()
    after, before = lax.rem(seq + 1, SEQ), lax.rem(seq + SEQ - 1, SEQ)
    greet(seq, dp, [(seq, lax.rem(dp + k, DP)) for k in range(1, DP)])
    spread = Scatter(seq, dp, wide_ref, wrecv, sems, 2)
    spread.start()

    raw, sizes, gain, rates, cums = rates_of(step_ref, table_ref)
    size_t = turned(sizes)
    end_t = turned(jnp.exp(cums[:, TOKENS - 1 :] - cums))
    for p in range(PAIRS):
        stepx_ref[:, p * 128 : p * 128 + 128] = widen(size_t, p)
        endx_ref[:, p * 128 : p * 128 + 128] = widen(end_t, p)
    key_s = split(act_ref[:, INNER : INNER + STATE])
    for ref in (dstep_ref, zsum_ref, ded_ref):
        ref[...] = jnp.zeros_like(ref)
    dkey_ref[...] = dk_ref[...]

    def pair(p, carry):
        cols = lanes(p)
        values = act_ref[:, cols]
        step = stepx_ref[:, cols]
        ending = endx_ref[:, cols]
        end = read_state(end_ref, p)
        end_s = split(end)
        z = dot3(key_s, end_s, NN) * ending
        dx = dx_ref[:, cols] + z
        dact_ref[:, cols] = dx * step + table_ref[6:7, cols] * dy_ref[:, cols]
        dstep_ref[...] += head_sum(dx * values, p)
        scaled = values * step
        zsum_ref[...] += head_sum(scaled * z, p)
        dkey_ref[...] += dot3(split(scaled * ending), end_s, NT)
        both = end * read_state(ent_ref, p)
        ded_ref[...] += head_sum(jnp.sum(both.reshape(STATE // 8, 8, 128), axis=0), p)
        return carry

    lax.fori_loop(0, PAIRS, pair, 0)
    dact_ref[:, INNER : INNER + STATE] = dkey_ref[...]
    dact_ref[:, INNER + STATE :] = dq_ref[...]
    dfilt_ref[0:8, :] = jnp.zeros((8, 128), F32)
    dfilt_ref[8 + TOKENS :, :] = jnp.zeros((8, 128), F32)
    small_ref[...] = jnp.zeros_like(small_ref)

    def filters(j, carry):
        cols = lanes(j)
        f = filtered_of(x_ref, table_ref, ext_ref, halo_ref[:, cols], cols)
        s = sigmoid(f)
        dfilt = dact_ref[:, cols] * (s * (1.0 + f * (1.0 - s)))
        dfilt_ref[8 : 8 + TOKENS, :] = dfilt
        dx = table_ref[TAPS - 1 : TAPS, cols] * dfilt
        back = table_ref[0:1, cols] * dfilt_ref[8:16, :]
        for k in range(TAPS):
            at = EDGE - TAPS + 1 + k
            small_ref[j, k : k + 1, :] = jnp.sum(dfilt * ext_ref[at : at + TOKENS, :], axis=0, keepdims=True)
            if k < TAPS - 1:
                dx = dx + table_ref[k : k + 1, cols] * dfilt_ref[11 - k : 11 - k + TOKENS, :]
            if 0 < k < TAPS - 1:
                back = back + table_ref[k : k + 1, cols] * dfilt_ref[8 - k : 16 - k, :]
        small_ref[j, TAPS : TAPS + 1, :] = jnp.sum(dfilt, axis=0, keepdims=True)
        gin_ref[:, cols] = dx.astype(BF16)
        tail_ref[:, cols] = dx[TOKENS - EDGE :, :]
        ret_ref[:, cols] = back
        return carry

    lax.fori_loop(0, CHANNELS // 128, filters, 0)
    halo = to_peer(ret_ref, rrecv, hsems.at[0], hsems.at[1], (before, dp))
    halo.start()
    zsum = zsum_ref[...]
    decays = jnp.exp(turned(cums)[TOKENS - 1 :, :])
    final = jnp.sum(zsum, axis=0, keepdims=True) + decays * jnp.sum(ded_ref[...], axis=0, keepdims=True)
    row = iota((TOKENS, 128), 0)
    dcum = dcum_ref[...] - zsum + jnp.where(row == TOKENS - 1, final, 0.0)
    shift = 1
    while shift < TOKENS:
        dcum = dcum + jnp.where(row < TOKENS - shift, pltpu.roll(dcum, TOKENS - shift, 0), 0.0)
        shift *= 2
    gain_t = turned(jnp.broadcast_to(gain, (HEADS, TOKENS)))
    draw = (dstep_ref[...] + dcum * gain_t) * turned(sigmoid(raw))
    gstep_ref[...] = jnp.transpose(draw)[:HEADS, :]
    for p in range(PAIRS):
        small_ref[p, 5:6, :] = dnorm_ref[:, p * 128 : p * 128 + 128]
    tiles = CHANNELS // 128
    small_ref[tiles, 0:1, :] = jnp.sum(draw, axis=0, keepdims=True)
    small_ref[tiles, 1:2, :] = jnp.sum(dcum * turned(rates), axis=0, keepdims=True)
    small_ref[tiles, 2:3, :] = jnp.sum(dskip_ref[...], axis=0, keepdims=True)
    narrow = Scatter(seq, dp, small_ref, srecv, sems, 0)
    narrow.start()

    spread.received()
    wacc[...] = jnp.zeros_like(wacc)

    def add(k, carry):
        wacc[...] += wrecv[k].astype(F32)
        return carry

    lax.fori_loop(0, SEQ, add, 0)
    wown[...] = wacc[...].astype(BF16)
    wide_all = Scatter(seq, dp, wown, wall, sems, 6, whole=True)
    wide_all.start()

    narrow.received()
    sdp[dp] = lax.fori_loop(0, SEQ, lambda k, total: total + srecv[k], jnp.zeros((8, 128), F32))

    def exchange(k, slot):
        return to_peer(sdp.at[dp], sdp.at[slot], dsems.at[0, k], dsems.at[1, slot], (seq, lax.rem(dp + k, DP)))

    for k in range(1, DP):
        exchange(k, dp).start()
    for k in range(1, DP):
        exchange(k, lax.rem(dp + k, DP)).wait_recv()
    sown[...] = sdp[0] + sdp[1] + sdp[2] + sdp[3]
    narrow_all = Scatter(seq, dp, sown, sall, sems, 4, whole=True)
    narrow_all.start()
    halo.wait_recv()
    fix = jnp.where(seq < SEQ - 1, rrecv[...], 0.0)
    zeros = jnp.zeros((EDGE - TAPS + 1, CHANNELS), F32)
    fix = jnp.concatenate([zeros, fix[: TAPS - 1, :]], axis=0)
    gin_ref[TOKENS - EDGE :, :] = (tail_ref[...] + fix).astype(BF16)
    narrow_all.received()
    for j in range(tiles):
        gfilt_ref[:, j * 128 : j * 128 + 128] = sall[j, 0 : TAPS + 1, :]
    for p in range(PAIRS):
        gnorm_ref[:, p * 128 : p * 128 + 128] = sall[p, 5:6, :]
    ghead_ref[...] = sall[tiles]
    wide_all.received()
    for j in range(WIDTH // 128):
        for c in range(ROWS // 16):
            chunk, at = divmod(j * ROWS + c * 16, PIECE)
            gweight_ref[c * 16 : c * 16 + 16, j * 128 : j * 128 + 128] = wall[chunk, at : at + 16, :].astype(F32)
    halo.wait_send()
    for k in range(1, DP):
        exchange(k, dp).wait_send()
    for scatter in (spread, narrow, wide_all, narrow_all):
        scatter.sent()


VMEM = pl.BlockSpec(memory_space=pltpu.VMEM)


def call(kernel, outs, scratch, args, collective, name):
    return pl.pallas_call(
        kernel,
        out_shape=[jax.ShapeDtypeStruct(shape, kind) for shape, kind in outs],
        in_specs=[VMEM] * len(args),
        out_specs=[VMEM] * len(outs),
        scratch_shapes=scratch,
        compiler_params=pltpu.CompilerParams(
            vmem_limit_bytes=62 * 2**20, collective_id=collective, has_side_effects=True
        ),
        name=name,
    )(*args)


def vmem(*shape, kind=F32):
    return pltpu.VMEM(shape, kind)


def padded(row):
    return jnp.pad(row, (0, CHANNELS - row.shape[0]))[None]


def body(
    conv_input, gate_input, step_input, filter_taps, filter_bias, step_bias, decay_log, skip_gain, norm_weight,
    output_weight, output_grad,
):
    raw_rows, gate_rows, step_rows, cotangent = conv_input[0], gate_input[0], step_input[0], output_grad[0]
    skips = jnp.broadcast_to(skip_gain[:, None], (HEADS, HEAD_DIM)).reshape(INNER)
    rows = [filter_taps, filter_bias[None], *map(padded, (norm_weight, skips, step_bias, decay_log))]
    table = jnp.concatenate([*rows, jnp.zeros((7, CHANNELS), F32)], axis=0)
    dma = pltpu.SemaphoreType.DMA
    wide, small, square = (TOKENS, INNER), (TOKENS, STATE), (TOKENS, TOKENS)
    chunks, states = (SEQ, 8, CHUNK), (SEQ, 8, HALF)
    scan = [vmem(*chunks), vmem(*chunks), vmem(*states), vmem(SEQ, 1, HALF)]
    columns = [vmem(HEADS, TOKENS, 128), vmem(HEADS, 1, TOKENS)]
    act, inside, normed_grad, entering, halo = call(
        forward_kernel,
        [((TOKENS, CHANNELS), F32), (wide, F32), (wide, F32), (states, F32), ((EDGE, CHANNELS), F32)],
        [vmem(EDGE, CHANNELS, kind=BF16), vmem(TOKENS + EDGE, 128), *scan, vmem(DP - 1, ROWS, WIDTH, kind=BF16),
         *columns, vmem(*wide), vmem(*square), dma((4, SEQ)), dma((6, 4)), dma((2,))],
        (raw_rows, table, step_rows, cotangent, output_weight),
        0, "forward",
    )
    gate_grad, dy, dx, dq, dk, dcum, dnorm, dskip, ending, partial = call(
        backward_kernel,
        [(wide, BF16), (wide, F32), (wide, F32), (small, F32), (small, F32), (small, F32), ((1, INNER), F32),
         ((8, 128), F32), (states, F32), ((SEQ * PIECE, 128), BF16)],
        [*scan, vmem(DP, TOKENS, ROWS, kind=BF16), vmem(DP - 1, TOKENS, ROWS, kind=BF16),
         vmem(DP - 1, TOKENS, WIDTH, kind=BF16), *columns, vmem(*wide), vmem(*wide), vmem(*square), vmem(*wide),
         vmem(*small), vmem(*square), dma((4, SEQ)), dma((4, DP - 1))],
        (act, gate_rows, table, step_rows, entering, inside, normed_grad, cotangent),
        1, "backward",
    )
    gin, gstep, gfilt, gnorm, ghead, gweight = call(
        last_kernel,
        [((TOKENS, CHANNELS), BF16), ((HEADS, TOKENS), F32), ((TAPS + 1, CHANNELS), F32), ((1, INNER), F32),
         ((8, 128), F32), ((ROWS, WIDTH), F32)],
        [vmem(TOKENS + EDGE, 128), vmem(TOKENS + 16, 128), vmem(*wide), vmem(*wide), vmem(TOKENS, CHANNELS),
         vmem(*small), vmem(*small), vmem(8, 128), vmem(*small), vmem(EDGE, CHANNELS), vmem(8, CHANNELS),
         vmem(8, CHANNELS), vmem(SEQ, 8, 128), vmem(SEQ, 8, 128), vmem(SEQ, 8, 128), vmem(8, 128), vmem(DP, 8, 128),
         vmem(SEQ, PIECE, 128, kind=BF16), vmem(SEQ, PIECE, 128, kind=BF16), vmem(PIECE, 128, kind=BF16),
         vmem(PIECE, 128), dma((8, SEQ)), dma((2, DP)), dma((2,))],
        (raw_rows, halo, table, act, step_rows, entering, ending, dy, dx, dq, dk, dcum, dnorm, dskip,
         partial.reshape(SEQ, PIECE, 128)),
        2, "last",
    )
    return gin[None], gate_grad[None], gstep[None], gweight, gfilt, gnorm[0], ghead[:3, :HEADS]


def solution(mesh):
    tokens, by_head, rows = P("dp", "seq", None), P("dp", None, "seq"), P("dp", None)
    return jax.shard_map(
        body,
        mesh=mesh,
        in_specs=(tokens, tokens, by_head, P(), P(), P(), P(), P(), P(), rows, tokens),
        out_specs=(tokens, tokens, by_head, rows, P(), P(), P()),
        check_vma=False,
    )
```

time: 971 us -> 241 us (0.25)
  waiting for transfers between devices: 570 us -> 0 us
  Pallas kernels: 0 us -> 225 us
  blocking collectives: 139 us -> 0 us
  matrix products: 86.4 us -> 0 us
  other arithmetic: 81.4 us -> 1.33 us
  local copies, waits for them, and re-layouts: 50.3 us -> 13.9 us
  starting transfers between devices: 19.1 us -> 0 us
  between operations: 17.5 us -> 0.69 us
    all_gather x8 -> x0, waiting for transfers between devices: 371 us -> none  [the longest x6 191 us: carried_in(): pieces = jax.tree.map(lambda part: lax.all_gather(part, axis), total)]
    pallas_call x0 -> x3, Pallas kernels: none -> 225 us  [call(): pl.pallas_call(kernel, out_shape=[jax.ShapeDtypeStruct(shape, kind) for s...]
    psum x1 -> x0, waiting for transfers between devices: 121 us -> none  [in_one(): total = lax.psum(jnp.concatenate([a.ravel() for a in arrays]), axis)]
    unnamed x2 -> x0, blocking collectives: 110 us -> none
    dot_general x14 -> x0, matrix products: 86.4 us -> none  [the longest x3 40.6 us: finish(): inside = jnp.einsum('hcts,cshp->cthp', weights, scaled, precision=HIGHEST)]
    reduce_scatter x1 -> x0, waiting for transfers between devices: 55.9 us -> none  [body(): lax.psum_scatter(lax.dot_general(normed_low, cotangent, (((0,), (0,)), ((...]
    all_gather x4 -> x0, blocking collectives: 28.5 us -> none  [carried_in(): pieces = jax.tree.map(lambda part: lax.all_gather(part, axis), total)]
    add x6 -> x0, other arithmetic: 27.9 us -> none  [affine(): later[0][:, None, None] * earlier[1] + later[1]]
  transfers between devices with their start and end apart: 19 -> 0, of which waited for: 11 -> 0; matrix products, arithmetic and copies ran while one was open for 16% -> 0% of each run, Pallas kernels for 0% -> 0%
where the time goes in v2:
time: 241 us; the launch traced here: 240 us
  Pallas kernels  225 us (93%)
  local copies, waits for them, and re-layouts  13.9 us (6%)
    pallas_call x3, Pallas kernels, call(): pl.pallas_call(kernel, out_shape=[jax.ShapeDtypeStruct(shape, kind) for s...  225 us
    unnamed x13, local copies, waits for them, and re-layouts  6.74 us

profile of v2, /device:TPU:0, one launch (start us, length us, event | category | flops | bytes accessed | tf_op | source)
XLA Modules:
  0.0 240.5 jit_solution(4628700293260327826)
XLA Ops:
  0.6 0.7 broadcast_in_dim.33
  1.3 0.7 pad.16
  2.0 0.7 pad.17
  2.7 0.7 pad.14
  3.4 0.7 broadcast_in_dim.35
  4.1 0.1 reshape.21
  4.3 2.2 concatenate.3.table_ref
  6.4 64.8 %forward.1 = (f32[256,2816]{1,0:T(8,128)}, f32[256,2560]{1,0:T(8,128)}, f32[256,2560]{1,0:T(8,128)}, f32[32,8,1280]{2,1,0:T(8,128)}, f32[16,2816]{1,0:T(8,128)}) custom-call(bf16[256,2816]{1,0:T(8,128)(2,1)} %bitcast.8, f32[16,2816]{1,0:T(8,128)} %concatenate.3.table_ref, f32[40,256]{1,0:T(8,128)} %bitcast.16, bf16[256,1280]{1,0:T(8,128)(2,1)} %bitcast.10, ...), custom_call_target="tpu_custom_call" | custom-call | tf_op jit(solution)/shard_map/forward/pallas_call | solution.py:592
  71.3 81.6 %backward.1 = (bf16[256,2560]{1,0:T(8,128)(2,1)}, f32[256,2560]{1,0:T(8,128)}, f32[256,2560]{1,0:T(8,128)}, f32[256,128]{1,0:T(8,128)}, f32[256,128]{1,0:T(8,128...) custom-call(f32[256,2816]{1,0:T(8,128)} %get-tuple-element.29.act_re, ...), custom_call_target="tpu_custom_call" | custom-call | tf_op jit(solution)/shard_map/backward/pallas_call | solution.py:592
  152.9 78.1 %last.1 = (bf16[256,2816]{1,0:T(8,128)(2,1)}, f32[40,256]{1,0:T(8,128)}, f32[5,2816]{1,0:T(8,128)}, f32[1,2560]{1,0:T(1,128)}, f32[8,128]{1,0:T(8,128)}, /*index=5*/f32[640,1280]{1,0:T(8,128)}) custom-call(bf16[256,2816]{1,0:T(8,128)(2,1)} %bitcast.9, f32[16,2816]{1,0:T(8,128)} %get-tuple-element.28.halo_ref, f32[16,2816]{1,0:T(8,128)} %concatenate.3.table_ref, ...), custom_call_target="tpu_custom_call" | custom-call | tf_op jit(solution)/shard_map/last/pallas_call | solution.py:592
  231.0 0.0 copy-start.1
  231.0 1.4 slice.3
  232.4 1.3 reduce
  233.7 0.0 copy-start
  233.7 2.7 %copy.23 = bf16[1,256,2816]{2,1,0:T(8,128)(2,1)} copy(bf16[1,256,2816]{2,1,0:T(8,128)(2,1)} %bitcast.13) | data formatting | bytes 2883584
  236.4 0.0 copy-done.1
  236.4 0.0 copy-start.3
  236.4 1.1 copy.24
  237.5 0.0 copy-done.3
  237.5 0.6 copy.25
  238.1 0.0 copy-done
  238.1 1.7 copy.26
  239.8 0.0 copy-done.2
  239.8 0.6 copy.27
  (7 shorter events, 0.1 us)
Async XLA Ops:
  231.0 5.4 %copy-start.1 = (bf16[256,2560]{1,0:T(8,128)(2,1)S(1)}, bf16[256,2560]{1,0:T(8,128)(2,1)}, u32[]{:S(2)}) copy-start(bf16[256,2560]{1,0:T(8,128)(2,1)} %get-tuple-element.43) | copy-start | bytes 3932164
  233.7 4.4 %copy-start = (f32[640,1280]{1,0:T(8,128)S(1)}, f32[640,1280]{1,0:T(8,128)}, u32[]{:S(2)}) copy-start(f32[640,1280]{1,0:T(8,128)} %get-tuple-element.59) | copy-start | bytes 9830404
  236.4 1.1 copy-start.3
  238.1 1.7 copy-start.2

commit v3 on v2

v3 whole, which is shorter than its diff:
```python
import jax
import jax.numpy as jnp
from jax import lax
from jax.experimental import pallas as pl
from jax.experimental.pallas import tpu as pltpu
from jax.sharding import PartitionSpec as P

HEADS = 40
HEAD_DIM = 64
STATE = 128
INNER = 2560
CHANNELS = 2816
WIDTH = 1280
TOKENS = 256
TAPS = 4
PAIRS = 20
HALF = 1280
SEQ = 32
DP = 4
ROWS = INNER // DP
EDGE = 16
PIECE = 208
MASKED = -1e30
EPSILON = 1e-05

F32 = jnp.float32
BF16 = jnp.bfloat16
MESH = pl.DeviceIdType.MESH
NN = ((1,), (0,))
NT = ((1,), (1,))
TN = ((0,), (0,))


def mm(a, b, dims):
    return lax.dot_general(a, b, (dims, ((), ())), preferred_element_type=F32)


def split(x):
    high = x.astype(BF16)
    return high, (x - high.astype(F32)).astype(BF16)


def dot3(a, b, dims):
    return mm(a[0], b[0], dims) + mm(a[0], b[1], dims) + mm(a[1], b[0], dims)


def iota(shape, dim):
    return lax.broadcasted_iota(jnp.int32, shape, dim)


def lanes(p):
    return pl.ds(pl.multiple_of(p * 128, 128), 128)


def turned(x):
    return jnp.transpose(jnp.concatenate([x, jnp.zeros((128 - HEADS, TOKENS), F32)], axis=0))


def rates_of(step_ref, table_ref):
    columns = jnp.transpose(jnp.concatenate([table_ref[7:9, :128], jnp.zeros((126, 128), F32)], axis=0))
    raw = step_ref[...] + columns[:HEADS, 0:1]
    sizes = jnp.maximum(raw, 0.0) + jnp.log1p(jnp.exp(-jnp.abs(raw)))
    gain = -jnp.exp(columns[:HEADS, 1:2])
    rates = sizes * gain
    lane = iota(rates.shape, 1)
    cums = rates
    shift = 1
    while shift < TOKENS:
        cums = cums + jnp.where(lane >= shift, pltpu.roll(cums, shift, 1), 0.0)
        shift *= 2
    return raw, sizes, gain, rates, cums


def widen(columns, p):
    first = iota((TOKENS, 128), 1) < HEAD_DIM
    return jnp.where(first, columns[:, 2 * p : 2 * p + 1], columns[:, 2 * p + 1 : 2 * p + 2])


def head_sum(v, p):
    into = (iota((128, 128), 1) == 2 * p + iota((128, 128), 0) // HEAD_DIM).astype(BF16)
    high, low = split(v)
    return mm(high, into, NN) + mm(low, into, NN)


def sigmoid(x):
    return 1.0 / (1.0 + jnp.exp(-x))


def filtered_of(x_ref, table_ref, ext_ref, edge, cols):
    ext_ref[0:EDGE, :] = edge
    ext_ref[EDGE : EDGE + TOKENS, :] = x_ref[:, cols].astype(F32)
    total = table_ref[TAPS : TAPS + 1, cols]
    for k in range(TAPS):
        at = EDGE - TAPS + 1 + k
        total = total + table_ref[k : k + 1, cols] * ext_ref[at : at + TOKENS, :]
    return total


def write_state(pay_ref, p, state):
    half = p // (PAIRS // 2)
    at = lanes(p - half * (PAIRS // 2))
    for c in range(SEQ // 2):
        pay_ref[half * (SEQ // 2) + c, :, at] = state[c * 8 : c * 8 + 8, :]


def read_state(ref, p):
    half = p // (PAIRS // 2)
    at = lanes(p - half * (PAIRS // 2))
    return jnp.concatenate([ref[half * (SEQ // 2) + c, :, at] for c in range(SEQ // 2)], axis=0)


def to_peer(src, dst, send, recv, device):
    return pltpu.make_async_remote_copy(
        src_ref=src, dst_ref=dst, send_sem=send, recv_sem=recv, device_id=device, device_id_type=MESH
    )


def greet(seq, dp, others):
    barrier = pltpu.get_barrier_semaphore()

    def hello(i, carry):
        peer = lax.rem(seq + i, SEQ)
        pl.semaphore_signal(barrier, inc=1, device_id=(peer, dp), device_id_type=MESH)
        return carry

    lax.fori_loop(1, SEQ, hello, 0)
    for other in others:
        pl.semaphore_signal(barrier, inc=1, device_id=other, device_id_type=MESH)
    pl.semaphore_wait(barrier, SEQ - 1 + len(others))


def each_peer(seq, act):
    def step(i, carry):
        act(i, lax.rem(seq + i, SEQ))
        return carry

    lax.fori_loop(1, SEQ, step, 0)


class Scatter:
    def __init__(self, seq, dp, src, dst, sems, row, whole=False):
        self.seq, self.dp, self.src, self.dst, self.sems, self.row, self.whole = seq, dp, src, dst, sems, row, whole

    def copy(self, i, peer, slot):
        src = self.src if self.whole else self.src.at[peer]
        sems = self.sems
        return to_peer(src, self.dst.at[slot], sems.at[self.row, i], sems.at[self.row + 1, slot], (peer, self.dp))

    def start(self):
        each_peer(self.seq, lambda i, peer: self.copy(i, peer, self.seq).start())
        self.dst[self.seq] = self.src[...] if self.whole else self.src[self.seq]

    def received(self):
        each_peer(self.seq, lambda i, peer: self.copy(i, peer, peer).wait_recv())

    def sent(self):
        each_peer(self.seq, lambda i, peer: self.copy(i, peer, self.seq).wait_send())


def coefficients(seq, drecv, coef):
    decays = jnp.concatenate([drecv[k, 0:1, :] for k in range(SEQ)], axis=0)
    head = (seq // (SEQ // 2)) * (HEADS // 2) + iota((128, HALF), 1) // HEAD_DIM
    into = (iota((128, HALF), 0) == head).astype(F32)
    wide = lax.dot_general(
        decays, into, (NN, ((), ())), preferred_element_type=F32, precision=lax.Precision.HIGHEST
    )
    for k in range(SEQ):
        coef[k] = wide[k : k + 1, :]


def scan_chunks(reverse, recv, outgoing, coef):
    def scan(j, state):
        k = SEQ - 1 - j if reverse else j
        outgoing[k] = state.astype(outgoing.dtype)
        return coef[k] * state + recv[k].astype(F32)

    lax.fori_loop(0, SEQ, scan, jnp.zeros((8, HALF), F32))


def place():
    seq, dp = lax.axis_index("seq"), lax.axis_index("dp")
    partner = dp + 1 - 2 * lax.rem(dp, 2)
    across = lax.rem(dp + 2, DP)
    return seq, dp, partner, across


def kernel(
    x_ref, gate_ref, table_ref, step_ref, cot_ref, w_ref,
    gin_ref, ggate_ref, gstep_ref, gfilt_ref, gnorm_ref, ghead_ref, gweight_ref,
    edge_ref, halo_ref, ext_ref, dfilt_ref, act_ref, scan_ref, ng_ref, stepx_ref, expx_ref, col_ref, cum_ref,
    scores_ref, turn_ref, dsc_ref, acc_ref, dq_ref, dk_ref, dcum_ref, dskip_ref, dstep_ref, zsum_ref, ded_ref,
    drecv, down_ref, coef, pay_ref, recv, outgoing, ent_ref, pay2_ref, recv2, outgoing2, end_ref,
    wblocks, low_ref, lrecv, crecv, part_ref, wrecv, wall, wown, wacc,
    tail_ref, ret_ref, rrecv, small_ref, srecv, sall, sown, sdp, sems, wsems, dsems, hsems, xsems,
):
    seq, dp, partner, across = place()
    corner = DP - 1 - dp
    beside = seq + 4 - 8 * lax.rem(seq // 4, 2)
    after, before = lax.rem(seq + 1, SEQ), lax.rem(seq + SEQ - 1, SEQ)
    greet(seq, dp, [(seq, partner), (seq, across), (seq, corner), (beside, across)])
    last_rows = x_ref.at[pl.ds(TOKENS - EDGE, EDGE)]
    halo = to_peer(last_rows, edge_ref, hsems.at[0], hsems.at[1], (after, dp))
    halo.start()
    quarter = ROWS // 4

    def piece(q):
        return pl.ds(q * quarter, quarter)

    cross = [
        to_peer(w_ref.at[piece(q)], wblocks.at[1, piece(q)], wsems.at[0, q], wsems.at[1, q], (beside, across))
        for q in range(4)
    ]
    relay = [
        to_peer(wblocks.at[1, piece(q)], wblocks.at[2, piece(q)], wsems.at[2, q], wsems.at[3, q], (seq, partner))
        for q in range(4)
    ]
    near = to_peer(w_ref, wblocks.at[0], wsems.at[4, 0], wsems.at[5, 0], (seq, partner))
    for copy in cross:
        copy.start()
    near.start()
    raw, sizes, gain, rates, cums = rates_of(step_ref, table_ref)
    cum_t = turned(cums)
    size_t = turned(sizes)
    decays = jnp.exp(cum_t[TOKENS - 1 :, :])
    down_ref[...] = jnp.broadcast_to(decays, (8, 128))
    decay_all = Scatter(seq, dp, down_ref, drecv, sems, 0, whole=True)
    decay_all.start()
    to_end = turned(jnp.exp(cums[:, TOKENS - 1 :] - cums))
    end_t = to_end * size_t
    halo.wait_recv()
    halo_ref[...] = jnp.where(seq > 0, edge_ref[...].astype(F32), 0.0)

    def activate(j, carry):
        cols = lanes(j)
        f = filtered_of(x_ref, table_ref, ext_ref, halo_ref[:, cols], cols)
        act_ref[:, cols] = f * sigmoid(f)
        return carry

    lax.fori_loop(0, CHANNELS // 128, activate, 0)
    key = act_ref[:, INNER : INNER + STATE]
    key_turned = split(jnp.transpose(key))
    for p in range(PAIRS):
        a = act_ref[:, p * 128 : p * 128 + 128] * widen(end_t, p)
        write_state(pay_ref, p, dot3(key_turned, split(a), NN))
    out = Scatter(seq, dp, pay_ref, recv, sems, 2)
    out.start()

    exp_t = jnp.exp(cum_t)
    for h in range(HEADS):
        cum_ref[h] = cums[h : h + 1, :]
        col_ref[h] = jnp.broadcast_to(cum_t[:, h : h + 1], (TOKENS, 128))
    for p in range(PAIRS):
        stepx_ref[:, p * 128 : p * 128 + 128] = widen(size_t, p)
        expx_ref[:, p * 128 : p * 128 + 128] = widen(exp_t, p)
    query = act_ref[:, INNER + STATE :]
    key_s, query_s = split(key), split(query)
    query_turned = split(jnp.transpose(query))
    scores_ref[...] = dot3(query_s, key_s, NT)
    first = iota((TOKENS, 128), 1) < HEAD_DIM
    rows, columns = iota((TOKENS, TOKENS), 0), iota((TOKENS, TOKENS), 1)

    def inside(p, carry):
        cols = lanes(p)
        high, low = split(act_ref[:, cols] * stepx_ref[:, cols])
        both = jnp.concatenate([high, low], axis=1)
        parts = []
        for i in range(2):
            h = 2 * p + i
            c = col_ref[h]
            e = jnp.exp(jnp.where(rows >= columns, jnp.concatenate([c, c], axis=1) - cum_ref[h], MASKED))
            wh, wl = split(scores_ref[...] * e)
            r = mm(wh, both, NN)
            parts.append(r[:, :128] + r[:, 128:] + mm(wl, high, NN))
        scan_ref[:, cols] = jnp.where(first, parts[0], parts[1])
        return carry

    def normed_grad(block, weights):
        at = pl.multiple_of(block * ROWS, 128)
        ng_ref[:, pl.ds(at, ROWS)] = mm(cot_ref[...], weights[...], NT)

    lax.fori_loop(0, PAIRS, inside, 0)
    normed_grad(dp, w_ref)
    decay_all.received()
    coefficients(seq, drecv, coef)
    out.received()
    scan_chunks(False, recv, outgoing, coef)
    back = Scatter(seq, dp, outgoing, ent_ref, sems, 4)
    back.start()
    near.wait_recv()
    normed_grad(partner, wblocks.at[0])
    for q in range(4):
        cross[q].wait_recv()
        relay[q].start()
    cot_near = to_peer(cot_ref, crecv.at[0], dsems.at[0, 0], dsems.at[1, 0], (seq, partner))
    cot_cross = to_peer(cot_ref, crecv.at[1], dsems.at[0, 1], dsems.at[1, 1], (seq, across))
    cot_relay = to_peer(crecv.at[1], crecv.at[2], dsems.at[0, 2], dsems.at[1, 2], (seq, partner))
    cot_near.start()
    cot_cross.start()
    normed_grad(across, wblocks.at[1])
    turn_ref[...] = dot3(key_s, query_s, NT)
    for copy in relay:
        copy.wait_recv()
    normed_grad(corner, wblocks.at[2])
    for ref in (acc_ref, dsc_ref, dq_ref, dcum_ref, dskip_ref, dstep_ref, zsum_ref, ded_ref, small_ref):
        ref[...] = jnp.zeros_like(ref)
    back.received()

    def forward(p, carry):
        cols = lanes(p)
        carried = dot3(query_s, split(read_state(ent_ref, p)), NN) * expx_ref[:, cols]
        scanned = scan_ref[:, cols] + carried + table_ref[6:7, cols] * act_ref[:, cols]
        scan_ref[:, cols] = scanned
        gate = gate_ref[:, cols].astype(F32)
        gated = scanned * (gate * sigmoid(gate))
        acc_ref[...] += gated * gated
        return carry

    lax.fori_loop(0, PAIRS, forward, 0)
    inverse = lax.rsqrt(jnp.sum(acc_ref[...], axis=1, keepdims=True) / INNER + EPSILON)
    acc_ref[...] = jnp.zeros_like(acc_ref)

    def norm(p, carry):
        cols = lanes(p)
        gate = gate_ref[:, cols].astype(F32)
        gated = scan_ref[:, cols] * (gate * sigmoid(gate))
        weight = table_ref[5:6, cols]
        unit = gated * inverse
        block = p // 5
        low_ref[block, :, lanes(p - block * 5)] = (unit * weight).astype(BF16)
        ng = ng_ref[:, cols]
        small_ref[p, 5:6, :] = jnp.sum(ng * unit, axis=0, keepdims=True)
        acc_ref[...] += ng * weight * gated
        return carry

    lax.fori_loop(0, PAIRS, norm, 0)
    lows = [
        to_peer(low_ref.at[other], lrecv.at[k], dsems.at[2, k], dsems.at[3, k], (seq, other))
        for k, other in enumerate((partner, across, corner))
    ]
    for copy in lows:
        copy.start()
    lean = jnp.sum(acc_ref[...], axis=1, keepdims=True) * (inverse * inverse * inverse) / INNER

    def cotangents(p, carry):
        cols = lanes(p)
        gate = gate_ref[:, cols].astype(F32)
        sloped = sigmoid(gate)
        silu = gate * sloped
        scanned = scan_ref[:, cols]
        dgated = inverse * (ng_ref[:, cols] * table_ref[5:6, cols]) - scanned * silu * lean
        ggate_ref[:, cols] = (dgated * scanned * (sloped * (1.0 + gate * (1.0 - sloped)))).astype(BF16)
        dy = dgated * silu
        ng_ref[:, cols] = dy
        write_state(pay2_ref, p, dot3(query_turned, split(dy * expx_ref[:, cols]), NN))
        return carry

    lax.fori_loop(0, PAIRS, cotangents, 0)
    out2 = Scatter(seq, dp, pay2_ref, recv2, sems, 6)
    out2.start()

    def backward(p, carry):
        cols = lanes(p)
        dy = ng_ref[:, cols]
        dh, dl = split(dy)
        both = jnp.concatenate([dh, dl], axis=1)
        twice = jnp.concatenate([dh, dh], axis=1)
        values = act_ref[:, cols]
        scaled = values * stepx_ref[:, cols]
        parts = []
        for i in range(2):
            h = 2 * p + i
            c = col_ref[h]
            e = jnp.exp(jnp.where(columns >= rows, cum_ref[h] - jnp.concatenate([c, c], axis=1), MASKED))
            wh, wl = split(turn_ref[...] * e)
            r = mm(wh, both, NN)
            parts.append(r[:, :128] + r[:, 128:] + mm(wl, dh, NN))
            own = first if i == 0 else jnp.logical_not(first)
            xh, xl = split(jnp.where(own, scaled, 0.0))
            dw = mm(jnp.concatenate([xh, xl], axis=1), twice, NT) + mm(xh, dl, NT)
            dsc_ref[...] += dw * e
        dx = jnp.where(first, parts[0], parts[1])
        dq_ref[...] += dot3(split(dy * expx_ref[:, cols]), split(read_state(ent_ref, p)), NT)
        skipped = dy * values
        dcum_ref[...] += head_sum(dy * scan_ref[:, cols] - skipped * table_ref[6:7, cols] - scaled * dx, p)
        dskip_ref[...] += head_sum(jnp.sum(skipped.reshape(TOKENS // 8, 8, 128), axis=0), p)
        scan_ref[:, cols] = dx
        return carry

    lax.fori_loop(0, PAIRS, backward, 0)
    for p in range(PAIRS):
        expx_ref[:, p * 128 : p * 128 + 128] = widen(to_end, p)
    cot_cross.wait_recv()
    cot_relay.start()
    out2.received()
    scan_chunks(True, recv2, outgoing2, coef)
    back2 = Scatter(seq, dp, outgoing2, end_ref, sems, 8)
    back2.start()
    dsc = dsc_ref[...]
    dk_ref[...] = dot3(split(dsc), query_s, NN)
    dq_ref[...] += dot3(split(jnp.transpose(dsc)), key_s, NN)
    cot_near.wait_recv()
    for copy in lows:
        copy.wait_recv()
    cot_relay.wait_recv()
    left = [jnp.transpose(block) for block in (low_ref[dp], lrecv[0], lrecv[1], lrecv[2])]
    right = [cot_ref, crecv.at[0], crecv.at[1], crecv.at[2]]
    for j in range(WIDTH // 256):
        total = mm(left[0], right[0][:, j * 256 : j * 256 + 256], NN)
        for k in range(1, DP):
            total = total + mm(left[k], right[k][:, j * 256 : j * 256 + 256], NN)
        for i in range(2):
            for c in range(ROWS // 16):
                chunk, at = divmod((2 * j + i) * ROWS + c * 16, PIECE)
                part_ref[chunk, at : at + 16, :] = total[c * 16 : c * 16 + 16, i * 128 : i * 128 + 128].astype(BF16)
    for c in range(10 * ROWS, SEQ * PIECE, 16):
        chunk, at = divmod(c, PIECE)
        part_ref[chunk, at : at + 16, :] = jnp.zeros((16, 128), BF16)
    spread = Scatter(seq, dp, part_ref, wrecv, sems, 10)
    spread.start()
    back2.received()

    def pair(p, carry):
        cols = lanes(p)
        values = act_ref[:, cols]
        step = stepx_ref[:, cols]
        ending = expx_ref[:, cols]
        end = read_state(end_ref, p)
        end_s = split(end)
        z = dot3(key_s, end_s, NN) * ending
        dx = scan_ref[:, cols] + z
        act_ref[:, cols] = dx * step + table_ref[6:7, cols] * ng_ref[:, cols]
        dstep_ref[...] += head_sum(dx * values, p)
        scaled = values * step
        zsum_ref[...] += head_sum(scaled * z, p)
        dk_ref[...] += dot3(split(scaled * ending), end_s, NT)
        both = end * read_state(ent_ref, p)
        ded_ref[...] += head_sum(jnp.sum(both.reshape(STATE // 8, 8, 128), axis=0), p)
        return carry

    lax.fori_loop(0, PAIRS, pair, 0)
    act_ref[:, INNER : INNER + STATE] = dk_ref[...]
    act_ref[:, INNER + STATE :] = dq_ref[...]
    dfilt_ref[0:8, :] = jnp.zeros((8, 128), F32)
    dfilt_ref[8 + TOKENS :, :] = jnp.zeros((8, 128), F32)

    def filters(j, carry):
        cols = lanes(j)
        f = filtered_of(x_ref, table_ref, ext_ref, halo_ref[:, cols], cols)
        s = sigmoid(f)
        dfilt = act_ref[:, cols] * (s * (1.0 + f * (1.0 - s)))
        dfilt_ref[8 : 8 + TOKENS, :] = dfilt
        dx = table_ref[TAPS - 1 : TAPS, cols] * dfilt
        lead = table_ref[0:1, cols] * dfilt_ref[8:16, :]
        for k in range(TAPS):
            at = EDGE - TAPS + 1 + k
            small_ref[j, k : k + 1, :] = jnp.sum(dfilt * ext_ref[at : at + TOKENS, :], axis=0, keepdims=True)
            if k < TAPS - 1:
                dx = dx + table_ref[k : k + 1, cols] * dfilt_ref[11 - k : 11 - k + TOKENS, :]
            if 0 < k < TAPS - 1:
                lead = lead + table_ref[k : k + 1, cols] * dfilt_ref[8 - k : 16 - k, :]
        small_ref[j, TAPS : TAPS + 1, :] = jnp.sum(dfilt, axis=0, keepdims=True)
        gin_ref[:, cols] = dx.astype(BF16)
        tail_ref[:, cols] = dx[TOKENS - EDGE :, :]
        ret_ref[:, cols] = lead
        return carry

    lax.fori_loop(0, CHANNELS // 128, filters, 0)
    returned = to_peer(ret_ref, rrecv, hsems.at[2], hsems.at[3], (before, dp))
    returned.start()
    zsum = zsum_ref[...]
    final = jnp.sum(zsum, axis=0, keepdims=True) + decays * jnp.sum(ded_ref[...], axis=0, keepdims=True)
    row = iota((TOKENS, 128), 0)
    dcum = dcum_ref[...] - zsum + jnp.where(row == TOKENS - 1, final, 0.0)
    shift = 1
    while shift < TOKENS:
        dcum = dcum + jnp.where(row < TOKENS - shift, pltpu.roll(dcum, TOKENS - shift, 0), 0.0)
        shift *= 2
    gain_t = turned(jnp.broadcast_to(gain, (HEADS, TOKENS)))
    draw = (dstep_ref[...] + dcum * gain_t) * turned(sigmoid(raw))
    gstep_ref[...] = jnp.transpose(draw)[:HEADS, :]
    tiles = CHANNELS // 128
    small_ref[tiles, 0:1, :] = jnp.sum(draw, axis=0, keepdims=True)
    small_ref[tiles, 1:2, :] = jnp.sum(dcum * turned(rates), axis=0, keepdims=True)
    small_ref[tiles, 2:3, :] = jnp.sum(dskip_ref[...], axis=0, keepdims=True)
    narrow = Scatter(seq, dp, small_ref, srecv, sems, 14)
    narrow.start()

    spread.received()
    wacc[...] = jnp.zeros_like(wacc)

    def add(k, carry):
        wacc[...] += wrecv[k].astype(F32)
        return carry

    lax.fori_loop(0, SEQ, add, 0)
    wown[...] = wacc[...].astype(BF16)
    wide_all = Scatter(seq, dp, wown, wall, sems, 12, whole=True)
    wide_all.start()

    narrow.received()
    sdp[dp] = lax.fori_loop(0, SEQ, lambda k, total: total + srecv[k], jnp.zeros((8, 128), F32))

    def exchange(k, slot):
        return to_peer(sdp.at[dp], sdp.at[slot], xsems.at[0, k], xsems.at[1, slot], (seq, lax.rem(dp + k, DP)))

    for k in range(1, DP):
        exchange(k, dp).start()
    for k in range(1, DP):
        exchange(k, lax.rem(dp + k, DP)).wait_recv()
    sown[...] = sdp[0] + sdp[1] + sdp[2] + sdp[3]
    narrow_all = Scatter(seq, dp, sown, sall, sems, 16, whole=True)
    narrow_all.start()
    returned.wait_recv()
    fix = jnp.where(seq < SEQ - 1, rrecv[...], 0.0)
    zeros = jnp.zeros((EDGE - TAPS + 1, CHANNELS), F32)
    fix = jnp.concatenate([zeros, fix[: TAPS - 1, :]], axis=0)
    gin_ref[TOKENS - EDGE :, :] = (tail_ref[...] + fix).astype(BF16)
    narrow_all.received()
    for j in range(tiles):
        gfilt_ref[:, j * 128 : j * 128 + 128] = sall[j, 0 : TAPS + 1, :]
    for p in range(PAIRS):
        gnorm_ref[:, p * 128 : p * 128 + 128] = sall[p, 5:6, :]
    ghead_ref[...] = sall[tiles]
    wide_all.received()
    for j in range(WIDTH // 128):
        for c in range(ROWS // 16):
            chunk, at = divmod(j * ROWS + c * 16, PIECE)
            gweight_ref[c * 16 : c * 16 + 16, j * 128 : j * 128 + 128] = wall[chunk, at : at + 16, :]
    for copy in [halo, near, *cross, *relay, cot_near, cot_cross, cot_relay, *lows, returned]:
        copy.wait_send()
    for k in range(1, DP):
        exchange(k, dp).wait_send()
    for scatter in (decay_all, out, back, out2, back2, spread, narrow, wide_all, narrow_all):
        scatter.sent()


VMEM = pl.BlockSpec(memory_space=pltpu.VMEM)


def vmem(*shape, kind=F32):
    return pltpu.VMEM(shape, kind)


def padded(row):
    return jnp.pad(row, (0, CHANNELS - row.shape[0]))[None]


SENT = F32


def body(
    conv_input, gate_input, step_input, filter_taps, filter_bias, step_bias, decay_log, skip_gain, norm_weight,
    output_weight, output_grad,
):
    skips = jnp.broadcast_to(skip_gain[:, None], (HEADS, HEAD_DIM)).reshape(INNER)
    rows = [filter_taps, filter_bias[None], *map(padded, (norm_weight, skips, step_bias, decay_log))]
    table = jnp.concatenate([*rows, jnp.zeros((7, CHANNELS), F32)], axis=0)
    args = (conv_input[0], gate_input[0], table, step_input[0], output_grad[0], output_weight)
    dma = pltpu.SemaphoreType.DMA
    wide, small, square = (TOKENS, INNER), (TOKENS, STATE), (TOKENS, TOKENS)
    states, pieces, tiles = (SEQ, 8, HALF), (SEQ, PIECE, 128), (SEQ, 8, 128)
    scan = [vmem(*states, kind=SENT)] * 4
    outs = [
        ((TOKENS, CHANNELS), BF16), (wide, BF16), ((HEADS, TOKENS), F32), ((TAPS + 1, CHANNELS), F32),
        ((1, INNER), F32), ((8, 128), F32), ((ROWS, WIDTH), BF16),
    ]
    gin, ggate, gstep, gfilt, gnorm, ghead, gweight = pl.pallas_call(
        kernel,
        out_shape=[jax.ShapeDtypeStruct(shape, kind) for shape, kind in outs],
        in_specs=[VMEM] * len(args),
        out_specs=[VMEM] * len(outs),
        scratch_shapes=[
            vmem(EDGE, CHANNELS, kind=BF16), vmem(EDGE, CHANNELS), vmem(TOKENS + EDGE, 128), vmem(TOKENS + 16, 128),
            vmem(TOKENS, CHANNELS), vmem(*wide), vmem(*wide), vmem(*wide), vmem(*wide),
            vmem(HEADS, TOKENS, 128), vmem(HEADS, 1, TOKENS), vmem(*square), vmem(*square), vmem(*square),
            *[vmem(*small)] * 4, vmem(8, 128), *[vmem(*small)] * 2, vmem(8, 128),
            vmem(*tiles), vmem(8, 128), vmem(SEQ, 1, HALF), *scan, *scan,
            vmem(DP - 1, ROWS, WIDTH, kind=BF16), vmem(DP, TOKENS, ROWS, kind=BF16),
            vmem(DP - 1, TOKENS, ROWS, kind=BF16), vmem(DP - 1, TOKENS, WIDTH, kind=BF16),
            *[vmem(*pieces, kind=BF16)] * 3, vmem(PIECE, 128, kind=BF16), vmem(PIECE, 128),
            vmem(EDGE, CHANNELS), *[vmem(8, CHANNELS)] * 2, *[vmem(*tiles)] * 3, vmem(8, 128), vmem(DP, 8, 128),
            dma((18, SEQ)), dma((6, 4)), dma((4, DP - 1)), dma((4,)), dma((2, DP)),
        ],
        compiler_params=pltpu.CompilerParams(
            vmem_limit_bytes=63 * 2**20, collective_id=0, has_side_effects=True
        ),
        name="layer_backward",
    )(*args)
    return gin[None], ggate[None], gstep[None], gweight.astype(F32), gfilt, gnorm[0], ghead[:3, :HEADS]


def solution(mesh):
    tokens, by_head, rows = P("dp", "seq", None), P("dp", None, "seq"), P("dp", None)
    return jax.shard_map(
        body,
        mesh=mesh,
        in_specs=(tokens, tokens, by_head, P(), P(), P(), P(), P(), P(), rows, tokens),
        out_specs=(tokens, tokens, by_head, rows, P(), P(), P()),
        check_vma=False,
    )
```

time: 241 us -> 202 us (0.84)
  Pallas kernels: 225 us -> 185 us
  other arithmetic: 1.33 us -> 4.82 us
  local copies, waits for them, and re-layouts: 13.9 us -> 11.2 us
    pallas_call x3 -> x1, Pallas kernels: 225 us -> 185 us  [body(): pl.pallas_call(kernel, out_shape=[jax.ShapeDtypeStruct(shape, kind) for s...]
    convert_element_type x0 -> x1, other arithmetic: none -> 3.49 us  [body(): gweight.astype(F32)]
    unnamed x13 -> x12, local copies, waits for them, and re-layouts: 6.74 us -> 4.16 us
where the time goes in v3:
time: 202 us
  Pallas kernels  185 us (92%)
  local copies, waits for them, and re-layouts  11.2 us (6%)
  other arithmetic  4.82 us (2%)
    pallas_call x1, Pallas kernels, body(): pl.pallas_call(kernel, out_shape=[jax.ShapeDtypeStruct(shape, kind) for s...  185 us
    unnamed x12, local copies, waits for them, and re-layouts  4.16 us

profile of v3, /device:TPU:0, one launch (start us, length us, event | category | flops | bytes accessed | tf_op | source)
XLA Modules:
  0.0 201.8 jit_solution(4832929921222096360)
XLA Ops:
  0.6 0.7 broadcast_in_dim.33
  1.3 0.7 pad.16
  2.0 0.7 pad.17
  2.7 0.7 pad.14
  3.4 0.7 broadcast_in_dim.35
  4.1 0.1 reshape.18
  4.3 2.2 %concatenate.3.table_ref = f32[16,2816]{1,0:T(8,128)} concatenate(f32[4,2816]{1,0:T(4,128)} %param.14, f32[1,2816]{1,0:T(1,128)S(1)} %broadcast_in_dim.33, f32[1,2816]{1,0:T(1,128)S(1)} %broadcast_in_dim.34, f32[1,2816]{1,0:T(1,128)S(1)} %broadcast_in_dim.36, f32[1,2816]{1,0:T(1,128)S(1)} %broadcast_in_dim.37, f32[1,2816]{1,0:T(1,128)S(1)} %broadcast_in_dim.38, ...), dimensions={0} | concatenate | bytes 360448 | tf_op jit(solution)/shard_map/concatenate | solution.py:557
  6.4 185.2 %layer_backward.1 = (bf16[256,2816]{1,0:T(8,128)(2,1)}, bf16[256,2560]{1,0:T(8,128)(2,1)}, f32[40,256]{1,0:T(8,128)}, f32[5,2816]{1,0:T(8,128)}, f32[1,2560]{1,0...) custom-call(bf16[256,2816]{1,0:T(8,128)(2,1)} %bitcast.7, bf16[256,2560]{1,0:T(8,128)(2,1)} %bitcast.9, ...), custom_call_target="tpu_custom_call" | custom-call | tf_op jit(solution)/shard_map/layer_backward/pallas_call | solution.py:567
  191.6 1.3 slice.3
  192.9 1.3 reduce
  194.2 0.0 copy-start
  194.2 3.5 %convert_element_type.9 = f32[640,1280]{1,0:T(8,128)} convert(bf16[640,1280]{1,0:T(8,128)(2,1)} %get-tuple-element.17) | non-fusion elementwise | flops 819200 | bytes 4915200 | tf_op jit(solution)/shard_map/convert_element_type | solution.py:589
  197.7 0.0 copy-done
  197.7 0.0 copy-start.1
  197.7 1.1 copy.22
  198.8 0.7 copy-done.1
  199.5 0.0 copy-start.3
  199.5 0.0 copy-start.2
  199.5 1.1 copy.23
  200.6 0.0 copy-done.3
  200.6 0.6 copy.24
  201.2 0.0 copy-done.2
  201.2 0.6 copy.25
  (6 shorter events, 0.1 us)
Async XLA Ops:
  194.2 3.5 %copy-start = (bf16[256,2816]{1,0:T(8,128)(2,1)S(1)}, bf16[256,2816]{1,0:T(8,128)(2,1)}, u32[]{:S(2)}) copy-start(bf16[256,2816]{1,0:T(8,128)(2,1)} %get-tuple-element.14) | copy-start | bytes 4325380
  197.7 1.8 copy-start.1
  199.5 1.1 copy-start.3
  199.5 1.7 copy-start.2

commit v4 on v3

--- a/solution.py
+++ b/solution.py
@@ -14,7 +14,11 @@
 TOKENS = 256
 TAPS = 4
 PAIRS = 20
-HALF = 1280
+GROUPS = 4
+EACH = PAIRS // GROUPS
+SPREAD = INNER // GROUPS
+BAND = 16
+BANDS = STATE // BAND
 SEQ = 32
 DP = 4
 ROWS = INNER // DP
@@ -56,8 +60,8 @@
     return jnp.transpose(jnp.concatenate([x, jnp.zeros((128 - HEADS, TOKENS), F32)], axis=0))
 
 
-def rates_of(step_ref, table_ref):
-    columns = jnp.transpose(jnp.concatenate([table_ref[7:9, :128], jnp.zeros((126, 128), F32)], axis=0))
+def rates_of(step_ref, heads_ref):
+    columns = jnp.transpose(jnp.pad(heads_ref[...], ((0, 125), (0, 128 - HEADS))))
     raw = step_ref[...] + columns[:HEADS, 0:1]
     sizes = jnp.maximum(raw, 0.0) + jnp.log1p(jnp.exp(-jnp.abs(raw)))
     gain = -jnp.exp(columns[:HEADS, 1:2])
@@ -97,16 +101,16 @@
 
 
 def write_state(pay_ref, p, state):
-    half = p // (PAIRS // 2)
-    at = lanes(p - half * (PAIRS // 2))
-    for c in range(SEQ // 2):
-        pay_ref[half * (SEQ // 2) + c, :, at] = state[c * 8 : c * 8 + 8, :]
+    group = p // EACH
+    at = lanes(p - group * EACH)
+    for c in range(BANDS):
+        pay_ref[group * BANDS + c, :, at] = state[c * BAND : c * BAND + BAND, :]
 
 
 def read_state(ref, p):
-    half = p // (PAIRS // 2)
-    at = lanes(p - half * (PAIRS // 2))
-    return jnp.concatenate([ref[half * (SEQ // 2) + c, :, at] for c in range(SEQ // 2)], axis=0)
+    group = p // EACH
+    at = lanes(p - group * EACH)
+    return jnp.concatenate([ref[group * BANDS + c, :, at] for c in range(BANDS)], axis=0)
 
 
 def to_peer(src, dst, send, recv, device):
@@ -126,7 +130,7 @@
     lax.fori_loop(1, SEQ, hello, 0)
     for other in others:
         pl.semaphore_signal(barrier, inc=1, device_id=other, device_id_type=MESH)
-    pl.semaphore_wait(barrier, SEQ - 1 + len(others))
+    return lambda: pl.semaphore_wait(barrier, SEQ - 1 + len(others))
 
 
 def each_peer(seq, act):
@@ -138,17 +142,21 @@
 
 
 class Scatter:
-    def __init__(self, seq, dp, src, dst, sems, row, whole=False):
-        self.seq, self.dp, self.src, self.dst, self.sems, self.row, self.whole = seq, dp, src, dst, sems, row, whole
+    def __init__(self, seq, dp, src, dst, sems, row, whole=False, pick=lambda peer: peer):
+        self.seq, self.dp, self.src, self.dst, self.sems, self.row = seq, dp, src, dst, sems, row
+        self.whole, self.pick = whole, pick
 
     def copy(self, i, peer, slot):
-        src = self.src if self.whole else self.src.at[peer]
+        src = self.src if self.whole else self.src.at[self.pick(peer)]
         sems = self.sems
         return to_peer(src, self.dst.at[slot], sems.at[self.row, i], sems.at[self.row + 1, slot], (peer, self.dp))
 
+    def keep(self):
+        self.dst[self.seq] = self.src[...] if self.whole else self.src[self.pick(self.seq)]
+
     def start(self):
         each_peer(self.seq, lambda i, peer: self.copy(i, peer, self.seq).start())
-        self.dst[self.seq] = self.src[...] if self.whole else self.src[self.seq]
+        self.keep()
 
     def received(self):
         each_peer(self.seq, lambda i, peer: self.copy(i, peer, peer).wait_recv())
@@ -156,11 +164,29 @@
     def sent(self):
         each_peer(self.seq, lambda i, peer: self.copy(i, peer, self.seq).wait_send())
 
+    def in_group(self, group, act):
+        def step(c, carry):
+            peer = group * BANDS + c
+
+            @pl.when(peer != self.seq)
+            def _():
+                act(lax.rem(peer - self.seq + SEQ, SEQ), peer)
+
+            return carry
+
+        lax.fori_loop(0, BANDS, step, 0)
+
+    def start_group(self, group):
+        self.in_group(group, lambda i, peer: self.copy(i, peer, self.seq).start())
+
+    def received_group(self, group):
+        self.in_group(group, lambda i, peer: self.copy(i, peer, peer).wait_recv())
+
 
 def coefficients(seq, drecv, coef):
     decays = jnp.concatenate([drecv[k, 0:1, :] for k in range(SEQ)], axis=0)
-    head = (seq // (SEQ // 2)) * (HEADS // 2) + iota((128, HALF), 1) // HEAD_DIM
-    into = (iota((128, HALF), 0) == head).astype(F32)
+    head = (seq // BANDS) * (HEADS // GROUPS) + iota((128, SPREAD), 1) // HEAD_DIM
+    into = (iota((128, SPREAD), 0) == head).astype(F32)
     wide = lax.dot_general(
         decays, into, (NN, ((), ())), preferred_element_type=F32, precision=lax.Precision.HIGHEST
     )
@@ -174,7 +200,7 @@
         outgoing[k] = state.astype(outgoing.dtype)
         return coef[k] * state + recv[k].astype(F32)
 
-    lax.fori_loop(0, SEQ, scan, jnp.zeros((8, HALF), F32))
+    lax.fori_loop(0, SEQ, scan, jnp.zeros((BAND, SPREAD), F32))
 
 
 def place():
@@ -185,9 +211,9 @@
 
 
 def kernel(
-    x_ref, gate_ref, table_ref, step_ref, cot_ref, w_ref,
+    x_ref, gate_ref, taps_ref, fbias_ref, weight_ref, heads_ref, step_ref, cot_ref, w_ref,
     gin_ref, ggate_ref, gstep_ref, gfilt_ref, gnorm_ref, ghead_ref, gweight_ref,
-    edge_ref, halo_ref, ext_ref, dfilt_ref, act_ref, scan_ref, ng_ref, stepx_ref, expx_ref, col_ref, cum_ref,
+    table_ref, edge_ref, halo_ref, ext_ref, dfilt_ref, act_ref, scan_ref, ng_ref, stepx_ref, expx_ref, col_ref, cum_ref,
     scores_ref, turn_ref, dsc_ref, acc_ref, dq_ref, dk_ref, dcum_ref, dskip_ref, dstep_ref, zsum_ref, ded_ref,
     drecv, down_ref, coef, pay_ref, recv, outgoing, ent_ref, pay2_ref, recv2, outgoing2, end_ref,
     wblocks, low_ref, lrecv, crecv, part_ref, wrecv, wall, wown, wacc,
@@ -197,7 +223,22 @@
     corner = DP - 1 - dp
     beside = seq + 4 - 8 * lax.rem(seq // 4, 2)
     after, before = lax.rem(seq + 1, SEQ), lax.rem(seq + SEQ - 1, SEQ)
-    greet(seq, dp, [(seq, partner), (seq, across), (seq, corner), (beside, across)])
+    met = greet(seq, dp, [(seq, partner), (seq, across), (seq, corner), (beside, across), (beside, corner)])
+    table_ref[0:TAPS, :] = taps_ref[...]
+    for j in range(CHANNELS // 128):
+        table_ref[TAPS : TAPS + 1, j * 128 : j * 128 + 128] = fbias_ref[j * 128 : j * 128 + 128].reshape(1, 128)
+    low_half = iota((1, 128), 1) < HEAD_DIM
+    for p in range(PAIRS):
+        at = slice(p * 128, p * 128 + 128)
+        table_ref[5:6, at] = weight_ref[at].reshape(1, 128)
+        skips = heads_ref[2:3, 2 * p : 2 * p + 2]
+        table_ref[6:7, at] = jnp.where(low_half, skips[:, 0:1], skips[:, 1:2])
+    raw, sizes, gain, rates, cums = rates_of(step_ref, heads_ref)
+    cum_t = turned(cums)
+    size_t = turned(sizes)
+    decays = jnp.exp(cum_t[TOKENS - 1 :, :])
+    down_ref[...] = jnp.broadcast_to(decays, (8, 128))
+    met()
     last_rows = x_ref.at[pl.ds(TOKENS - EDGE, EDGE)]
     halo = to_peer(last_rows, edge_ref, hsems.at[0], hsems.at[1], (after, dp))
     halo.start()
@@ -218,11 +259,6 @@
     for copy in cross:
         copy.start()
     near.start()
-    raw, sizes, gain, rates, cums = rates_of(step_ref, table_ref)
-    cum_t = turned(cums)
-    size_t = turned(sizes)
-    decays = jnp.exp(cum_t[TOKENS - 1 :, :])
-    down_ref[...] = jnp.broadcast_to(decays, (8, 128))
     decay_all = Scatter(seq, dp, down_ref, drecv, sems, 0, whole=True)
     decay_all.start()
     to_end = turned(jnp.exp(cums[:, TOKENS - 1 :] - cums))
@@ -236,14 +272,16 @@
         act_ref[:, cols] = f * sigmoid(f)
         return carry
 
-    lax.fori_loop(0, CHANNELS // 128, activate, 0)
+    lax.fori_loop(0, CHANNELS // 128, activate, 0, unroll=2)
     key = act_ref[:, INNER : INNER + STATE]
     key_turned = split(jnp.transpose(key))
+    out = Scatter(seq, dp, pay_ref, recv, sems, 2)
     for p in range(PAIRS):
         a = act_ref[:, p * 128 : p * 128 + 128] * widen(end_t, p)
         write_state(pay_ref, p, dot3(key_turned, split(a), NN))
-    out = Scatter(seq, dp, pay_ref, recv, sems, 2)
-    out.start()
+        if p % EACH == EACH - 1:
+            out.start_group(p // EACH)
+    out.keep()
 
     exp_t = jnp.exp(cum_t)
     for h in range(HEADS):
@@ -292,7 +330,7 @@
         cross[q].wait_recv()
         relay[q].start()
     cot_near = to_peer(cot_ref, crecv.at[0], dsems.at[0, 0], dsems.at[1, 0], (seq, partner))
-    cot_cross = to_peer(cot_ref, crecv.at[1], dsems.at[0, 1], dsems.at[1, 1], (seq, across))
+    cot_cross = to_peer(cot_ref, crecv.at[1], dsems.at[0, 1], dsems.at[1, 1], (beside, across))
     cot_relay = to_peer(crecv.at[1], crecv.at[2], dsems.at[0, 2], dsems.at[1, 2], (seq, partner))
     cot_near.start()
     cot_cross.start()
@@ -303,7 +341,8 @@
     normed_grad(corner, wblocks.at[2])
     for ref in (acc_ref, dsc_ref, dq_ref, dcum_ref, dskip_ref, dstep_ref, zsum_ref, ded_ref, small_ref):
         ref[...] = jnp.zeros_like(ref)
-    back.received()
+    decay_all.sent()
+    out.sent()
 
     def forward(p, carry):
         cols = lanes(p)
@@ -315,7 +354,10 @@
         acc_ref[...] += gated * gated
         return carry
 
-    lax.fori_loop(0, PAIRS, forward, 0)
+    for turn in (0, 1, 3, 2):
+        group = lax.rem(seq // BANDS + turn, GROUPS)
+        back.received_group(group)
+        lax.fori_loop(0, EACH, lambda i, carry: forward(group * EACH + i, carry), 0, unroll=EACH)
     inverse = lax.rsqrt(jnp.sum(acc_ref[...], axis=1, keepdims=True) / INNER + EPSILON)
     acc_ref[...] = jnp.zeros_like(acc_ref)
 
@@ -332,10 +374,10 @@
         acc_ref[...] += ng * weight * gated
         return carry
 
-    lax.fori_loop(0, PAIRS, norm, 0)
+    lax.fori_loop(0, PAIRS, norm, 0, unroll=2)
     lows = [
-        to_peer(low_ref.at[other], lrecv.at[k], dsems.at[2, k], dsems.at[3, k], (seq, other))
-        for k, other in enumerate((partner, across, corner))
+        to_peer(low_ref.at[other], lrecv.at[k], dsems.at[2, k], dsems.at[3, k], (at, other))
+        for k, (at, other) in enumerate(((seq, partner), (beside, across), (beside, corner)))
     ]
     for copy in lows:
         copy.start()
@@ -354,9 +396,12 @@
         write_state(pay2_ref, p, dot3(query_turned, split(dy * expx_ref[:, cols]), NN))
         return carry
 
-    lax.fori_loop(0, PAIRS, cotangents, 0)
     out2 = Scatter(seq, dp, pay2_ref, recv2, sems, 6)
-    out2.start()
+    for turn in (2, 1, 3, 0):
+        group = lax.rem(seq // BANDS + turn, GROUPS)
+        lax.fori_loop(0, EACH, lambda i, carry: cotangents(group * EACH + i, carry), 0, unroll=EACH)
+        out2.start_group(group)
+    out2.keep()
 
     def backward(p, carry):
         cols = lanes(p)
@@ -391,6 +436,7 @@
         expx_ref[:, p * 128 : p * 128 + 128] = widen(to_end, p)
     cot_cross.wait_recv()
     cot_relay.start()
+    back.sent()
     out2.received()
     scan_chunks(True, recv2, outgoing2, coef)
     back2 = Scatter(seq, dp, outgoing2, end_ref, sems, 8)
@@ -416,8 +462,9 @@
         chunk, at = divmod(c, PIECE)
         part_ref[chunk, at : at + 16, :] = jnp.zeros((16, 128), BF16)
     spread = Scatter(seq, dp, part_ref, wrecv, sems, 10)
+    out2.sent()
+    back2.received()
     spread.start()
-    back2.received()
 
     def pair(p, carry):
         cols = lanes(p)
@@ -437,7 +484,7 @@
         ded_ref[...] += head_sum(jnp.sum(both.reshape(STATE // 8, 8, 128), axis=0), p)
         return carry
 
-    lax.fori_loop(0, PAIRS, pair, 0)
+    lax.fori_loop(0, PAIRS, pair, 0, unroll=2)
     act_ref[:, INNER : INNER + STATE] = dk_ref[...]
     act_ref[:, INNER + STATE :] = dq_ref[...]
     dfilt_ref[0:8, :] = jnp.zeros((8, 128), F32)
@@ -464,7 +511,7 @@
         ret_ref[:, cols] = lead
         return carry
 
-    lax.fori_loop(0, CHANNELS // 128, filters, 0)
+    lax.fori_loop(0, CHANNELS // 128, filters, 0, unroll=2)
     returned = to_peer(ret_ref, rrecv, hsems.at[2], hsems.at[3], (before, dp))
     returned.start()
     zsum = zsum_ref[...]
@@ -482,7 +529,10 @@
     small_ref[tiles, 0:1, :] = jnp.sum(draw, axis=0, keepdims=True)
     small_ref[tiles, 1:2, :] = jnp.sum(dcum * turned(rates), axis=0, keepdims=True)
     small_ref[tiles, 2:3, :] = jnp.sum(dskip_ref[...], axis=0, keepdims=True)
-    narrow = Scatter(seq, dp, small_ref, srecv, sems, 14)
+    def pick(peer):
+        return peer + (4 - 8 * lax.rem(peer // 4, 2)) * (dp // 2)
+
+    narrow = Scatter(seq, dp, small_ref, srecv, sems, 14, pick=pick)
     narrow.start()
 
     spread.received()
@@ -497,16 +547,20 @@
     wide_all = Scatter(seq, dp, wown, wall, sems, 12, whole=True)
     wide_all.start()
 
+    back2.sent()
+    spread.sent()
     narrow.received()
     sdp[dp] = lax.fori_loop(0, SEQ, lambda k, total: total + srecv[k], jnp.zeros((8, 128), F32))
 
+    others = ((seq, partner), (beside, across), (beside, corner))
+
     def exchange(k, slot):
-        return to_peer(sdp.at[dp], sdp.at[slot], xsems.at[0, k], xsems.at[1, slot], (seq, lax.rem(dp + k, DP)))
-
-    for k in range(1, DP):
+        return to_peer(sdp.at[dp], sdp.at[slot], xsems.at[0, k], xsems.at[1, slot], others[k])
+
+    for k in range(DP - 1):
         exchange(k, dp).start()
-    for k in range(1, DP):
-        exchange(k, lax.rem(dp + k, DP)).wait_recv()
+    for k in range(DP - 1):
+        exchange(k, others[k][1]).wait_recv()
     sown[...] = sdp[0] + sdp[1] + sdp[2] + sdp[3]
     narrow_all = Scatter(seq, dp, sown, sall, sems, 16, whole=True)
     narrow_all.start()
@@ -517,20 +571,20 @@
     gin_ref[TOKENS - EDGE :, :] = (tail_ref[...] + fix).astype(BF16)
     narrow_all.received()
     for j in range(tiles):
-        gfilt_ref[:, j * 128 : j * 128 + 128] = sall[j, 0 : TAPS + 1, :]
+        gfilt_ref[:, j * 128 : j * 128 + 128] = sall[pick(j), 0 : TAPS + 1, :]
     for p in range(PAIRS):
-        gnorm_ref[:, p * 128 : p * 128 + 128] = sall[p, 5:6, :]
-    ghead_ref[...] = sall[tiles]
+        gnorm_ref[p * 128 : p * 128 + 128] = sall[pick(p), 5, :]
+    ghead_ref[...] = sall[pick(tiles), 0:3, 0:HEADS]
     wide_all.received()
     for j in range(WIDTH // 128):
         for c in range(ROWS // 16):
             chunk, at = divmod(j * ROWS + c * 16, PIECE)
-            gweight_ref[c * 16 : c * 16 + 16, j * 128 : j * 128 + 128] = wall[chunk, at : at + 16, :]
+            gweight_ref[c * 16 : c * 16 + 16, j * 128 : j * 128 + 128] = wall[chunk, at : at + 16, :].astype(F32)
     for copy in [halo, near, *cross, *relay, cot_near, cot_cross, cot_relay, *lows, returned]:
         copy.wait_send()
-    for k in range(1, DP):
+    for k in range(DP - 1):
         exchange(k, dp).wait_send()
-    for scatter in (decay_all, out, back, out2, back2, spread, narrow, wide_all, narrow_all):
+    for scatter in (narrow, wide_all, narrow_all):
         scatter.sent()
 
 
@@ -539,10 +593,6 @@
 
 def vmem(*shape, kind=F32):
     return pltpu.VMEM(shape, kind)
-
-
-def padded(row):
-    return jnp.pad(row, (0, CHANNELS - row.shape[0]))[None]
 
 
 SENT = F32
@@ -552,17 +602,15 @@
     conv_input, gate_input, step_input, filter_taps, filter_bias, step_bias, decay_log, skip_gain, norm_weight,
     output_weight, output_grad,
 ):
-    skips = jnp.broadcast_to(skip_gain[:, None], (HEADS, HEAD_DIM)).reshape(INNER)
-    rows = [filter_taps, filter_bias[None], *map(padded, (norm_weight, skips, step_bias, decay_log))]
-    table = jnp.concatenate([*rows, jnp.zeros((7, CHANNELS), F32)], axis=0)
-    args = (conv_input[0], gate_input[0], table, step_input[0], output_grad[0], output_weight)
+    heads = jnp.stack([step_bias, decay_log, skip_gain])
+    args = (conv_input[0], gate_input[0], filter_taps, filter_bias, norm_weight, heads, step_input[0], output_grad[0], output_weight)
     dma = pltpu.SemaphoreType.DMA
     wide, small, square = (TOKENS, INNER), (TOKENS, STATE), (TOKENS, TOKENS)
-    states, pieces, tiles = (SEQ, 8, HALF), (SEQ, PIECE, 128), (SEQ, 8, 128)
+    states, pieces, tiles = (SEQ, BAND, SPREAD), (SEQ, PIECE, 128), (SEQ, 8, 128)
     scan = [vmem(*states, kind=SENT)] * 4
     outs = [
         ((TOKENS, CHANNELS), BF16), (wide, BF16), ((HEADS, TOKENS), F32), ((TAPS + 1, CHANNELS), F32),
-        ((1, INNER), F32), ((8, 128), F32), ((ROWS, WIDTH), BF16),
+        ((INNER,), F32), ((3, HEADS), F32), ((ROWS, WIDTH), F32),
     ]
     gin, ggate, gstep, gfilt, gnorm, ghead, gweight = pl.pallas_call(
         kernel,
@@ -570,11 +618,11 @@
         in_specs=[VMEM] * len(args),
         out_specs=[VMEM] * len(outs),
         scratch_shapes=[
-            vmem(EDGE, CHANNELS, kind=BF16), vmem(EDGE, CHANNELS), vmem(TOKENS + EDGE, 128), vmem(TOKENS + 16, 128),
+            vmem(8, CHANNELS), vmem(EDGE, CHANNELS, kind=BF16), vmem(EDGE, CHANNELS), vmem(TOKENS + EDGE, 128), vmem(TOKENS + 16, 128),
             vmem(TOKENS, CHANNELS), vmem(*wide), vmem(*wide), vmem(*wide), vmem(*wide),
             vmem(HEADS, TOKENS, 128), vmem(HEADS, 1, TOKENS), vmem(*square), vmem(*square), vmem(*square),
             *[vmem(*small)] * 4, vmem(8, 128), *[vmem(*small)] * 2, vmem(8, 128),
-            vmem(*tiles), vmem(8, 128), vmem(SEQ, 1, HALF), *scan, *scan,
+            vmem(*tiles), vmem(8, 128), vmem(SEQ, 1, SPREAD), *scan, *scan,
             vmem(DP - 1, ROWS, WIDTH, kind=BF16), vmem(DP, TOKENS, ROWS, kind=BF16),
             vmem(DP - 1, TOKENS, ROWS, kind=BF16), vmem(DP - 1, TOKENS, WIDTH, kind=BF16),
             *[vmem(*pieces, kind=BF16)] * 3, vmem(PIECE, 128, kind=BF16), vmem(PIECE, 128),
@@ -586,7 +634,7 @@
         ),
         name="layer_backward",
     )(*args)
-    return gin[None], ggate[None], gstep[None], gweight.astype(F32), gfilt, gnorm[0], ghead[:3, :HEADS]
+    return gin[None], ggate[None], gstep[None], gweight, gfilt, gnorm, ghead
 
 
 def solution(mesh):

time: 202 us -> 180 us (0.89)
  the two profiles are of different devices: /device:TPU:0 before, /device:TPU:4 now
where the time goes in v4:
time: 180 us
  Pallas kernels  168 us (93%)
  local copies, waits for them, and re-layouts  9.33 us (5%)
    pallas_call x1, Pallas kernels, body(): pl.pallas_call(kernel, out_shape=[jax.ShapeDtypeStruct(shape, kind) for s...  168 us
    unnamed x17, local copies, waits for them, and re-layouts  9.33 us

profile of v4, /device:TPU:4, one launch (start us, length us, event | category | flops | bytes accessed | tf_op | source)
XLA Modules:
  0.0 179.6 jit_solution(16140286892289260987)
XLA Ops:
  0.6 1.3 pad_maximum_fusion.heads_ref
  1.9 168.3 %layer_backward.1 = (bf16[256,2816]{1,0:T(8,128)(2,1)}, bf16[256,2560]{1,0:T(8,128)(2,1)}, f32[40,256]{1,0:T(8,128)}, f32[5,2816]{1,0:T(8,128)}, f32[2560]{0:T(1...) custom-call(bf16[256,2816]{1,0:T(8,128)(2,1)} %bitcast.11, bf16[256,2560]{1,0:T(8,128)(2,1)} %bitcast.13, f32[4,2816]{1,0:T(4,128)} %taps_ref.1, ...), custom_call_target="tpu_custom_call" | custom-call | tf_op jit(solution)/shard_map/layer_backward/pallas_call | solution.py:615
  170.2 0.0 copy-start
  170.2 2.7 %copy.25 = bf16[1,256,2816]{2,1,0:T(8,128)(2,1)} copy(bf16[1,256,2816]{2,1,0:T(8,128)(2,1)} %bitcast.10) | data formatting | bytes 2883584
  172.9 0.0 copy-start.2
  172.9 2.5 %copy.26 = bf16[1,256,2560]{2,1,0:T(8,128)(2,1)} copy(bf16[1,256,2560]{2,1,0:T(8,128)(2,1)} %bitcast.12) | data formatting | bytes 2621440
  175.4 0.0 copy-done.2
  175.4 0.6 copy.27
  176.0 0.0 copy-done
  176.0 0.0 copy-start.1
  176.0 0.0 copy-start.3
  176.0 0.0 copy-start.4
  176.0 1.7 copy.28
  177.7 0.0 copy-done.1
  177.7 0.6 copy.29
  178.4 0.0 copy-done.3
  178.4 0.6 copy.30
  179.0 0.0 copy-done.4
  179.0 0.6 copy.31
Async XLA Ops:
  170.2 5.8 %copy-start = (f32[640,1280]{1,0:T(8,128)S(1)}, f32[640,1280]{1,0:T(8,128)}, u32[]{:S(2)}) copy-start(f32[640,1280]{1,0:T(8,128)} %get-tuple-element.31) | copy-start | bytes 9830404
  172.9 2.5 %copy-start.2 = (f32[40,256]{1,0:T(8,128)S(1)}, f32[40,256]{1,0:T(8,128)}, u32[]{:S(2)}) copy-start(f32[40,256]{1,0:T(8,128)} %get-tuple-element.16) | copy-start | bytes 122884
  176.0 1.7 copy-start.1
  176.0 2.4 %copy-start.3 = (f32[2560]{0:T(1024)S(1)}, f32[2560]{0:T(1024)}, u32[]{:S(2)}) copy-start(f32[2560]{0:T(1024)} %get-tuple-element.33) | copy-start | bytes 30724
  176.0 3.0 %copy-start.4 = (f32[3,40]{1,0:T(4,128)S(1)}, f32[3,40]{1,0:T(4,128)}, u32[]{:S(2)}) copy-start(f32[3,40]{1,0:T(4,128)} %get-tuple-element.34) | copy-start | bytes 1444

commit v5 on v4

--- a/solution.py
+++ b/solution.py
@@ -23,6 +23,7 @@
 DP = 4
 ROWS = INNER // DP
 EDGE = 16
+FIRST = 112
 PIECE = 208
 MASKED = -1e30
 EPSILON = 1e-05
@@ -90,13 +91,13 @@
     return 1.0 / (1.0 + jnp.exp(-x))
 
 
-def filtered_of(x_ref, table_ref, ext_ref, edge, cols):
-    ext_ref[0:EDGE, :] = edge
-    ext_ref[EDGE : EDGE + TOKENS, :] = x_ref[:, cols].astype(F32)
+def filtered_of(x_ref, table_ref, ext_ref, edge, cols, count=TOKENS):
+    ext_ref[0:EDGE, :] = jnp.broadcast_to(edge, (EDGE, 128))
+    ext_ref[EDGE : EDGE + count, :] = x_ref[0:count, cols].astype(F32)
     total = table_ref[TAPS : TAPS + 1, cols]
     for k in range(TAPS):
         at = EDGE - TAPS + 1 + k
-        total = total + table_ref[k : k + 1, cols] * ext_ref[at : at + TOKENS, :]
+        total = total + table_ref[k : k + 1, cols] * ext_ref[at : at + count, :]
     return total
 
 
@@ -181,6 +182,42 @@
 
     def received_group(self, group):
         self.in_group(group, lambda i, peer: self.copy(i, peer, peer).wait_recv())
+
+
+class Tree:
+    def __init__(self, a, y, c, dp, device_of, buf, sems):
+        self.a, self.y, self.c, self.dp, self.device_of, self.buf, self.sems = a, y, c, dp, device_of, buf, sems
+
+    def copy(self, leg, k, arriving):
+        a, y, c = self.a, self.y, self.c
+        if leg == 0:
+            other, mine = lax.rem(a + k, 4), a
+            device, base, size = self.device_of(other, y, c), c * 8 + y * 4 + (other if arriving else mine), 1
+        elif leg == 1:
+            other, mine = 1 - y, y
+            device, base, size = self.device_of(a, other, c), c * 8 + (other if arriving else mine) * 4, 4
+        else:
+            other, mine = lax.rem(c + k, 4), c
+            device, base, size = self.device_of(a, y, other), (other if arriving else mine) * 8, 8
+        part = self.buf.at[pl.ds(base, size)]
+        recv = self.sems.at[2 * leg + 1, other if arriving else mine]
+        return to_peer(part, part, self.sems.at[2 * leg, k], recv, (device, self.dp))
+
+    def counts(self, leg):
+        return (1,) if leg == 1 else (1, 2, 3)
+
+    def start(self, leg):
+        for k in self.counts(leg):
+            self.copy(leg, k, False).start()
+
+    def received(self, leg):
+        for k in self.counts(leg):
+            self.copy(leg, k, True).wait_recv()
+
+    def sent(self):
+        for leg in range(3):
+            for k in self.counts(leg):
+                self.copy(leg, k, False).wait_send()
 
 
 def coefficients(seq, drecv, coef):
@@ -212,12 +249,12 @@
 
 def kernel(
     x_ref, gate_ref, taps_ref, fbias_ref, weight_ref, heads_ref, step_ref, cot_ref, w_ref,
-    gin_ref, ggate_ref, gstep_ref, gfilt_ref, gnorm_ref, ghead_ref, gweight_ref,
+    gin_ref, ggate_ref, gstep_ref, gfilt_ref, gnorm_ref, ghead_ref, wall, wall2,
     table_ref, edge_ref, halo_ref, ext_ref, dfilt_ref, act_ref, scan_ref, ng_ref, stepx_ref, expx_ref, col_ref, cum_ref,
     scores_ref, turn_ref, dsc_ref, acc_ref, dq_ref, dk_ref, dcum_ref, dskip_ref, dstep_ref, zsum_ref, ded_ref,
     drecv, down_ref, coef, pay_ref, recv, outgoing, ent_ref, pay2_ref, recv2, outgoing2, end_ref,
-    wblocks, low_ref, lrecv, crecv, part_ref, wrecv, wall, wown, wacc,
-    tail_ref, ret_ref, rrecv, small_ref, srecv, sall, sown, sdp, sems, wsems, dsems, hsems, xsems,
+    wblocks, low_ref, lrecv, crecv, part_ref, wrecv, wacc,
+    tail_ref, ret_ref, rrecv, small_ref, srecv, sall, sown, sdp, sems, wsems, dsems, hsems, xsems, tsems,
 ):
     seq, dp, partner, across = place()
     corner = DP - 1 - dp
@@ -263,16 +300,23 @@
     decay_all.start()
     to_end = turned(jnp.exp(cums[:, TOKENS - 1 :] - cums))
     end_t = to_end * size_t
+
+    def activate(j, carry):
+        cols = lanes(j)
+        f = filtered_of(x_ref, table_ref, ext_ref, 0.0, cols)
+        act_ref[:, cols] = f * sigmoid(f)
+        return carry
+
+    def mend(j, carry):
+        cols = lanes(j)
+        f = filtered_of(x_ref, table_ref, ext_ref, halo_ref[:, cols], cols, EDGE)
+        act_ref[0:EDGE, cols] = f * sigmoid(f)
+        return carry
+
+    lax.fori_loop(0, CHANNELS // 128, activate, 0, unroll=2)
     halo.wait_recv()
     halo_ref[...] = jnp.where(seq > 0, edge_ref[...].astype(F32), 0.0)
-
-    def activate(j, carry):
-        cols = lanes(j)
-        f = filtered_of(x_ref, table_ref, ext_ref, halo_ref[:, cols], cols)
-        act_ref[:, cols] = f * sigmoid(f)
-        return carry
-
-    lax.fori_loop(0, CHANNELS // 128, activate, 0, unroll=2)
+    lax.fori_loop(0, CHANNELS // 128, mend, 0, unroll=11)
     key = act_ref[:, INNER : INNER + STATE]
     key_turned = split(jnp.transpose(key))
     out = Scatter(seq, dp, pay_ref, recv, sems, 2)
@@ -543,9 +587,15 @@
         return carry
 
     lax.fori_loop(0, SEQ, add, 0)
-    wown[...] = wacc[...].astype(BF16)
-    wide_all = Scatter(seq, dp, wown, wall, sems, 12, whole=True)
-    wide_all.start()
+    x, y, z = seq // 8, lax.rem(seq // 4, 2), lax.rem(seq, 4)
+    trees = [
+        Tree(z, y, x, dp, lambda a, y, c: c * 8 + y * 4 + a, wall, tsems.at[0]),
+        Tree(x, y, z, dp, lambda a, y, c: a * 8 + y * 4 + c, wall2, tsems.at[1]),
+    ]
+    wall[seq] = wacc[0:FIRST, :].astype(BF16)
+    wall2[z * 8 + y * 4 + x] = wacc[FIRST:, :].astype(BF16)
+    for tree in trees:
+        tree.start(0)
 
     back2.sent()
     spread.sent()
@@ -559,11 +609,17 @@
 
     for k in range(DP - 1):
         exchange(k, dp).start()
+    for tree in trees:
+        tree.received(0)
+        tree.start(1)
     for k in range(DP - 1):
         exchange(k, others[k][1]).wait_recv()
     sown[...] = sdp[0] + sdp[1] + sdp[2] + sdp[3]
     narrow_all = Scatter(seq, dp, sown, sall, sems, 16, whole=True)
     narrow_all.start()
+    for tree in trees:
+        tree.received(1)
+        tree.start(2)
     returned.wait_recv()
     fix = jnp.where(seq < SEQ - 1, rrecv[...], 0.0)
     zeros = jnp.zeros((EDGE - TAPS + 1, CHANNELS), F32)
@@ -575,17 +631,34 @@
     for p in range(PAIRS):
         gnorm_ref[p * 128 : p * 128 + 128] = sall[pick(p), 5, :]
     ghead_ref[...] = sall[pick(tiles), 0:3, 0:HEADS]
-    wide_all.received()
-    for j in range(WIDTH // 128):
-        for c in range(ROWS // 16):
-            chunk, at = divmod(j * ROWS + c * 16, PIECE)
-            gweight_ref[c * 16 : c * 16 + 16, j * 128 : j * 128 + 128] = wall[chunk, at : at + 16, :].astype(F32)
+    for tree in trees:
+        tree.received(2)
+    for tree in trees:
+        tree.sent()
     for copy in [halo, near, *cross, *relay, cot_near, cot_cross, cot_relay, *lows, returned]:
         copy.wait_send()
     for k in range(DP - 1):
         exchange(k, dp).wait_send()
-    for scatter in (narrow, wide_all, narrow_all):
+    for scatter in (narrow, narrow_all):
         scatter.sent()
+
+
+def part_of(walls, chunk, at):
+    if at < FIRST:
+        return walls[0][chunk, at : at + 16, :]
+    x, y, z = chunk // 8, chunk // 4 % 2, chunk % 4
+    return walls[1][z * 8 + y * 4 + x, at - FIRST : at - FIRST + 16, :]
+
+
+def finish_kernel(*refs):
+    half = len(refs) - 7
+    for src, dst in zip(refs[:6], refs[half : half + 6]):
+        dst[...] = src[...]
+    walls, gweight_ref = refs[6:half], refs[-1]
+    for j in range(WIDTH // 128):
+        for c in range(ROWS // 16):
+            chunk, at = divmod(j * ROWS + c * 16, PIECE)
+            gweight_ref[c * 16 : c * 16 + 16, j * 128 : j * 128 + 128] = part_of(walls, chunk, at).astype(F32)
 
 
 VMEM = pl.BlockSpec(memory_space=pltpu.VMEM)
@@ -608,11 +681,12 @@
     wide, small, square = (TOKENS, INNER), (TOKENS, STATE), (TOKENS, TOKENS)
     states, pieces, tiles = (SEQ, BAND, SPREAD), (SEQ, PIECE, 128), (SEQ, 8, 128)
     scan = [vmem(*states, kind=SENT)] * 4
+    walls = [((SEQ, FIRST, 128), BF16), ((SEQ, PIECE - FIRST, 128), BF16)]
     outs = [
         ((TOKENS, CHANNELS), BF16), (wide, BF16), ((HEADS, TOKENS), F32), ((TAPS + 1, CHANNELS), F32),
-        ((INNER,), F32), ((3, HEADS), F32), ((ROWS, WIDTH), F32),
+        ((INNER,), F32), ((3, HEADS), F32), *walls,
     ]
-    gin, ggate, gstep, gfilt, gnorm, ghead, gweight = pl.pallas_call(
+    results = pl.pallas_call(
         kernel,
         out_shape=[jax.ShapeDtypeStruct(shape, kind) for shape, kind in outs],
         in_specs=[VMEM] * len(args),
@@ -625,15 +699,24 @@
             vmem(*tiles), vmem(8, 128), vmem(SEQ, 1, SPREAD), *scan, *scan,
             vmem(DP - 1, ROWS, WIDTH, kind=BF16), vmem(DP, TOKENS, ROWS, kind=BF16),
             vmem(DP - 1, TOKENS, ROWS, kind=BF16), vmem(DP - 1, TOKENS, WIDTH, kind=BF16),
-            *[vmem(*pieces, kind=BF16)] * 3, vmem(PIECE, 128, kind=BF16), vmem(PIECE, 128),
+            *[vmem(*pieces, kind=BF16)] * 2, vmem(PIECE, 128),
             vmem(EDGE, CHANNELS), *[vmem(8, CHANNELS)] * 2, *[vmem(*tiles)] * 3, vmem(8, 128), vmem(DP, 8, 128),
-            dma((18, SEQ)), dma((6, 4)), dma((4, DP - 1)), dma((4,)), dma((2, DP)),
+            dma((18, SEQ)), dma((6, 4)), dma((4, DP - 1)), dma((4,)), dma((2, DP)), dma((2, 6, 4)),
         ],
         compiler_params=pltpu.CompilerParams(
             vmem_limit_bytes=63 * 2**20, collective_id=0, has_side_effects=True
         ),
         name="layer_backward",
     )(*args)
+    finals = [*outs[:6], ((ROWS, WIDTH), F32)]
+    gin, ggate, gstep, gfilt, gnorm, ghead, gweight = pl.pallas_call(
+        finish_kernel,
+        out_shape=[jax.ShapeDtypeStruct(shape, kind) for shape, kind in finals],
+        in_specs=[VMEM] * len(outs),
+        out_specs=[VMEM] * len(finals),
+        compiler_params=pltpu.CompilerParams(vmem_limit_bytes=62 * 2**20),
+        name="finish",
+    )(*results)
     return gin[None], ggate[None], gstep[None], gweight, gfilt, gnorm, ghead
 
 

time: 180 us -> 164 us (0.911)
  the two profiles are of different devices: /device:TPU:4 before, /device:TPU:0 now
where the time goes in v5:
time: 164 us; the launch traced here: 163 us
  Pallas kernels  161 us (98%)
    pallas_call x1, Pallas kernels, body(): pl.pallas_call(kernel, out_shape=[jax.ShapeDtypeStruct(shape, kind) for s...  156 us
    pallas_call x1, Pallas kernels, body(): pl.pallas_call(finish_kernel, out_shape=[jax.ShapeDtypeStruct(shape, kind...  5.06 us

profile of v5, /device:TPU:0, one launch (start us, length us, event | category | flops | bytes accessed | tf_op | source)
XLA Modules:
  0.0 163.4 jit_solution(12358358977465967925)
XLA Ops:
  0.6 1.3 pad_maximum_fusion.heads_ref
  1.9 156.4 %layer_backward.1 = (bf16[256,2816]{1,0:T(8,128)(2,1)}, bf16[256,2560]{1,0:T(8,128)(2,1)}, f32[40,256]{1,0:T(8,128)}, f32[5,2816]{1,0:T(8,128)}, f32[2560]{0:T(1...) custom-call(bf16[256,2816]{1,0:T(8,128)(2,1)} %bitcast.10, ...), custom_call_target="tpu_custom_call" | custom-call | tf_op jit(solution)/shard_map/layer_backward/pallas_call | solution.py:689
  158.3 5.1 %finish.1 = (bf16[256,2816]{1,0:T(8,128)(2,1)}, bf16[256,2560]{1,0:T(8,128)(2,1)}, f32[40,256]{1,0:T(8,128)}, f32[5,2816]{1,0:T(8,128)}, f32[2560]{0:T(1024)}, /*index=5*/f32[3,40]{1,0:T(4,128)}, f32[640,1280]{1,0:T(8,128)}) custom-call(bf16[256,2816]{1,0:T(8,128)(2,1)} %get-tuple-element.22.refs_0_, bf16[256,2560]{1,0:T(8,128)(2,1)} %get-tuple-element.23.refs_1_, ...), custom_call_target="tpu_custom_call" | custom-call | tf_op jit(solution)/shard_map/finish/pallas_call | solution.py:712

commit v6 on v5

--- a/solution.py
+++ b/solution.py
@@ -220,6 +220,71 @@
                 self.copy(leg, k, False).wait_send()
 
 
+class Fold:
+    def __init__(self, a, y, c, dp, device_of, src, r0, s0, r1, s1, r2, sems):
+        self.a, self.y, self.c, self.dp, self.device_of = a, y, c, dp, device_of
+        self.src, self.r0, self.s0, self.r1, self.s1, self.r2, self.sems = src, r0, s0, r1, s1, r2, sems
+
+    def copy(self, leg, k, arriving):
+        a, y, c = self.a, self.y, self.c
+        if leg == 0:
+            other, mine = lax.rem(c + k, 4), c
+            device, src, dst = self.device_of(a, y, other), self.src.at[pl.ds(other * 8, 8)], self.r0
+            dst = dst.at[other if arriving else mine]
+        elif leg == 1:
+            other, mine = 1 - y, y
+            device, src, dst = self.device_of(a, other, c), self.s0.at[pl.ds(other * 4, 4)], self.r1
+        else:
+            other, mine = lax.rem(a + k, 4), a
+            device, src, dst = self.device_of(other, y, c), self.s1.at[other], self.r2
+            dst = dst.at[other if arriving else mine]
+        recv = self.sems.at[2 * leg + 1, other if arriving else mine]
+        return to_peer(src, dst, self.sems.at[2 * leg, k], recv, (device, self.dp))
+
+    def counts(self, leg):
+        return (1,) if leg == 1 else (1, 2, 3)
+
+    def start(self, leg):
+        for k in self.counts(leg):
+            self.copy(leg, k, False).start()
+
+    def received(self, leg):
+        for k in self.counts(leg):
+            self.copy(leg, k, True).wait_recv()
+
+    def first(self):
+        self.received(0)
+        c = self.c
+
+        def add(i, carry):
+            total = self.src[c * 8 + i].astype(F32)
+            for k in (1, 2, 3):
+                total = total + self.r0[lax.rem(c + k, 4), i].astype(F32)
+            self.s0[i] = total
+            return carry
+
+        lax.fori_loop(0, 8, add, 0)
+        self.start(1)
+
+    def second(self):
+        self.received(1)
+        for i in range(4):
+            self.s1[i] = self.s0[self.y * 4 + i] + self.r1[i]
+        self.start(2)
+
+    def third(self):
+        self.received(2)
+        total = self.s1[self.a]
+        for k in (1, 2, 3):
+            total = total + self.r2[lax.rem(self.a + k, 4)]
+        return total
+
+    def sent(self):
+        for leg in range(3):
+            for k in self.counts(leg):
+                self.copy(leg, k, False).wait_send()
+
+
 def coefficients(seq, drecv, coef):
     decays = jnp.concatenate([drecv[k, 0:1, :] for k in range(SEQ)], axis=0)
     head = (seq // BANDS) * (HEADS // GROUPS) + iota((128, SPREAD), 1) // HEAD_DIM
@@ -240,6 +305,23 @@
     lax.fori_loop(0, SEQ, scan, jnp.zeros((BAND, SPREAD), F32))
 
 
+def turned_slot(chunk):
+    return chunk % 4 * 8 + chunk // 4 % 2 * 4 + chunk // 8
+
+
+def place_part(parts, chunk, at, value):
+    if at < FIRST:
+        parts[0][chunk, at : at + 16, :] = value
+    else:
+        parts[1][turned_slot(chunk), at - FIRST : at - FIRST + 16, :] = value
+
+
+def part_of(parts, chunk, at):
+    if at < FIRST:
+        return parts[0][chunk, at : at + 16, :]
+    return parts[1][turned_slot(chunk), at - FIRST : at - FIRST + 16, :]
+
+
 def place():
     seq, dp = lax.axis_index("seq"), lax.axis_index("dp")
     partner = dp + 1 - 2 * lax.rem(dp, 2)
@@ -253,9 +335,11 @@
     table_ref, edge_ref, halo_ref, ext_ref, dfilt_ref, act_ref, scan_ref, ng_ref, stepx_ref, expx_ref, col_ref, cum_ref,
     scores_ref, turn_ref, dsc_ref, acc_ref, dq_ref, dk_ref, dcum_ref, dskip_ref, dstep_ref, zsum_ref, ded_ref,
     drecv, down_ref, coef, pay_ref, recv, outgoing, ent_ref, pay2_ref, recv2, outgoing2, end_ref,
-    wblocks, low_ref, lrecv, crecv, part_ref, wrecv, wacc,
-    tail_ref, ret_ref, rrecv, small_ref, srecv, sall, sown, sdp, sems, wsems, dsems, hsems, xsems, tsems,
+    wblocks, low_ref, lrecv, crecv, part_ref, part2_ref, *rest,
 ):
+    folding, rest = rest[:10], rest[10:]
+    tail_ref, ret_ref, rrecv, small_ref, srecv, sall, sown, sdp, sems, wsems, dsems, hsems, xsems, tsems = rest
+    parts = (part_ref, part2_ref)
     seq, dp, partner, across = place()
     corner = DP - 1 - dp
     beside = seq + 4 - 8 * lax.rem(seq // 4, 2)
@@ -501,14 +585,17 @@
         for i in range(2):
             for c in range(ROWS // 16):
                 chunk, at = divmod((2 * j + i) * ROWS + c * 16, PIECE)
-                part_ref[chunk, at : at + 16, :] = total[c * 16 : c * 16 + 16, i * 128 : i * 128 + 128].astype(BF16)
+                place_part(parts, chunk, at, total[c * 16 : c * 16 + 16, i * 128 : i * 128 + 128].astype(BF16))
     for c in range(10 * ROWS, SEQ * PIECE, 16):
         chunk, at = divmod(c, PIECE)
-        part_ref[chunk, at : at + 16, :] = jnp.zeros((16, 128), BF16)
-    spread = Scatter(seq, dp, part_ref, wrecv, sems, 10)
+        place_part(parts, chunk, at, jnp.zeros((16, 128), BF16))
+    x, y, z = seq // 8, lax.rem(seq // 4, 2), lax.rem(seq, 4)
+    ways = (
+        (z, y, x, dp, lambda a, y, c: c * 8 + y * 4 + a),
+        (x, y, z, dp, lambda a, y, c: a * 8 + y * 4 + c),
+    )
+    folds = [Fold(*ways[i], parts[i], *folding[5 * i : 5 * i + 5], tsems.at[2 + i]) for i in range(2)]
     out2.sent()
-    back2.received()
-    spread.start()
 
     def pair(p, carry):
         cols = lanes(p)
@@ -528,7 +615,12 @@
         ded_ref[...] += head_sum(jnp.sum(both.reshape(STATE // 8, 8, 128), axis=0), p)
         return carry
 
+    back2.received()
+    for fold in folds:
+        fold.start(0)
     lax.fori_loop(0, PAIRS, pair, 0, unroll=2)
+    for fold in folds:
+        fold.first()
     act_ref[:, INNER : INNER + STATE] = dk_ref[...]
     act_ref[:, INNER + STATE :] = dq_ref[...]
     dfilt_ref[0:8, :] = jnp.zeros((8, 128), F32)
@@ -558,6 +650,8 @@
     lax.fori_loop(0, CHANNELS // 128, filters, 0, unroll=2)
     returned = to_peer(ret_ref, rrecv, hsems.at[2], hsems.at[3], (before, dp))
     returned.start()
+    for fold in folds:
+        fold.second()
     zsum = zsum_ref[...]
     final = jnp.sum(zsum, axis=0, keepdims=True) + decays * jnp.sum(ded_ref[...], axis=0, keepdims=True)
     row = iota((TOKENS, 128), 0)
@@ -579,26 +673,15 @@
     narrow = Scatter(seq, dp, small_ref, srecv, sems, 14, pick=pick)
     narrow.start()
 
-    spread.received()
-    wacc[...] = jnp.zeros_like(wacc)
-
-    def add(k, carry):
-        wacc[...] += wrecv[k].astype(F32)
-        return carry
-
-    lax.fori_loop(0, SEQ, add, 0)
-    x, y, z = seq // 8, lax.rem(seq // 4, 2), lax.rem(seq, 4)
-    trees = [
-        Tree(z, y, x, dp, lambda a, y, c: c * 8 + y * 4 + a, wall, tsems.at[0]),
-        Tree(x, y, z, dp, lambda a, y, c: a * 8 + y * 4 + c, wall2, tsems.at[1]),
-    ]
-    wall[seq] = wacc[0:FIRST, :].astype(BF16)
-    wall2[z * 8 + y * 4 + x] = wacc[FIRST:, :].astype(BF16)
+    trees = [Tree(*ways[i], (wall, wall2)[i], tsems.at[i]) for i in range(2)]
+    wall[seq] = folds[0].third().astype(BF16)
+    wall2[z * 8 + y * 4 + x] = folds[1].third().astype(BF16)
     for tree in trees:
         tree.start(0)
 
     back2.sent()
-    spread.sent()
+    for fold in folds:
+        fold.sent()
     narrow.received()
     sdp[dp] = lax.fori_loop(0, SEQ, lambda k, total: total + srecv[k], jnp.zeros((8, 128), F32))
 
@@ -643,13 +726,6 @@
         scatter.sent()
 
 
-def part_of(walls, chunk, at):
-    if at < FIRST:
-        return walls[0][chunk, at : at + 16, :]
-    x, y, z = chunk // 8, chunk // 4 % 2, chunk % 4
-    return walls[1][z * 8 + y * 4 + x, at - FIRST : at - FIRST + 16, :]
-
-
 def finish_kernel(*refs):
     half = len(refs) - 7
     for src, dst in zip(refs[:6], refs[half : half + 6]):
@@ -679,9 +755,14 @@
     args = (conv_input[0], gate_input[0], filter_taps, filter_bias, norm_weight, heads, step_input[0], output_grad[0], output_weight)
     dma = pltpu.SemaphoreType.DMA
     wide, small, square = (TOKENS, INNER), (TOKENS, STATE), (TOKENS, TOKENS)
-    states, pieces, tiles = (SEQ, BAND, SPREAD), (SEQ, PIECE, 128), (SEQ, 8, 128)
+    states, tiles = (SEQ, BAND, SPREAD), (SEQ, 8, 128)
     scan = [vmem(*states, kind=SENT)] * 4
     walls = [((SEQ, FIRST, 128), BF16), ((SEQ, PIECE - FIRST, 128), BF16)]
+    halves = [vmem(*shape, kind=kind) for shape, kind in walls]
+
+    def folding(n):
+        return [vmem(4, 8, n, 128, kind=BF16), vmem(8, n, 128), *[vmem(4, n, 128)] * 3]
+
     outs = [
         ((TOKENS, CHANNELS), BF16), (wide, BF16), ((HEADS, TOKENS), F32), ((TAPS + 1, CHANNELS), F32),
         ((INNER,), F32), ((3, HEADS), F32), *walls,
@@ -699,9 +780,9 @@
             vmem(*tiles), vmem(8, 128), vmem(SEQ, 1, SPREAD), *scan, *scan,
             vmem(DP - 1, ROWS, WIDTH, kind=BF16), vmem(DP, TOKENS, ROWS, kind=BF16),
             vmem(DP - 1, TOKENS, ROWS, kind=BF16), vmem(DP - 1, TOKENS, WIDTH, kind=BF16),
-            *[vmem(*pieces, kind=BF16)] * 2, vmem(PIECE, 128),
+            *halves, *folding(FIRST), *folding(PIECE - FIRST),
             vmem(EDGE, CHANNELS), *[vmem(8, CHANNELS)] * 2, *[vmem(*tiles)] * 3, vmem(8, 128), vmem(DP, 8, 128),
-            dma((18, SEQ)), dma((6, 4)), dma((4, DP - 1)), dma((4,)), dma((2, DP)), dma((2, 6, 4)),
+            dma((18, SEQ)), dma((6, 4)), dma((4, DP - 1)), dma((4,)), dma((2, DP)), dma((4, 6, 4)),
         ],
         compiler_params=pltpu.CompilerParams(
             vmem_limit_bytes=63 * 2**20, collective_id=0, has_side_effects=True

time: 164 us -> 164 us (level)
  no operation moved by 1% of the time
where the time goes in v6:
time: 164 us; the launch traced here: 163 us
  Pallas kernels  161 us (98%)
    pallas_call x1, Pallas kernels, body(): pl.pallas_call(kernel, out_shape=[jax.ShapeDtypeStruct(shape, kind) for s...  156 us
    pallas_call x1, Pallas kernels, body(): pl.pallas_call(finish_kernel, out_shape=[jax.ShapeDtypeStruct(shape, kind...  5.06 us

profile of v6, /device:TPU:0, one launch (start us, length us, event | category | flops | bytes accessed | tf_op | source)
XLA Modules:
  0.0 163.0 jit_solution(5961651717335140245)
XLA Ops:
  0.6 1.3 pad_maximum_fusion.heads_ref
  1.9 156.0 %layer_backward.1 = (bf16[256,2816]{1,0:T(8,128)(2,1)}, bf16[256,2560]{1,0:T(8,128)(2,1)}, f32[40,256]{1,0:T(8,128)}, f32[5,2816]{1,0:T(8,128)}, f32[2560]{0:T(1...) custom-call(bf16[256,2816]{1,0:T(8,128)(2,1)} %bitcast.10, ...), custom_call_target="tpu_custom_call" | custom-call | tf_op jit(solution)/shard_map/layer_backward/pallas_call | solution.py:770
  157.9 5.1 %finish.1 = (bf16[256,2816]{1,0:T(8,128)(2,1)}, bf16[256,2560]{1,0:T(8,128)(2,1)}, f32[40,256]{1,0:T(8,128)}, f32[5,2816]{1,0:T(8,128)}, f32[2560]{0:T(1024)}, /*index=5*/f32[3,40]{1,0:T(4,128)}, f32[640,1280]{1,0:T(8,128)}) custom-call(bf16[256,2816]{1,0:T(8,128)(2,1)} %get-tuple-element.22.refs_0_, bf16[256,2560]{1,0:T(8,128)(2,1)} %get-tuple-element.23.refs_1_, ...), custom_call_target="tpu_custom_call" | custom-call | tf_op jit(solution)/shard_map/finish/pallas_call | solution.py:793
